TPU v7x, 32 devices: a whole 2x2x4 slice. The times are simulated.
32 devices in a mesh: dom: 32 (over z, y, x, core).
Axes of the slice: x: 2, y: 2, z: 4, core: 2. Of those that a mesh axis runs over, the one named last changes fastest.
Arguments:
- particles: bfloat16 [1024, 2, 7488], P('dom'), may hold values from -6 to 6
- references: bfloat16 [32, 2, 7488], P('dom'), may hold values from -6 to 6
- assignment: int32 [1024, 1], P('dom'), may hold values from 0 to 31
- orientation: int32 [1024], P('dom'), may hold values from 0 to 35
- tilt_range: int32 [2, 1024], P(None, 'dom'), may hold values from 0 to 20
Outputs:
- scores: float32 [1024, 32], P('dom')
- class_means: float32 [32, 2, 7488], P('dom')
- class_load: float32 [32], replicated
Inputs may be any that keep to these rules, and one draw needn't show every extreme that they name: `assignment`: every class has at least one particle.
All inputs are finite; a program needn't handle non-finite values.
Results may differ from a plain program's by a relative error of at most 0.0035.
Values may be sent and summed in bfloat16 or wider, within the bound.
No kernel may reach another device: no remote copies, remote signals or barrier semaphores. Data moves between devices by JAX's collectives and lax.ppermute only.
A program may use at most 128 MiB of HBM per device.

v0:
```python
import math

import jax
import jax.numpy as jnp
from jax import lax
from jax.sharding import PartitionSpec as P

GRID = 24
ORIENTS = 36
COEF = 7488


EPS = 1e-06
GAIN = 6.0
TAU = 0.5
member_rows = 256


def tables():
    index = jnp.arange(COEF, dtype=jnp.int32)
    plane = index // (GRID * GRID)
    rest = index % (GRID * GRID)
    col_x = rest // GRID
    col_z = rest % GRID
    freq_x = ((col_x + GRID // 2) % GRID - GRID // 2).astype(jnp.float32)
    freq_y = plane.astype(jnp.float32)
    freq_z = ((col_z + GRID // 2) % GRID - GRID // 2).astype(jnp.float32)
    return (freq_x, freq_y, freq_z)


def wedge_weights(orient, low_bin, high_bin):
    freq_x, freq_y, freq_z = tables()
    angle = orient.astype(jnp.float32) * (2.0 * math.pi / ORIENTS)
    along = -freq_x[None, :] * jnp.sin(angle)[:, None] + freq_y[None, :] * jnp.cos(angle)[:, None]
    radius = along * along + freq_z[None, :] * freq_z[None, :] + 1.0
    cos_two = (along * along - freq_z[None, :] * freq_z[None, :]) / radius
    sin_two = -2.0 * along * freq_z[None, :] / radius
    low = -(40.0 + 1.5 * low_bin.astype(jnp.float32)) * (math.pi / 180.0)
    high = (40.0 + 1.5 * high_bin.astype(jnp.float32)) * (math.pi / 180.0)
    centre = (low + high)[:, None]
    width = (high - low)[:, None]
    return jax.nn.sigmoid(
        GAIN * (cos_two * jnp.cos(centre) + sin_two * jnp.sin(centre) - jnp.cos(width))
    )


def body(particles, references, assignment, orientation, tilt_range):
    part_rows = particles.shape[0]
    coef = particles.shape[2]
    owned = references.shape[0]
    devices = lax.axis_size("dom")
    classes = owned * devices
    total = part_rows * devices
    cls = assignment[:, 0]
    wedge = wedge_weights(orientation, tilt_range[0], tilt_range[1])
    pf = particles.astype(jnp.float32)
    weighted = (wedge[:, None, :] * pf).astype(jnp.bfloat16)
    flat = weighted.reshape(part_rows, 2 * coef)
    wedge_low = wedge.astype(jnp.bfloat16)
    power = jnp.sum(wedge * (pf[:, 0] * pf[:, 0] + pf[:, 1] * pf[:, 1]), axis=1)
    piece = lax.all_gather(references, "dom", axis=0, tiled=True)
    count = piece.shape[0]
    p32 = piece.astype(jnp.float32)
    ref_power = (p32[:, 0] * p32[:, 0] + p32[:, 1] * p32[:, 1]).astype(jnp.bfloat16)
    intersection = lax.dot_general(
        flat,
        piece.reshape(count, 2 * coef),
        (((1,), (1,)), ((), ())),
        preferred_element_type=jnp.float32,
    )
    energy = lax.dot_general(
        wedge_low, ref_power, (((1,), (1,)), ((), ())), preferred_element_type=jnp.float32
    )
    scores = intersection / (
        math.sqrt(coef) * jnp.sqrt((energy / coef + EPS) * (power[:, None] / coef + EPS))
    )
    ids = lax.iota(jnp.int32, owned * lax.axis_size("dom"))
    onehot = (ids[:, None] == cls[None, :]).astype(jnp.bfloat16)
    numer = lax.psum_scatter(
        jnp.dot(onehot, flat, preferred_element_type=jnp.float32),
        "dom",
        scatter_dimension=0,
        tiled=True,
    )
    labels = jnp.stack([cls, orientation, tilt_range[0], tilt_range[1]])
    every = lax.all_gather(labels, "dom", axis=1, tiled=True)
    class_ids = jnp.arange(classes, dtype=jnp.int32)
    counts = jnp.sum((class_ids[:, None] == every[0][None, :]).astype(jnp.float32), axis=1)
    own_class = lax.axis_index("dom") * owned + 0
    chosen = every[0] == own_class
    members = jnp.nonzero(chosen, size=total + member_rows, fill_value=0)[0].astype(jnp.int32)
    members_count = jnp.sum(chosen.astype(jnp.int32))
    block_count = (members_count + member_rows - 1) // member_rows

    def member_block(block, acc):
        square_sum, wedge_sum = acc
        first = (block * member_rows).astype(jnp.int32)
        picked = lax.dynamic_slice_in_dim(members, first, member_rows, 0)
        valid = (first + lax.iota(jnp.int32, member_rows) < members_count).astype(jnp.float32)
        member_wedge = wedge_weights(every[1][picked], every[2][picked], every[3][picked])
        squares = (member_wedge * member_wedge).astype(jnp.bfloat16).astype(jnp.float32)
        square_sum = square_sum + jnp.sum(valid[:, None] * squares, axis=0)
        wedge_sum = wedge_sum + jnp.sum(valid * jnp.sum(member_wedge, axis=1))
        return (square_sum, wedge_sum)

    square_sum, wedge_sum = lax.fori_loop(
        0, block_count, member_block, (jnp.zeros((coef,), jnp.float32), jnp.zeros((), jnp.float32))
    )
    denom_rows = [square_sum]
    total_rows = [wedge_sum]
    denom = jnp.stack(denom_rows)
    own_totals = jnp.stack(total_rows)
    bottom = denom + TAU * (own_totals[:, None] / coef + 1.0)
    class_means = numer.reshape(owned, 2, coef) / bottom[:, None, :]
    class_load = counts * classes / total
    return (scores, class_means, class_load)


def solution(mesh):
    in_specs = (
        P("dom", None, None),
        P("dom", None, None),
        P("dom", None),
        P("dom"),
        P(None, "dom"),
    )
    out_specs = (P("dom", None), P("dom", None, None), P())
    return jax.shard_map(body, mesh=mesh, in_specs=in_specs, out_specs=out_specs, check_vma=False)
```

profile of v0, /device:TPU:0, one launch (start us, length us, event | category | flops | bytes accessed | tf_op | source)
XLA Modules:
  0.0 159.8 jit_solution(15406478561462494399)
XLA Ops:
  7.4 1.3 copy_convert_fusion
  8.9 1.1 fusion.34
  10.0 0.2 multiply_convert_fusion.1
  10.1 0.7 copy.29
  10.9 0.7 reshape.483
  11.7 1.7 %fusion.62 = f32[32,14976]{1,0:T(8,128)} fusion(bf16[32,14976]{1,0:T(8,128)(2,1)S(1)} %reshape.483, s32[32]{0:T(128)S(1)} %bitcast.59), kind=kOutput, calls=%fused_computation.115 | convolution fusion | flops 30671872 | bytes 2875520 | tf_op jit(solution)/shard_map/dot_general | solution.py:80
  13.3 47.1 %all_gather.6 = bf16[32,2,7488]{2,1,0:T(2,128)(2,1)S(1)} all-gather(bf16[1,2,7488]{2,1,0:T(2,128)(2,1)S(1)} %copy-done.1), channel_id=1, replica_groups=mesh['dom'=32] {'dom'}, dimensions={0}, use_global_device_ids=true | all-gather | bytes 988416 | tf_op jit(solution)/shard_map/all_gather | solution.py:61
  60.4 0.4 convolution_bitcast_fusion
  60.8 0.1 copy_convert_fusion.1
  61.0 36.9 %all-gather = s32[32,32,4]{1,2,0:T(4,128)S(1)} all-gather(s32[1,32,4]{1,2,0:T(4,128)S(1)} %add_bitcast_fusion), channel_id=1, replica_groups=mesh['dom'=32] {'dom'}, dimensions={0}, use_global_device_ids=true | all-gather | bytes 16896 | tf_op jit(solution)/shard_map/all_gather | solution.py:86
  97.9 0.1 reshape.532
  98.0 0.6 convert_reduce_fusion.1
  99.3 0.1 convert_reduce_fusion
  99.4 0.3 reduce-window.16
  99.8 0.1 slice_reduce_fusion.1
  100.0 7.6 %scatter_custom_fusion = s32[1280]{0:T(1024)S(1)} fusion(s32[1024]{0:T(1024)S(1)} %bitcast.58, s32[1024]{0:T(1024)S(1)} %broadcast.1000, s32[]{:T(128)} %constant.257.clone.1), kind=kCustom, calls=%fused_computation.126 | custom fusion | flops 1024 | bytes 5124 | tf_op jit(solution)/shard_map/scatter-add | solution.py:91
  107.7 0.3 reduce-window.24
  108.0 0.1 slice_reduce_fusion
  108.2 0.7 fusion.64
  108.9 13.8 %while.15 = (s32[]{:T(128)}, f32[7488]{0:T(1024)S(1)}, f32[]{:T(128)}, s32[]{:T(128)}, s32[]{:T(128)}, /*index=5*/s32[4,1024]{1,0:T(4,128)S(1)}, s32[1280]{0:T(1...) while((s32[]{:T(128)}, f32[7488]{0:T(1024)S(1)}, f32[]{:T(128)}, s32[]{:T(128)}, s32[]{:T(128)}, ...), condition=%wide.region_12.13_spmd, body=%wide.region_8.12_spmd.sunk | while | flops 46529604 | bytes 420039 | solution.py:106
  109.2 1.4 gather_fusion
  110.6 1.4 gather_fusion.1
  112.0 1.4 gather_fusion.2
  113.6 0.7 fusion.87
  114.3 6.5 %fusion.88 = (f32[256]{0:T(256)S(1)}, f32[7488]{0:T(1024)S(1)}) fusion(f32[256]{0:T(256)S(1)} %get-tuple-element.240, f32[256]{0:T(256)S(1)} %sin.43, f32[7488]{0:T(1024)S(1)} %get-tuple-element.242, f32[256]{0:T(256)S(1)} %get-tuple-element.243, f32[7488]{0:T(1024)S(1)} %fusion.85, f32[256]{0:T(256)S(1)} %get-tuple-element.244, f32[7488]{0:T(1024)S(1)} %fusion.86, ...), kind=kLoop, calls=%fused_computation.7.clone.1 | loop fusion | flops 45998528 | bytes 156928 | tf_op jit(solution)/shard_map/while/body/reduce_sum | solution.py:103
  120.8 1.3 select_reduce_fusion.2
  122.7 0.5 broadcast_multiply_fusion.2
  123.2 1.6 fusion.30
  124.8 26.2 %all-reduce.3.cloned.1.call-done = f32[32,14976]{1,0:T(8,128)} async-done(((f32[32,14976]{1,0:T(8,128)}), f32[32,14976]{1,0:T(8,128)}) %all-reduce.3.cloned.1.call-update) | async-done | bytes 1916944
  151.0 1.2 dynamic-slice_reduce_fusion
  152.1 0.1 reshape.484
  152.3 0.7 broadcast_divide_fusion
  (40 shorter events, 1.1 us)
Async XLA Ops:
  7.2 1.6 copy-start.2
  7.2 1.7 %copy-start.4 = (s32[32]{0:T(128)S(1)}, s32[32]{0:T(128)}, u32[]{:S(2)}) copy-start(s32[32]{0:T(128)} %param.10) | copy-start | bytes 388
  7.2 143.8 %all-reduce.3.cloned.1.call-start = ((), (), s32[]{:S(2)}) async-start(), calls=%async_computation | async-start | bytes 3833856
  8.8 1.2 copy-start
  10.1 1.5 copy-start.3
  11.6 1.7 %copy-start.1 = (bf16[1,2,7488]{2,1,0:T(2,128)(2,1)S(1)}, bf16[1,2,7488]{2,1,0:T(2,128)(2,1)}, u32[]{:S(2)}) copy-start(bf16[1,2,7488]{2,1,0:T(2,128)(2,1)} %param.8) | copy-start | bytes 89860
Sparse Core Ops, SparseCore 0:
  13.5 137.4 all-reduce.2
where the time goes:
time: 160 us
  blocking collectives  84 us (52%)
  waiting for transfers between devices  26.2 us (16%)
  other arithmetic  22.7 us (14%)
  between operations  14.9 us (9%)
  local copies, waits for them, and re-layouts  7.43 us (5%)
  matrix products  3.61 us (2%)
    all_gather x1, blocking collectives, body(): piece = lax.all_gather(references, 'dom', axis=0, tiled=True)  47.1 us
    all_gather x1, blocking collectives, body(): every = lax.all_gather(labels, 'dom', axis=1, tiled=True)  36.9 us
    unnamed x2, waiting for transfers between devices  26.2 us
    reduce_sum x2, other arithmetic, member_block(): wedge_sum = wedge_sum + jnp.sum(valid * jnp.sum(member_wedge, axis=1))  7.77 us
    scatter-add x1, other arithmetic, body(): jnp.nonzero(chosen, size=total + member_rows, fill_value=0)[0]  7.63 us
  transfers between devices with their start and end apart: 1, of which 1 were waited for; matrix products, arithmetic and copies ran while one was open for 16% of the time, Pallas kernels for 0%

commit v1 on v0

--- a/solution.py
+++ b/solution.py
@@ -49,45 +49,68 @@
     coef = particles.shape[2]
     owned = references.shape[0]
     devices = lax.axis_size("dom")
+    chips = devices // 2
     classes = owned * devices
     total = part_rows * devices
+    assert owned == 1 and classes <= 256 and (4 * part_rows) % 2 == 0
+    me = lax.axis_index("dom")
+    core = me % 2
+    groups = [[2 * q + c for q in range(chips)] for c in range(2)]
+    swap = [(d, d ^ 1) for d in range(devices)]
+
     cls = assignment[:, 0]
+    labels = jnp.stack([cls, orientation, tilt_range[0], tilt_range[1]])
+    tail = labels.astype(jnp.bfloat16).reshape(1, 2, 2 * part_rows)
+    packet = jnp.concatenate([references, tail], axis=2)
+    packet = jnp.broadcast_to(packet, (chips, 2, coef + 2 * part_rows))
+    same = lax.all_to_all(packet, "dom", 0, 0, axis_index_groups=groups, tiled=True)
+
     wedge = wedge_weights(orientation, tilt_range[0], tilt_range[1])
     pf = particles.astype(jnp.float32)
     weighted = (wedge[:, None, :] * pf).astype(jnp.bfloat16)
     flat = weighted.reshape(part_rows, 2 * coef)
     wedge_low = wedge.astype(jnp.bfloat16)
     power = jnp.sum(wedge * (pf[:, 0] * pf[:, 0] + pf[:, 1] * pf[:, 1]), axis=1)
-    piece = lax.all_gather(references, "dom", axis=0, tiled=True)
-    count = piece.shape[0]
-    p32 = piece.astype(jnp.float32)
-    ref_power = (p32[:, 0] * p32[:, 0] + p32[:, 1] * p32[:, 1]).astype(jnp.bfloat16)
-    intersection = lax.dot_general(
-        flat,
-        piece.reshape(count, 2 * coef),
-        (((1,), (1,)), ((), ())),
-        preferred_element_type=jnp.float32,
-    )
-    energy = lax.dot_general(
-        wedge_low, ref_power, (((1,), (1,)), ((), ())), preferred_element_type=jnp.float32
-    )
-    scores = intersection / (
-        math.sqrt(coef) * jnp.sqrt((energy / coef + EPS) * (power[:, None] / coef + EPS))
-    )
-    ids = lax.iota(jnp.int32, owned * lax.axis_size("dom"))
-    onehot = (ids[:, None] == cls[None, :]).astype(jnp.bfloat16)
-    numer = lax.psum_scatter(
-        jnp.dot(onehot, flat, preferred_element_type=jnp.float32),
-        "dom",
-        scatter_dimension=0,
-        tiled=True,
-    )
-    labels = jnp.stack([cls, orientation, tilt_range[0], tilt_range[1]])
-    every = lax.all_gather(labels, "dom", axis=1, tiled=True)
+
+    q_ids = lax.iota(jnp.int32, chips)
+
+    def sums(parity):
+        onehot = ((2 * q_ids + parity)[:, None] == cls[None, :]).astype(jnp.bfloat16)
+        return jnp.dot(onehot, flat, preferred_element_type=jnp.float32)
+
+    got = lax.ppermute(sums(1 - core), "dom", swap)
+    chip_sum = (sums(core) + got).astype(jnp.bfloat16)
+    arrived = lax.all_to_all(chip_sum, "dom", 0, 0, axis_index_groups=groups, tiled=True)
+
+    other = lax.ppermute(same, "dom", swap)
+
+    def score_part(block):
+        piece = block[:, :, :coef]
+        p32 = piece.astype(jnp.float32)
+        ref_power = (p32[:, 0] * p32[:, 0] + p32[:, 1] * p32[:, 1]).astype(jnp.bfloat16)
+        intersection = lax.dot_general(
+            flat,
+            piece.reshape(chips, 2 * coef),
+            (((1,), (1,)), ((), ())),
+            preferred_element_type=jnp.float32,
+        )
+        energy = lax.dot_general(
+            wedge_low, ref_power, (((1,), (1,)), ((), ())), preferred_element_type=jnp.float32
+        )
+        return intersection / (
+            math.sqrt(coef) * jnp.sqrt((energy / coef + EPS) * (power[:, None] / coef + EPS))
+        )
+
+    mine, theirs = score_part(same), score_part(other)
+    scores = jnp.where(
+        core == 0, jnp.stack([mine, theirs], axis=2), jnp.stack([theirs, mine], axis=2)
+    ).reshape(part_rows, classes)
+
+    every = jnp.concatenate([same[:, :, coef:], other[:, :, coef:]]).reshape(devices, 4, part_rows)
+    every = every.transpose(1, 0, 2).reshape(4, total).astype(jnp.int32)
     class_ids = jnp.arange(classes, dtype=jnp.int32)
     counts = jnp.sum((class_ids[:, None] == every[0][None, :]).astype(jnp.float32), axis=1)
-    own_class = lax.axis_index("dom") * owned + 0
-    chosen = every[0] == own_class
+    chosen = every[0] == me
     members = jnp.nonzero(chosen, size=total + member_rows, fill_value=0)[0].astype(jnp.int32)
     members_count = jnp.sum(chosen.astype(jnp.int32))
     block_count = (members_count + member_rows - 1) // member_rows
@@ -106,12 +129,9 @@
     square_sum, wedge_sum = lax.fori_loop(
         0, block_count, member_block, (jnp.zeros((coef,), jnp.float32), jnp.zeros((), jnp.float32))
     )
-    denom_rows = [square_sum]
-    total_rows = [wedge_sum]
-    denom = jnp.stack(denom_rows)
-    own_totals = jnp.stack(total_rows)
-    bottom = denom + TAU * (own_totals[:, None] / coef + 1.0)
-    class_means = numer.reshape(owned, 2, coef) / bottom[:, None, :]
+    numer = jnp.sum(arrived.astype(jnp.float32), axis=0).reshape(owned, 2, coef)
+    bottom = square_sum + TAU * (wedge_sum / coef + 1.0)
+    class_means = numer / bottom[None, None, :]
     class_load = counts * classes / total
     return (scores, class_means, class_load)
 

time: 160 us -> 68.1 us (0.43)
  blocking collectives: 84 us -> 0 us
  waiting for transfers between devices: 26.2 us -> 8.45 us
  between operations: 14.9 us -> 1.61 us
  starting transfers between devices: 0.04 us -> 12.2 us
  other arithmetic: 22.7 us -> 27.9 us
  local copies, waits for them, and re-layouts: 7.43 us -> 11 us
  matrix products: 3.61 us -> 5.4 us
    all_gather x2 -> x0, blocking collectives: 84 us -> none  [the longest x1 47.1 us: body(): piece = lax.all_gather(references, 'dom', axis=0, tiled=True)]
    unnamed x2 -> x0, waiting for transfers between devices: 26.2 us -> none
    all_to_all x0 -> x2, starting transfers between devices: none -> 12.2 us  [the longest x1 8.34 us: body(): lax.all_to_all(packet, 'dom', 0, 0, axis_index_groups=groups, tiled=True)]
    all_to_all x0 -> x2, waiting for transfers between devices: none -> 8.44 us  [the longest x1 8.44 us: body(): lax.all_to_all(packet, 'dom', 0, 0, axis_index_groups=groups, tiled=True)]
    another operation x5 -> x9, other arithmetic: 0.69 us -> 2.79 us
    dot_general x3 -> x6, matrix products: 3.61 us -> 5.4 us  [the longest x2 2.81 us: sums(): return jnp.dot(onehot, flat, preferred_element_type=jnp.float32)]
  transfers between devices with their start and end apart: 1 -> 4, of which waited for: 1 -> 1; matrix products, arithmetic and copies ran while one was open for 16% -> 56% of each run, Pallas kernels for 0% -> 0%
where the time goes in v1:
time: 68.1 us; the launch traced here: 67.5 us
  other arithmetic  27.9 us (41%)
  starting transfers between devices  12.2 us (18%)
  local copies, waits for them, and re-layouts  11 us (16%)
  waiting for transfers between devices  8.45 us (12%)
  matrix products  5.4 us (8%)
  between operations  1.61 us (2%)
  loops' own time  0.91 us (1%)
    all_to_all x1, waiting for transfers between devices, body(): lax.all_to_all(packet, 'dom', 0, 0, axis_index_groups=groups, tiled=True)  8.44 us
    all_to_all x1, starting transfers between devices, body(): lax.all_to_all(packet, 'dom', 0, 0, axis_index_groups=groups, tiled=True)  8.34 us
    reduce_sum x2, other arithmetic, member_block(): wedge_sum = wedge_sum + jnp.sum(valid * jnp.sum(member_wedge, axis=1))  7.8 us
    scatter-add x1, other arithmetic, body(): jnp.nonzero(chosen, size=total + member_rows, fill_value=0)[0]  7.63 us
    all_to_all x1, starting transfers between devices, body(): lax.all_to_all(chip_sum, 'dom', 0, 0, axis_index_groups=groups, tiled=True)  3.81 us
    dot_general x2, matrix products, sums(): return jnp.dot(onehot, flat, preferred_element_type=jnp.float32)  2.81 us
    unnamed x7, local copies, waits for them, and re-layouts  2.67 us
    dot_general x2, matrix products, score_part(): lax.dot_general(wedge_low, ref_power, (((1,), (1,)), ((), ())), preferred...  1.86 us
  transfers between devices with their start and end apart: 4, of which 1 were waited for; matrix products, arithmetic and copies ran while one was open for 56% of the time, Pallas kernels for 0%

profile of v1, /device:TPU:0, one launch (start us, length us, event | category | flops | bytes accessed | tf_op | source)
XLA Modules:
  0.0 67.5 jit_solution(9918806627863942154)
XLA Ops:
  0.6 0.8 %convert.16 = bf16[2,32]{1,0:T(2,128)(2,1)S(1)} convert(s32[2,32]{1,0:T(2,128)} %param.11) | non-fusion elementwise | flops 64 | bytes 384 | tf_op jit(solution)/shard_map/convert.5
  1.4 0.7 convert_bitcast_fusion
  2.1 0.7 convert_bitcast_fusion.1
  2.8 0.8 %maximum_bitcast_fusion = bf16[2,7552]{1,0:T(2,128)(2,1)S(1)} fusion(bf16[1,2,64]{2,1,0:T(2,128)(2,1)S(1)} %convert_element_type.273, bf16[1,2,7488]{2,1,0:T(2,128)(2,1)} %param.8), kind=kLoop, calls=%fused_computation.130 | loop fusion | flops 60416 | bytes 60416 | tf_op jit(solution)/shard_map/broadcast_in_dim | solution.py:65
  3.7 1.1 %broadcast_in_dim.20 = bf16[16,2,7552]{2,1,0:T(2,128)(2,1)} broadcast(bf16[2,7552]{1,0:T(2,128)(2,1)S(1)} %maximum_bitcast_fusion), dimensions={1,2} | broadcast | bytes 513536 | tf_op jit(solution)/shard_map/broadcast_in_dim | solution.py:65
  4.7 8.3 %all-to-all-start = ((bf16[16,2,7552]{2,1,0:T(2,128)(2,1)}), bf16[16,2,7552]{2,1,0:T(2,128)(2,1)S(1)}, u32[]{:S(2)}, u32[]{:S(2)}) async-start(bf16[16,2,7552]{2,1,0:T(2,128)(2,1)} %broadcast_in_dim.20), calls=%async_computation | async-start | bytes 966656 | tf_op jit(solution)/shard_map/all_to_all | solution.py:66
  13.1 0.8 %cosine_bitcast_fusion.1 = (f32[32]{0:T(128)S(1)}, f32[32]{0:T(128)S(1)}, f32[32]{0:T(128)S(1)}) fusion(s32[2,32]{1,0:T(2,128)} %param.11), kind=kLoop, calls=%fused_computation.162 | loop fusion | flops 352 | bytes 640 | tf_op jit(solution)/shard_map/cos | solution.py:43
  14.1 0.7 %fusion.92 = (f32[32]{0:T(128)S(1)}, f32[32]{0:T(128)S(1)}) fusion(s32[32]{0:T(128)} %param.10), kind=kLoop, calls=%fused_computation.173 | loop fusion | flops 64 | bytes 384 | tf_op jit(solution)/shard_map/sin | solution.py:34
  14.9 1.1 %add_divide_fusion.1 = (f32[32,7488]{1,0:T(8,128)S(1)}, f32[32]{0:T(128)S(1)}) fusion(f32[32]{0:T(128)S(1)} %get-tuple-element.190, f32[32]{0:T(128)S(1)} %get-tuple-element.189, f32[7488]{0:T(1024)S(1)} %get-tuple-element.194, f32[32]{0:T(128)S(1)} %get-tuple-element.188, f32[7488]{0:T(1024)S(1)} %fusion.77, f32[32]{0:T(128)S(1)} %get-tuple-element.192, ...), kind=kLoop, calls=%fused_computation.79 | loop fusion | flops 5511136 | bytes 2995968 | tf_op jit(solution)/shard_map/div | solution.py:42
  16.2 0.7 %copy.34 = bf16[32,2,7488]{2,1,0:T(2,128)(2,1)S(1)} copy(bf16[32,2,7488]{2,0,1:T(8,128)(2,1)S(1)} %multiply_convert_fusion.1) | data formatting | bytes 1916928 | tf_op jit(solution)/shard_map/convert_element_type | solution.py:70
  16.9 0.7 %reshape.516 = bf16[32,14976]{1,0:T(8,128)(2,1)S(1)} reshape(bf16[32,2,7488]{2,1,0:T(2,128)(2,1)S(1)} %copy.34) | data formatting | bytes 1916928 | tf_op jit(solution)/shard_map/reshape | solution.py:71
  17.7 1.3 %fusion.80 = f32[16,14976]{1,0:T(8,128)} fusion(bf16[32,14976]{1,0:T(8,128)(2,1)S(1)} %reshape.516, s32[32]{0:T(128)S(1)} %bitcast.70, s32[16]{0:T(128)S(1)} %fusion.89), kind=kOutput, calls=%fused_computation.147 | convolution fusion | flops 15335936 | bytes 1917120 | tf_op jit(solution)/shard_map/dot_general | solution.py:79
  19.0 8.4 %all-to-all-done = bf16[16,2,7552]{2,1,0:T(2,128)(2,1)S(1)} async-done(((bf16[16,2,7552]{2,1,0:T(2,128)(2,1)}), bf16[16,2,7552]{2,1,0:T(2,128)(2,1)S(1)}, u32[]{:S(2)}, u32[]{:S(2)}) %all-to-all-start) | async-done | bytes 483360 | tf_op jit(solution)/shard_map/all_to_all | solution.py:66
  28.1 0.9 %fusion.37 = f32[32,16,1]{0,1,2:T(8,128)S(1)} fusion(f32[32,16]{0,1:T(8,128)S(1)} %convolution_bitcast_fusion.1, f32[16,2,7488]{2,0,1:T(8,128)S(1)} %slice_convert_fusion.1, f32[32]{0:T(128)S(1)} %multiply_add_fusion, f32[32]{0:T(128)S(1)} %get-tuple-element.190, f32[32]{0:T(128)S(1)} %get-tuple-element.189, f32[7488]{0:T(1024)S(1)} %get-tuple-element.194, ...), kind=kOutput, calls=%fused_computation.69 | convolution fusion | flops 12702208 | bytes 1083136 | tf_op jit(solution)/shard_map/dot_general | solution.py:97
  29.0 1.5 %fusion.27 = bf16[16,1,14976]{2,0,1:T(8,128)(2,1)S(1)} fusion(f32[16,14976]{1,0:T(8,128)} %collective-permute-done.1, bf16[32,14976]{1,0:T(8,128)(2,1)S(1)} %reshape.516, s32[32]{0:T(128)S(1)} %bitcast.71, s32[16]{0:T(128)S(1)} %fusion.90), kind=kOutput, calls=%fused_computation.54 | convolution fusion | flops 15815168 | bytes 2396352 | tf_op jit(solution)/shard_map/dot_general | solution.py:79
  31.1 0.9 %reduce.13 = bf16[16,14976]{1,0:T(8,128)(2,1)S(1)} reduce(bf16[16,1,14976]{2,0,1:T(8,128)(2,1)S(1)} %fusion.27, bf16[]{:T(256)} %broadcast.1199), dimensions={1}, to_apply=%copy.35.reduce_sub_computation | reduce | bytes 958466 | tf_op jit(solution)/shard_map/all_to_all | solution.py:83
  32.0 1.3 %reshape.583 = bf16[16,2,7488]{2,1,0:T(2,128)(2,1)} reshape(bf16[16,14976]{1,0:T(8,128)(2,1)S(1)} %reduce.13) | data formatting | bytes 958464
  33.2 3.8 %all-to-all-start.1 = ((bf16[16,2,7488]{2,1,0:T(2,128)(2,1)}), bf16[16,2,7488]{2,1,0:T(2,128)(2,1)S(1)}, u32[]{:S(2)}, u32[]{:S(2)}) async-start(bf16[16,2,7488]{2,1,0:T(2,128)(2,1)} %reshape.583), calls=%async_computation.1 | async-start | bytes 966656 | tf_op jit(solution)/shard_map/all_to_all | solution.py:83
  39.6 7.6 %scatter_custom_fusion = s32[1280]{0:T(1024)S(1)} fusion(s32[1024]{0:T(1024)S(1)} %bitcast.69, s32[1024]{0:T(1024)S(1)} %broadcast.1043, s32[]{:T(128)} %constant.265.clone.1), kind=kCustom, calls=%fused_computation.151 | custom fusion | flops 1024 | bytes 5124 | tf_op jit(solution)/shard_map/scatter-add | solution.py:114
  47.7 0.7 %fusion.79 = s32[1280]{0:T(1024)S(1)} fusion(s32[10,128]{1,0:T(8,128)S(1)} %reduce-window.24, s32[10]{0:T(128)S(1)} %slice_reduce_fusion.1, s32[]{:T(128)} %convert_reduce_fusion.2), kind=kLoop, calls=%fused_computation.144 | loop fusion | flops 17920 | bytes 10284 | tf_op jit(solution)/shard_map/jit(_where)/select_n | solution.py:114
  48.4 13.8 %while.15 = (s32[]{:T(128)}, f32[7488]{0:T(1024)S(1)}, f32[]{:T(128)}, s32[]{:T(128)}, s32[]{:T(128)}, /*index=5*/s32[4,1024]{1,0:T(4,128)S(1)}, s32[1280]{0:T(1...) while((s32[]{:T(128)}, f32[7488]{0:T(1024)S(1)}, f32[]{:T(128)}, s32[]{:T(128)}, s32[]{:T(128)}, ...), condition=%wide.region_12.13_spmd, body=%wide.region_8.12_spmd.sunk | while | flops 46529604 | bytes 420039 | solution.py:129
  48.8 1.4 %gather_fusion = s32[256]{0:T(256)S(1)} fusion(s32[1024]{0:T(1024)S(1)} %bitcast.63, s32[1024]{0:T(1024)S(1)} %pad_clamp_fusion.2), kind=kCustom, calls=%fused_computation.clone.1 | custom fusion | bytes 3072 | tf_op jit(solution)/shard_map/while/body/gather | solution.py:123
  50.1 1.4 %gather_fusion.1 = s32[256]{0:T(256)S(1)} fusion(s32[1024]{0:T(1024)S(1)} %bitcast.62, s32[1024]{0:T(1024)S(1)} %pad_clamp_fusion.2), kind=kCustom, calls=%fused_computation.1.clone.1 | custom fusion | bytes 3072 | tf_op jit(solution)/shard_map/while/body/gather | solution.py:123
  51.5 1.4 %gather_fusion.2 = s32[256]{0:T(256)S(1)} fusion(s32[1024]{0:T(1024)S(1)} %bitcast.61, s32[1024]{0:T(1024)S(1)} %pad_clamp_fusion.2), kind=kCustom, calls=%fused_computation.2.clone.1 | custom fusion | bytes 3072 | tf_op jit(solution)/shard_map/while/body/gather | solution.py:123
  53.2 0.7 fusion.112
  53.8 6.5 %fusion.113 = (f32[256]{0:T(256)S(1)}, f32[7488]{0:T(1024)S(1)}) fusion(f32[256]{0:T(256)S(1)} %get-tuple-element.254, f32[256]{0:T(256)S(1)} %sin.43, f32[7488]{0:T(1024)S(1)} %get-tuple-element.256, f32[256]{0:T(256)S(1)} %get-tuple-element.257, f32[7488]{0:T(1024)S(1)} %fusion.110, f32[256]{0:T(256)S(1)} %get-tuple-element.258, ...), kind=kLoop, calls=%fused_computation.7.clone.1 | loop fusion | flops 45998528 | bytes 156928 | tf_op jit(solution)/shard_map/while/body/reduce_sum | solution.py:126
  60.4 1.3 %select_reduce_fusion.2 = f32[]{:T(128)} fusion(f32[256]{0:T(256)S(1)} %get-tuple-element.262, s32[]{:T(128)} %get-tuple-element.289, s32[]{:T(128)S(6)} %mul.946), kind=kLoop, calls=%fused_computation.42.clone.1 | loop fusion | flops 1023 | bytes 1036 | tf_op jit(solution)/shard_map/while/body/reduce_sum | solution.py:126
  62.3 0.9 %fusion.31 = f32[32,16]{0,1:T(8,128)S(1)} fusion(f32[16,2,7488]{2,0,1:T(8,128)S(1)} %slice_convert_fusion, f32[32]{0:T(128)S(1)} %multiply_add_fusion, f32[32]{0:T(128)S(1)} %get-tuple-element.190, f32[32]{0:T(128)S(1)} %get-tuple-element.189, f32[7488]{0:T(1024)S(1)} %get-tuple-element.194, f32[32]{0:T(128)S(1)} %get-tuple-element.188, ...), kind=kOutput, calls=%fused_computation.62 | convolution fusion | flops 12701696 | bytes 1081088 | tf_op jit(solution)/shard_map/dot_general | solution.py:97
  63.7 0.7 %copy.39 = f32[32,32]{1,0:T(8,128)} copy(f32[32,32]{0,1:T(8,128)S(1)} %bitcast.66) | data formatting | bytes 8192
  65.0 0.7 %reshape.584 = bf16[16,1,14976]{2,1,0:T(2,128)(2,1)S(1)} reshape(bf16[16,2,7488]{2,1,0:T(2,128)(2,1)S(1)} %all-to-all-done.1) | data formatting | bytes 958464
  65.7 1.1 %convert_reduce_fusion = f32[14976]{0:T(1024)S(1)} fusion(bf16[16,1,14976]{2,1,0:T(2,128)(2,1)S(1)} %reshape.584), kind=kLoop, calls=%fused_computation.80 | loop fusion | flops 464256 | bytes 539136 | tf_op jit(solution)/shard_map/reduce_sum | solution.py:132
  66.9 0.7 broadcast_divide_fusion
  (63 shorter events, 5.6 us)
Async XLA Ops:
  0.6 14.2 %copy-start = (bf16[32,2,7488]{2,1,0:T(2,128)(2,1)S(1)}, bf16[32,2,7488]{2,1,0:T(2,128)(2,1)}, u32[]{:S(2)}) copy-start(bf16[32,2,7488]{2,1,0:T(2,128)(2,1)} %param.7) | copy-start | bytes 2875396
  4.7 22.7 %all-to-all-start = ((bf16[16,2,7552]{2,1,0:T(2,128)(2,1)}), bf16[16,2,7552]{2,1,0:T(2,128)(2,1)S(1)}, u32[]{:S(2)}, u32[]{:S(2)}) async-start(bf16[16,2,7552]{2,1,0:T(2,128)(2,1)} %broadcast_in_dim.20), calls=%async_computation | async-start | bytes 966656 | tf_op jit(solution)/shard_map/all_to_all | solution.py:66
  16.2 1.5 %copy-start.1 = (s32[32,1]{0,1:T(1,128)S(1)}, s32[32,1]{0,1:T(1,128)}, u32[]{:S(2)}) copy-start(s32[32,1]{0,1:T(1,128)} %param.9) | copy-start | bytes 388
  19.0 10.1 %collective-permute-start.1 = (f32[16,14976]{1,0:T(8,128)}, f32[16,14976]{1,0:T(8,128)}, u32[]{:S(2)}, u32[]{:S(2)}) collective-permute-start(f32[16,14976]{1,0:T(8,128)} %fusion.80), channel_id=1, source_target_pairs={{0,1},{1,0},{2,3},{3,2},{4,5},{5,4},{6,7},{7,6},{8,9},{9,8},{10,11... | collective-permute-start | bytes 2875400 | tf_op jit(solution)/shard_map/ppermute | solution.py:81
  27.5 9.6 %collective-permute-start = (bf16[16,2,7552]{2,0,1:T(8,128)(2,1)S(1)}, bf16[16,2,7552]{2,0,1:T(8,128)(2,1)S(1)}, u32[]{:S(2)}, u32[]{:S(2)}) collective-permute-start(bf16[16,2,7552]{2,0,1:T(8,128)(2,1)S(1)} %copy.31), channel_id=1, source_target_pairs={{0,1},{1,0},{2,3},{3,2},{4,5},{5,4},{6,7},{7,6},{8,9},{9,8},{10,11... | collective-permute-start | bytes 1449992 | tf_op jit(solution)/shard_map/ppermute | solution.py:85
  33.2 31.8 %all-to-all-start.1 = ((bf16[16,2,7488]{2,1,0:T(2,128)(2,1)}), bf16[16,2,7488]{2,1,0:T(2,128)(2,1)S(1)}, u32[]{:S(2)}, u32[]{:S(2)}) async-start(bf16[16,2,7488]{2,1,0:T(2,128)(2,1)} %reshape.583), calls=%async_computation.1 | async-start | bytes 966656 | tf_op jit(solution)/shard_map/all_to_all | solution.py:83

commit v2 on v0

v2 whole, which is shorter than its diff:
```python
import functools
import math

import jax
import jax.numpy as jnp
from jax import lax
from jax.experimental import pallas as pl
from jax.experimental.pallas import tpu as pltpu
from jax.sharding import PartitionSpec as P


GRID = 24
ORIENTS = 36

EPS = 1e-06
GAIN = 6.0
TAU = 0.5
LOG2E = math.log2(math.e)
LANES = 128
STEP = 256
CHUNK = 512
GROUP = 128
FAR = 4
VMEM = pltpu.VMEM
f32 = jnp.float32
bf16 = jnp.bfloat16
i32 = jnp.int32


def iota(shape, axis):
    return lax.broadcasted_iota(i32, shape, axis)


def dot(a, b):
    return jnp.dot(a, b, preferred_element_type=f32)


def dot_nt(a, b):
    return lax.dot_general(a, b, (((1,), (1,)), ((), ())), preferred_element_type=f32)


def freqs(index):
    plane = jnp.floor((index + 0.5) * (1.0 / (GRID * GRID)))
    rest = index - plane * (GRID * GRID)
    col_x = jnp.floor((rest + 0.5) * (1.0 / GRID))
    col_z = rest - col_x * GRID
    half = GRID // 2
    freq_x = jnp.where(col_x < half, col_x, col_x - GRID)
    freq_z = jnp.where(col_z < half, col_z, col_z - GRID)
    return freq_x, plane, freq_z


def wedge_of(freq_x, freq_y, freq_z, sin_a, cos_a, cos_c, sin_c, cos_w):
    along = freq_y * cos_a - freq_x * sin_a
    sq = along * along
    zsq = freq_z * freq_z
    inverse = 1.0 / (sq + (zsq + 1.0))
    power = (cos_c * (sq - zsq) + sin_c * (along * freq_z)) * inverse + cos_w
    return 1.0 / (1.0 + jnp.exp2(power))


def by_lane(values, width):
    lane = iota((1, width), 1)
    row = jnp.zeros((1, width), f32)
    for i, value in enumerate(values):
        row = jnp.where(lane == i, f32(value), row)
    return row


def turns(orient, low_bin, high_bin, width):
    quarter = 0.5 * math.pi
    bin_ = 1.5 * math.pi / 180.0
    wide = 80.0 * math.pi / 180.0
    scale = GAIN * LOG2E
    turn = (
        orient * by_lane([2.0 * math.pi / ORIENTS] * 2, width)
        + low_bin * by_lane([0.0, 0.0, -bin_, -bin_, bin_], width)
        + high_bin * by_lane([0.0, 0.0, bin_, bin_, bin_], width)
        + by_lane([0.0, quarter, quarter, 0.0, quarter + wide], width)
    )
    return jnp.sin(turn) * by_lane([1.0, 1.0, -scale, 2.0 * scale, scale], width)


def to_column(row):
    size = row.shape[1]
    same = iota((size, size), 0) == iota((size, size), 1)
    return jnp.sum(jnp.where(same, row, 0.0), axis=1, keepdims=True)


def pack_kernel(padded, ref_ref, cls_ref, orient_ref, tilt_ref, packet_ref, pack, sems):
    coef = ref_ref.shape[2]
    parts = orient_ref.shape[0]
    cls = cls_ref[...].reshape(1, parts)
    orient = orient_ref[...].reshape(1, parts)
    first = jnp.where(iota((2, parts), 0) == 0, cls, orient).astype(f32).astype(bf16)
    second = tilt_ref[...].astype(f32).astype(bf16)
    source, lane = iota((parts, LANES), 0), iota((parts, LANES), 1)
    labels = dot(first, (lane == source).astype(bf16)) + dot(
        second, (lane == source + parts).astype(bf16)
    )
    pack[:, 0:coef] = ref_ref[0]
    pack[:, padded : padded + LANES] = labels.astype(bf16)
    copies = [
        pltpu.make_async_copy(pack, packet_ref.at[q], sems.at[q])
        for q in range(packet_ref.shape[0])
    ]
    for copy in copies:
        copy.start()
    for copy in copies:
        copy.wait()


def pre_kernel(
    coef, chips, rows, half,
    x_ref, cls_ref, orient_ref, tilt_ref,
    keep_ref, send_ref, weighted_ref, low_ref, power_ref,
):
    parts = x_ref.shape[0]
    padded = low_ref.shape[1]
    full = coef // STEP * STEP
    cls = cls_ref[...].reshape(1, parts)
    orient = orient_ref[...].reshape(1, parts)
    core = lax.axis_index("dom") % 2
    order = iota((2 * chips, parts), 0)
    order = jnp.where(order < chips, 2 * order + core, 2 * (order - chips) + 1 - core)
    hot = (order == cls).astype(bf16)
    turn = turns(
        to_column(orient.astype(f32)),
        to_column(tilt_ref[0:1, :].astype(f32)),
        to_column(tilt_ref[1:2, :].astype(f32)),
        LANES,
    )
    factors = [turn[:, i : i + 1] for i in range(5)]
    out_row, in_row = iota((2 * parts, 2 * parts), 0), iota((2 * parts, 2 * parts), 1)
    wanted = jnp.where(out_row < parts, 2 * out_row, 2 * (out_row - parts) + 1)
    split = (in_row == wanted).astype(bf16)

    def block(x, start, width, valid):
        both = dot(split, x.reshape(2 * parts, x.shape[2]))
        if valid < width:
            both = jnp.concatenate([both, jnp.zeros((2 * parts, width - valid), f32)], axis=1)
        real, imag = both[:parts], both[parts:]
        index = (iota((1, width), 1) + start).astype(f32)
        wedge = wedge_of(*freqs(index), *factors)
        if valid < width:
            wedge = jnp.where(index < coef, wedge, 0.0)
        cols = pl.ds(start, width)
        low_ref[:, cols] = wedge.astype(bf16)
        energy = wedge * (real * real + imag * imag)
        total = energy[:, :LANES]
        for j in range(1, width // LANES):
            total = total + energy[:, j * LANES : (j + 1) * LANES]
        power_ref[...] += total
        tile = start // LANES
        for part, value in enumerate((real, imag)):
            value = (wedge * value).astype(bf16)
            weighted_ref[part * parts : (part + 1) * parts, cols] = value
            summed = dot(hot, value)
            for j in range(width // LANES):
                for q in range(0, chips, 8):
                    place = pl.ds(q * rows + part * half + tile + j, 8, stride=rows)
                    lanes = slice(j * LANES, (j + 1) * LANES)
                    keep_ref[place, :] = summed[q : q + 8, lanes]
                    send_ref[place, :] = summed[chips + q : chips + q + 8, lanes]

    power_ref[...] = jnp.zeros_like(power_ref)

    def step(s, carry):
        start = pl.multiple_of(s * STEP, STEP)
        block(x_ref[:, :, pl.ds(start, STEP)], start, STEP, STEP)
        return carry

    lax.fori_loop(0, full // STEP, step, 0)
    block(x_ref[:, :, full:coef], full, padded - full, coef - full)


def add_kernel(chips, rows, room, keep_ref, got_ref, out_ref):
    for q in range(chips):
        place = pl.ds(q * rows, room)
        out_ref[q] = (keep_ref[place, :] + got_ref[place, :]).astype(bf16)


def table_kernel(table_ref):
    for t in range(table_ref.shape[2] // LANES):
        index = (iota((8, LANES), 1) + t * LANES).astype(f32)
        for i, row in enumerate(freqs(index)):
            table_ref[i, :, t * LANES : (t + 1) * LANES] = row


def post_kernel(
    coef, same_ref, other_ref, weighted_ref, low_ref, power_ref, table,
    score_ref, load_ref, bottom_ref,
    squares, listed,
):
    chips = same_ref.shape[0]
    parts, padded = low_ref.shape
    devices = 2 * chips
    per_far = chips // FAR
    classes = score_ref.shape[1]
    tiles = padded // LANES
    me = lax.axis_index("dom")
    core = me % 2

    def picker(parity):
        out_row, in_row = iota((2 * devices, 2 * chips), 0), iota((2 * devices, 2 * chips), 1)
        part = (out_row >= devices).astype(i32)
        device = out_row - part * devices
        chip = device // 2
        near = (chip % per_far) ^ (me // 2 % per_far)
        place = near * FAR + chip // per_far
        return (in_row == 2 * place + part) & (device % 2 == parity)

    pick_a, pick_b = picker(core).astype(bf16), picker(1 - core).astype(bf16)

    def rows_of(start, width):
        cols = pl.ds(start, width)
        a = same_ref[:, :, cols].reshape(2 * chips, width)
        b = other_ref[:, :, cols].reshape(2 * chips, width)
        return dot(pick_a, a) + dot(pick_b, b)

    labels = rows_of(padded, LANES)
    cls, orient = labels[:devices, :parts], labels[devices:, :parts]
    low_bin, high_bin = labels[:devices, parts : 2 * parts], labels[devices:, parts : 2 * parts]
    class_col = iota((classes, parts), 0).astype(f32)
    tally = jnp.zeros((classes, parts), f32)
    for r in range(devices):
        tally = tally + jnp.where(cls[r : r + 1] == class_col, 1.0, 0.0)
    tally = jnp.sum(tally, axis=1, keepdims=True)
    diagonal = iota((classes, classes), 0) == iota((classes, classes), 1)
    counts = jnp.sum(jnp.where(diagonal, tally, 0.0), axis=0, keepdims=True)
    load_ref[...] = counts * (classes / (devices * parts))

    chosen = cls == me.astype(f32)
    mask = chosen.astype(bf16)
    before = (iota((parts, parts), 0) < iota((parts, parts), 1)).astype(bf16)
    above = (iota((devices, devices), 0) > iota((devices, devices), 1)).astype(bf16)
    in_row = dot(mask, jnp.ones((parts, parts), bf16))
    rank = dot(mask, before) + dot(above, in_row.astype(bf16))
    rank = jnp.where(chosen, rank, -1.0)
    count = jnp.sum(jnp.where(chosen, 1.0, 0.0)).astype(i32)

    squares[...] = jnp.zeros_like(squares)

    def group(g, total):
        base = (g * GROUP).astype(f32)
        slot = iota((GROUP, parts), 0).astype(f32) + base
        values = [jnp.zeros((GROUP, 1), f32)] * 3
        columns = jnp.zeros((GROUP, 8), f32)
        pick = iota((8, parts), 0)
        for r in range(devices):
            hit = (rank[r : r + 1] == slot).astype(bf16)
            row = jnp.where(pick == 0, orient[r : r + 1], jnp.where(pick == 1, low_bin[r : r + 1], high_bin[r : r + 1]))
            columns = columns + dot_nt(hit, row.astype(bf16))
        turn = turns(columns[:, 0:1], columns[:, 1:2], columns[:, 2:3], 8)
        empty = iota((GROUP, 8), 0) + g * GROUP >= count
        listed[...] = jnp.where(empty & (iota((GROUP, 8), 1) == 4), 100.0, turn)
        left = jnp.minimum(count - g * GROUP, GROUP)

        def eight(e, total):
            params = listed[pl.ds(pl.multiple_of(e * 8, 8), 8), :]
            factors = [jnp.broadcast_to(params[:, i : i + 1], (8, LANES)) for i in range(5)]
            for t in range(tiles):
                cols = slice(t * LANES, (t + 1) * LANES)
                wedge = wedge_of(table[0, :, cols], table[1, :, cols], table[2, :, cols], *factors)
                squares[:, cols] += (wedge * wedge).astype(bf16).astype(f32)
                if (t + 1) * LANES > coef:
                    wedge = jnp.where(iota((8, LANES), 1) < coef - t * LANES, wedge, 0.0)
                total = total + wedge
            return total

        return lax.fori_loop(0, (left + 7) // 8, eight, total)

    total = lax.fori_loop(0, (count + GROUP - 1) // GROUP, group, jnp.zeros((8, LANES), f32))
    extra = TAU * (jnp.sum(total, keepdims=True) * (1.0 / coef) + 1.0)
    for t in range(tiles):
        cols = slice(t * LANES, (t + 1) * LANES)
        bottom_ref[t : t + 1, :] = jnp.sum(squares[:, cols], axis=0, keepdims=True) + extra

    intersection = jnp.zeros((parts, classes), f32)
    energy = jnp.zeros((parts, classes), f32)
    for start in range(0, padded, CHUNK):
        width = min(CHUNK, padded - start)
        cols = slice(start, start + width)
        both = rows_of(start, width)
        real, imag = both[:devices], both[devices:]
        ref_power = (real * real + imag * imag).astype(bf16)
        intersection = intersection + dot_nt(weighted_ref[:parts, cols], real.astype(bf16))
        intersection = intersection + dot_nt(weighted_ref[parts:, cols], imag.astype(bf16))
        energy = energy + dot_nt(low_ref[:, cols], ref_power)
    power = jnp.sum(power_ref[...], axis=1, keepdims=True)
    score_ref[...] = intersection / (
        math.sqrt(coef) * jnp.sqrt((energy / coef + EPS) * (power / coef + EPS))
    )


def final_kernel(coef, half, arrived_ref, bottom_ref, out_ref, ratio):
    tiles = -(-coef // LANES)
    total = arrived_ref[0].astype(f32)
    for q in range(1, arrived_ref.shape[0]):
        total = total + arrived_ref[q].astype(f32)
    bottom = bottom_ref[...]
    ratio[0:half, :] = total[0:half] / bottom[0:half]
    ratio[half : 2 * half, :] = total[half : 2 * half] / bottom[0:half]
    for t in range(tiles):
        width = min(LANES, coef - t * LANES)
        pair = ratio[pl.ds(t, 2, stride=half), :]
        out_ref[0, :, pl.ds(t * LANES, width)] = pair[:, :width]


def limit(*arrays):
    size = sum(math.prod(a.shape) * max(2, jnp.dtype(a.dtype).itemsize) for a in arrays)
    return pltpu.CompilerParams(vmem_limit_bytes=(4 << 20) + size)


def body(particles, references, assignment, orientation, tilt_range):
    part_rows = particles.shape[0]
    coef = particles.shape[2]
    owned = references.shape[0]
    devices = lax.axis_size("dom")
    chips = devices // 2
    classes = owned * devices
    assert owned == 1 and classes <= 256 and chips % 8 == 0 and chips & (chips - 1) == 0 and 2 * part_rows <= LANES
    groups = [[2 * q + c for q in range(chips)] for c in range(2)]
    near = devices // FAR
    far = [[d + near * q for q in range(FAR)] for d in range(near)]
    swap = [(d, d ^ 1) for d in range(devices)]
    tiles = -(-coef // LANES)
    half = -(-tiles // 4) * 4
    room = 2 * half
    rows = room + 1
    padded = tiles * LANES
    wide = padded + LANES
    assert padded - coef // STEP * STEP <= LANES
    shape = jax.ShapeDtypeStruct
    hbm = pl.BlockSpec(memory_space=pltpu.HBM)
    vmem = pl.BlockSpec(memory_space=VMEM)

    cls = assignment.reshape(part_rows)
    packet = pl.pallas_call(
        functools.partial(pack_kernel, padded),
        out_shape=shape((FAR, 2, wide), bf16),
        in_specs=[vmem] * 4,
        out_specs=hbm,
        scratch_shapes=[VMEM((2, wide), bf16), pltpu.SemaphoreType.DMA((FAR,))],
        compiler_params=pltpu.CompilerParams(vmem_limit_bytes=4 << 20),
        name="pack",
    )(references, cls, orientation, tilt_range)

    same = lax.all_to_all(packet, "dom", 0, 0, axis_index_groups=far, tiled=True)
    outs = (
        shape((chips * rows, LANES), f32),
        shape((chips * rows, LANES), f32),
        shape((2 * part_rows, padded), bf16),
        shape((part_rows, padded), bf16),
        shape((part_rows, LANES), f32),
    )
    keep, send, weighted, low, power = pl.pallas_call(
        functools.partial(pre_kernel, coef, chips, rows, half),
        out_shape=outs,
        in_specs=[vmem, vmem, vmem, vmem],
        out_specs=(vmem, vmem, vmem, vmem, vmem),
        compiler_params=limit(*outs, particles),
        name="pre",
    )(particles, cls, orientation, tilt_range)
    got = lax.ppermute(send, "dom", swap)
    chip_sum = pl.pallas_call(
        functools.partial(add_kernel, chips, rows, room),
        out_shape=shape((chips, room, LANES), bf16),
        in_specs=[vmem, vmem],
        out_specs=vmem,
        compiler_params=limit(keep, got, keep),
        name="add",
    )(keep, got)
    arrived = lax.all_to_all(chip_sum, "dom", 0, 0, axis_index_groups=groups, tiled=True)
    table = pl.pallas_call(
        table_kernel,
        out_shape=shape((3, 8, padded), f32),
        out_specs=vmem,
        compiler_params=pltpu.CompilerParams(vmem_limit_bytes=4 << 20),
        name="table",
    )()
    bit = 1
    while bit < chips // FAR:
        swapped = lax.ppermute(same, "dom", [(d, d ^ (2 * bit)) for d in range(devices)])
        same = jnp.concatenate([same, swapped])
        bit *= 2
    other = lax.ppermute(same, "dom", swap)

    outs = (
        shape((part_rows, classes), f32),
        shape((1, classes), f32),
        shape((-(-tiles // 8) * 8, LANES), f32),
    )
    scores, load, bottom = pl.pallas_call(
        functools.partial(post_kernel, coef),
        out_shape=outs,
        in_specs=[vmem] * 6,
        out_specs=(vmem, vmem, vmem),
        scratch_shapes=[
            VMEM((8, padded), f32),
            VMEM((GROUP, 8), f32),
        ],
        compiler_params=limit(same, other, weighted, low, table, *outs),
        name="post",
    )(same, other, weighted, low, power, table)

    class_means = pl.pallas_call(
        functools.partial(final_kernel, coef, half),
        out_shape=shape((owned, 2, coef), f32),
        in_specs=[vmem, vmem],
        out_specs=vmem,
        scratch_shapes=[VMEM((room, LANES), f32)],
        compiler_params=limit(arrived),
        name="means",
    )(arrived, bottom)
    return (scores, class_means, load.reshape(classes))


def solution(mesh):
    in_specs = (
        P("dom", None, None),
        P("dom", None, None),
        P("dom", None),
        P("dom"),
        P(None, "dom"),
    )
    out_specs = (P("dom", None), P("dom", None, None), P())
    return jax.shard_map(body, mesh=mesh, in_specs=in_specs, out_specs=out_specs, check_vma=False)
```

time: 160 us -> 53 us (0.33)
  blocking collectives: 84 us -> 0 us
  other arithmetic: 22.7 us -> 1.92 us
  Pallas kernels: 0 us -> 16 us
  starting transfers between devices: 0.04 us -> 15.6 us
  waiting for transfers between devices: 26.2 us -> 11.9 us
  between operations: 14.9 us -> 0.72 us
  matrix products: 3.61 us -> 0 us
    all_gather x2 -> x0, blocking collectives: 84 us -> none  [the longest x1 47.1 us: body(): piece = lax.all_gather(references, 'dom', axis=0, tiled=True)]
    unnamed x2 -> x0, waiting for transfers between devices: 26.2 us -> none
    pallas_call x0 -> x6, Pallas kernels: none -> 16 us  [the longest x1 9.21 us: body(): pl.pallas_call(functools.partial(pre_kernel, coef, chips, rows, half), ou...]
    all_to_all x0 -> x2, starting transfers between devices: none -> 12.5 us  [the longest x1 6.36 us: body(): lax.all_to_all(packet, 'dom', 0, 0, axis_index_groups=far, tiled=True)]
    reduce_sum x5 -> x0, other arithmetic: 9.6 us -> none  [the longest x2 7.77 us: member_block(): wedge_sum = wedge_sum + jnp.sum(valid * jnp.sum(member_wedge, axis=1))]
    scatter-add x1 -> x0, other arithmetic: 7.63 us -> none  [body(): jnp.nonzero(chosen, size=total + member_rows, fill_value=0)[0]]
    all_to_all x0 -> x2, waiting for transfers between devices: none -> 6.81 us  [the longest x1 6.81 us: body(): lax.all_to_all(chip_sum, 'dom', 0, 0, axis_index_groups=groups, tiled=True)]
    ppermute x0 -> x4, waiting for transfers between devices: none -> 5.13 us  [the longest x2 3.43 us: body(): lax.ppermute(same, 'dom', [(d, d ^ 2 * bit) for d in range(devices)])]
  transfers between devices with their start and end apart: 1 -> 6, of which waited for: 1 -> 3; matrix products, arithmetic and copies ran while one was open for 16% -> 8% of each run, Pallas kernels for 0% -> 28%
where the time goes in v2:
time: 53 us; the launch traced here: 52.5 us
  Pallas kernels  16 us (30%)
  starting transfers between devices  15.6 us (29%)
  waiting for transfers between devices  11.9 us (22%)
  local copies, waits for them, and re-layouts  6.33 us (12%)
  other arithmetic  1.92 us (4%)
  between operations  0.72 us (1%)
    pallas_call x1, Pallas kernels, body(): pl.pallas_call(functools.partial(pre_kernel, coef, chips, rows, half), ou...  9.21 us
    all_to_all x1, waiting for transfers between devices, body(): lax.all_to_all(chip_sum, 'dom', 0, 0, axis_index_groups=groups, tiled=True)  6.81 us
    all_to_all x1, starting transfers between devices, body(): lax.all_to_all(packet, 'dom', 0, 0, axis_index_groups=far, tiled=True)  6.36 us
    all_to_all x1, starting transfers between devices, body(): lax.all_to_all(chip_sum, 'dom', 0, 0, axis_index_groups=groups, tiled=True)  6.13 us
    unnamed x18, local copies, waits for them, and re-layouts  5.2 us
    pallas_call x1, Pallas kernels, body(): pl.pallas_call(functools.partial(post_kernel, coef), out_shape=outs, in_s...  4.14 us
    ppermute x2, waiting for transfers between devices, body(): lax.ppermute(same, 'dom', [(d, d ^ 2 * bit) for d in range(devices)])  3.43 us
    ppermute x2, starting transfers between devices, body(): lax.ppermute(same, 'dom', [(d, d ^ 2 * bit) for d in range(devices)])  3.01 us
  transfers between devices with their start and end apart: 6, of which 3 were waited for; matrix products, arithmetic and copies ran while one was open for 8% of the time, Pallas kernels for 28%

profile of v2, /device:TPU:0, one launch (start us, length us, event | category | flops | bytes accessed | tf_op | source)
XLA Modules:
  0.0 52.5 jit_solution(5733047011350535373)
XLA Ops:
  0.6 0.0 copy-start.4
  0.6 0.0 copy-start.5
  0.7 0.7 %copy-done.4 = s32[2,32]{1,0:T(2,128)S(1)} copy-done((s32[2,32]{1,0:T(2,128)S(1)}, s32[2,32]{1,0:T(2,128)}, u32[]{:S(2)}) %copy-start.4) | copy-done | bytes 280
  1.3 0.8 %copy-done.3 = bf16[1,2,7488]{2,1,0:T(2,128)(2,1)S(1)} copy-done((bf16[1,2,7488]{2,1,0:T(2,128)(2,1)S(1)}, bf16[1,2,7488]{2,1,0:T(2,128)(2,1)}, u32[]{:S(2)}) %copy-start.3) | copy-done | bytes 29976
  2.1 0.7 %copy-done.6 = s32[32]{0:T(128)S(1)} copy-done((s32[32]{0:T(128)S(1)}, s32[32]{0:T(128)}, u32[]{:S(2)}) %copy-start.6) | copy-done | bytes 152
  2.7 0.8 %pack.1 = bf16[4,2,7680]{2,1,0:T(2,128)(2,1)} custom-call(bf16[1,2,7488]{2,1,0:T(2,128)(2,1)S(1)} %copy-done.3, s32[32]{0:T(128)S(1)} %bitcast.2, s32[32]{0:T(128)S(1)} %copy-done.6, s32[2,32]{1,0:T(2,128)S(1)} %copy-done.4), custom_call_target="tpu_custom_call" | custom-call | tf_op jit(solution)/shard_map/pack/pallas_call | solution.py:339
  3.5 0.0 copy-start.7
  3.5 6.4 %all-to-all-start = ((bf16[4,2,7680]{2,1,0:T(2,128)(2,1)}), bf16[4,2,7680]{2,1,0:T(2,128)(2,1)}, u32[]{:S(2)}, u32[]{:S(2)}) async-start(bf16[4,2,7680]{2,1,0:T(2,128)(2,1)} %pack.1), calls=%async_computation | async-start | bytes 245760 | tf_op jit(solution)/shard_map/all_to_all | solution.py:349
  9.9 0.0 copy-done.7
  9.9 1.2 %copy-done = bf16[32,2,7488]{2,1,0:T(2,128)(2,1)S(1)} copy-done((bf16[32,2,7488]{2,1,0:T(2,128)(2,1)S(1)}, bf16[32,2,7488]{2,1,0:T(2,128)(2,1)}, u32[]{:S(2)}) %copy-start) | copy-done | bytes 958488
  11.1 9.2 %pre.1 = (f32[1936,128]{1,0:T(8,128)S(1)}, f32[1936,128]{1,0:T(8,128)}, bf16[64,7552]{1,0:T(8,128)(2,1)S(1)}, bf16[32,7552]{1,0:T(8,128)(2,1)S(1)}, f32[32,128]{1,0:T(8,128)S(1)}) custom-call(bf16[32,2,7488]{2,1,0:T(2,128)(2,1)S(1)} %copy-done, s32[32]{0:T(128)S(1)} %bitcast.3, s32[32]{0:T(128)S(1)} %copy-done.7, s32[2,32]{1,0:T(2,128)S(1)} %copy-done.4), custom_call_target="tpu_custom_call" | custom-call | tf_op jit(solution)/shard_map/pre/pallas_call | solution.py:357
  20.3 0.8 %copy-done.1 = bf16[32,7552]{1,0:T(8,128)(2,1)} copy-done((bf16[32,7552]{1,0:T(8,128)(2,1)}, bf16[32,7552]{1,0:T(8,128)(2,1)S(1)}, u32[]{:S(2)}) %copy-start.1) | copy-done | bytes 483352
  21.1 0.0 collective-permute-start.3
  21.1 0.0 all-to-all-done
  21.1 1.5 %collective-permute-start = (bf16[4,2,7680]{2,1,0:T(2,128)(2,1)}, bf16[4,2,7680]{2,1,0:T(2,128)(2,1)S(1)}, u32[]{:S(2)}, u32[]{:S(2)}) collective-permute-start(bf16[4,2,7680]{2,1,0:T(2,128)(2,1)} %all-to-all-done), channel_id=1, source_target_pairs={{0,2},{1,3},{2,0},{3,1},{4,6},{5,7},{6,4},{7,5},{8,10},{9,11},{10,... | collective-permute-start | bytes 368648 | tf_op jit(solution)/shard_map/ppermute | solution.py:384
  22.6 1.0 %constant_dynamic-update-slice_fusion.2 = bf16[16,2,7680]{2,1,0:T(2,128)(2,1)S(1)} fusion(bf16[4,2,7680]{2,1,0:T(2,128)(2,1)} %all-to-all-done), kind=kLoop, calls=%fused_computation.3 | loop fusion | bytes 245760
  23.6 3.4 %collective-permute-done = bf16[4,2,7680]{2,1,0:T(2,128)(2,1)S(1)} collective-permute-done((bf16[4,2,7680]{2,1,0:T(2,128)(2,1)}, bf16[4,2,7680]{2,1,0:T(2,128)(2,1)S(1)}, u32[]{:S(2)}, u32[]{:S(2)}) %collective-permute-start) | collective-permute-done | bytes 122912 | tf_op jit(solution)/shard_map/ppermute | solution.py:384
  27.1 1.9 %pad_maximum_fusion = bf16[8,2,7680]{2,1,0:T(2,128)(2,1)} fusion(bf16[4,2,7680]{2,1,0:T(2,128)(2,1)S(1)} %collective-permute-done, bf16[4,2,7680]{2,1,0:T(2,128)(2,1)} %all-to-all-done), kind=kLoop, calls=%fused_computation | loop fusion | flops 122880 | bytes 491520 | tf_op jit(solution)/shard_map/concatenate | solution.py:385
  29.0 1.5 %collective-permute-start.1 = (bf16[8,2,7680]{2,1,0:T(2,128)(2,1)}, bf16[8,2,7680]{2,1,0:T(2,128)(2,1)}, u32[]{:S(2)}, u32[]{:S(2)}) collective-permute-start(bf16[8,2,7680]{2,1,0:T(2,128)(2,1)} %pad_maximum_fusion), channel_id=1, source_target_pairs={{0,4},{1,5},{2,6},{3,7},{4,0},{5,1},{6,2},{7,3},{8,12},{9,13},{10,... | collective-permute-start | bytes 737288 | tf_op jit(solution)/shard_map/ppermute | solution.py:384
  30.5 0.1 constant_dynamic-update-slice_fusion.1
  30.6 0.0 collective-permute-done.3.got_ref
  30.6 0.9 %add.1 = bf16[16,120,128]{2,1,0:T(8,128)(2,1)} custom-call(f32[1936,128]{1,0:T(8,128)S(1)} %get-tuple-element.15.keep_ref, f32[1936,128]{1,0:T(8,128)S(1)} %collective-permute-done.3.got_ref), custom_call_target="tpu_custom_call" | custom-call | tf_op jit(solution)/shard_map/add/pallas_call | solution.py:366
  31.6 6.1 %all-to-all-start.1 = ((bf16[16,120,128]{2,1,0:T(8,128)(2,1)}), bf16[16,120,128]{2,1,0:T(8,128)(2,1)S(1)}, u32[]{:S(2)}, u32[]{:S(2)}) async-start(bf16[16,120,128]{2,1,0:T(8,128)(2,1)} %add.1), calls=%async_computation.1 | async-start | bytes 983040 | tf_op jit(solution)/shard_map/all_to_all | solution.py:374
  37.7 0.0 collective-permute-done.1
  37.7 1.1 %constant_dynamic-update-slice_fusion.same_ref = bf16[16,2,7680]{2,1,0:T(2,128)(2,1)S(1)} fusion(bf16[16,2,7680]{2,1,0:T(2,128)(2,1)S(1)} %constant_dynamic-update-slice_fusion.1, bf16[8,2,7680]{2,1,0:T(2,128)(2,1)} %collective-permute-done.1), kind=kLoop, calls=%fused_computation.1 | loop fusion | bytes 491520 | tf_op jit(solution)/shard_map/concatenate | solution.py:385
  38.8 0.0 copy-start.2
  38.9 0.1 collective-permute-start.2
  38.9 0.2 table.1
  39.1 1.7 %collective-permute-done.2.other_ref = bf16[16,2,7680]{2,1,0:T(2,128)(2,1)S(1)} collective-permute-done((bf16[16,2,7680]{2,1,0:T(2,128)(2,1)S(1)}, bf16[16,2,7680]{2,1,0:T(2,128)(2,1)S(1)}, u32[]{:S(2)}, u32[]{:S(2)}) %collective-permute-start.2) | collective-permute-done | bytes 491552 | tf_op jit(solution)/shard_map/ppermute | solution.py:387
  40.8 4.1 %post.1 = (f32[32,32]{1,0:T(8,128)}, f32[1,32]{1,0:T(1,128)}, f32[64,128]{1,0:T(8,128)S(1)}) custom-call(bf16[16,2,7680]{2,1,0:T(2,128)(2,1)S(1)} %constant_dynamic-update-slice_fusion.same_ref, bf16[16,2,7680]{2,1,0:T(2,128)(2,1)S(1)} %collective-permute-done.2.other_ref, bf16[64,7552]{1,0:T(8,128)(2,1)S(1)} %get-tuple-element.11.weighted_ref, ...), custom_call_target="tpu_custom_call" | custom-call | tf_op jit(solution)/shard_map/post/pallas_call | solution.py:394
  44.9 6.8 %all-to-all-done.1.arrived_ref = bf16[16,120,128]{2,1,0:T(8,128)(2,1)S(1)} async-done(((bf16[16,120,128]{2,1,0:T(8,128)(2,1)}), bf16[16,120,128]{2,1,0:T(8,128)(2,1)S(1)}, u32[]{:S(2)}, u32[]{:S(2)}) %all-to-all-start.1) | async-done | bytes 491552 | tf_op jit(solution)/shard_map/all_to_all | solution.py:374
  51.7 0.7 %means.1 = f32[1,2,7488]{2,1,0:T(2,128)} custom-call(bf16[16,120,128]{2,1,0:T(8,128)(2,1)S(1)} %all-to-all-done.1.arrived_ref, f32[64,128]{1,0:T(8,128)S(1)} %get-tuple-element.17.bottom_ref), custom_call_target="tpu_custom_call" | custom-call | tf_op jit(solution)/shard_map/means/pallas_call | solution.py:407
  (6 shorter events, 0.0 us)
Async XLA Ops:
  0.6 0.7 %copy-start.4 = (s32[2,32]{1,0:T(2,128)S(1)}, s32[2,32]{1,0:T(2,128)}, u32[]{:S(2)}) copy-start(s32[2,32]{1,0:T(2,128)} %tilt_ref.3) | copy-start | bytes 772
  0.6 0.7 %copy-start.5 = (s32[32,1]{0,1:T(1,128)S(1)}, s32[32,1]{0,1:T(1,128)}, u32[]{:S(2)}) copy-start(s32[32,1]{0,1:T(1,128)} %param.7) | copy-start | bytes 388
  1.3 0.8 %copy-start.3 = (bf16[1,2,7488]{2,1,0:T(2,128)(2,1)S(1)}, bf16[1,2,7488]{2,1,0:T(2,128)(2,1)}, u32[]{:S(2)}) copy-start(bf16[1,2,7488]{2,1,0:T(2,128)(2,1)} %ref_ref.1) | copy-start | bytes 89860
  2.1 0.7 %copy-start.6 = (s32[32]{0:T(128)S(1)}, s32[32]{0:T(128)}, u32[]{:S(2)}) copy-start(s32[32]{0:T(128)} %orient_ref.3) | copy-start | bytes 388
  3.5 6.4 %copy-start.7 = (s32[32]{0:T(128)S(1)}, s32[32]{0:T(128)}, u32[]{:S(2)}) copy-start(s32[32]{0:T(128)} %orient_ref.3) | copy-start | bytes 388
  3.5 17.6 %all-to-all-start = ((bf16[4,2,7680]{2,1,0:T(2,128)(2,1)}), bf16[4,2,7680]{2,1,0:T(2,128)(2,1)}, u32[]{:S(2)}, u32[]{:S(2)}) async-start(bf16[4,2,7680]{2,1,0:T(2,128)(2,1)} %pack.1), calls=%async_computation | async-start | bytes 245760 | tf_op jit(solution)/shard_map/all_to_all | solution.py:349
  9.9 1.2 %copy-start = (bf16[32,2,7488]{2,1,0:T(2,128)(2,1)S(1)}, bf16[32,2,7488]{2,1,0:T(2,128)(2,1)}, u32[]{:S(2)}) copy-start(bf16[32,2,7488]{2,1,0:T(2,128)(2,1)} %x_ref.1) | copy-start | bytes 2875396
  20.3 0.8 %copy-start.1 = (bf16[32,7552]{1,0:T(8,128)(2,1)}, bf16[32,7552]{1,0:T(8,128)(2,1)S(1)}, u32[]{:S(2)}) copy-start(bf16[32,7552]{1,0:T(8,128)(2,1)S(1)} %get-tuple-element.12.low_ref) | copy-start | bytes 1449988
  21.1 9.5 %collective-permute-start.3 = (f32[1936,128]{1,0:T(8,128)}, f32[1936,128]{1,0:T(8,128)S(1)}, u32[]{:S(2)}, u32[]{:S(2)}) collective-permute-start(f32[1936,128]{1,0:T(8,128)} %get-tuple-element.16), channel_id=1, source_target_pairs={{0,1},{1,0},{2,3},{3,2},{4,5},{5,4},{6,7},{7,6},{8,9},{9,8},{10,11... | collective-permute-start | bytes 2973704 | tf_op jit(solution)/shard_map/ppermute | solution.py:365
  21.1 5.9 %collective-permute-start = (bf16[4,2,7680]{2,1,0:T(2,128)(2,1)}, bf16[4,2,7680]{2,1,0:T(2,128)(2,1)S(1)}, u32[]{:S(2)}, u32[]{:S(2)}) collective-permute-start(bf16[4,2,7680]{2,1,0:T(2,128)(2,1)} %all-to-all-done), channel_id=1, source_target_pairs={{0,2},{1,3},{2,0},{3,1},{4,6},{5,7},{6,4},{7,5},{8,10},{9,11},{10,... | collective-permute-start | bytes 368648 | tf_op jit(solution)/shard_map/ppermute | solution.py:384
  29.0 8.7 %collective-permute-start.1 = (bf16[8,2,7680]{2,1,0:T(2,128)(2,1)}, bf16[8,2,7680]{2,1,0:T(2,128)(2,1)}, u32[]{:S(2)}, u32[]{:S(2)}) collective-permute-start(bf16[8,2,7680]{2,1,0:T(2,128)(2,1)} %pad_maximum_fusion), channel_id=1, source_target_pairs={{0,4},{1,5},{2,6},{3,7},{4,0},{5,1},{6,2},{7,3},{8,12},{9,13},{10,... | collective-permute-start | bytes 737288 | tf_op jit(solution)/shard_map/ppermute | solution.py:384
  31.6 20.2 %all-to-all-start.1 = ((bf16[16,120,128]{2,1,0:T(8,128)(2,1)}), bf16[16,120,128]{2,1,0:T(8,128)(2,1)S(1)}, u32[]{:S(2)}, u32[]{:S(2)}) async-start(bf16[16,120,128]{2,1,0:T(8,128)(2,1)} %add.1), calls=%async_computation.1 | async-start | bytes 983040 | tf_op jit(solution)/shard_map/all_to_all | solution.py:374
  38.8 1.9 %copy-start.2 = (bf16[32,7552]{1,0:T(8,128)(2,1)S(1)}, bf16[32,7552]{1,0:T(8,128)(2,1)}, u32[]{:S(2)}) copy-start(bf16[32,7552]{1,0:T(8,128)(2,1)} %copy-done.1) | copy-start | bytes 1449988
  38.9 1.9 %collective-permute-start.2 = (bf16[16,2,7680]{2,1,0:T(2,128)(2,1)S(1)}, bf16[16,2,7680]{2,1,0:T(2,128)(2,1)S(1)}, u32[]{:S(2)}, u32[]{:S(2)}) collective-permute-start(bf16[16,2,7680]{2,1,0:T(2,128)(2,1)S(1)} %constant_dynamic-update-slice_fusion.same_ref), channel_id=1, source_target_pairs={{0,1},{1,0},{2,3},{3,2},{4,5},{5,4},{6,7},{7,6},{8,9},{9,8},{10,11... | collective-permute-start | bytes 1474568 | tf_op jit(solution)/shard_map/ppermute | solution.py:387

commit v3 on v2

--- a/solution.py
+++ b/solution.py
@@ -17,7 +17,7 @@
 TAU = 0.5
 LOG2E = math.log2(math.e)
 LANES = 128
-STEP = 256
+STEP = 512
 CHUNK = 512
 GROUP = 128
 FAR = 4
@@ -87,9 +87,22 @@
     return jnp.sum(jnp.where(same, row, 0.0), axis=1, keepdims=True)
 
 
-def pack_kernel(padded, ref_ref, cls_ref, orient_ref, tilt_ref, packet_ref, pack, sems):
-    coef = ref_ref.shape[2]
+def pack_kernel(
+    padded, ref_hbm, cls_hbm, orient_hbm, tilt_hbm, packet_ref,
+    ref_buf, cls_ref, orient_ref, tilt_ref, pack, in_sems, sems,
+):
+    coef = ref_hbm.shape[2]
     parts = orient_ref.shape[0]
+    loads = [
+        pltpu.make_async_copy(source, target, in_sems.at[i])
+        for i, (source, target) in enumerate(
+            ((ref_hbm, ref_buf), (cls_hbm, cls_ref), (orient_hbm, orient_ref), (tilt_hbm, tilt_ref))
+        )
+    ]
+    for copy in loads:
+        copy.start()
+    for copy in loads:
+        copy.wait()
     cls = cls_ref[...].reshape(1, parts)
     orient = orient_ref[...].reshape(1, parts)
     first = jnp.where(iota((2, parts), 0) == 0, cls, orient).astype(f32).astype(bf16)
@@ -98,7 +111,8 @@
     labels = dot(first, (lane == source).astype(bf16)) + dot(
         second, (lane == source + parts).astype(bf16)
     )
-    pack[:, 0:coef] = ref_ref[0]
+    pack[:, padded - LANES : padded] = jnp.zeros((2, LANES), bf16)
+    pack[:, 0:coef] = ref_buf[0]
     pack[:, padded : padded + LANES] = labels.astype(bf16)
     copies = [
         pltpu.make_async_copy(pack, packet_ref.at[q], sems.at[q])
@@ -110,20 +124,9 @@
         copy.wait()
 
 
-def pre_kernel(
-    coef, chips, rows, half,
-    x_ref, cls_ref, orient_ref, tilt_ref,
-    keep_ref, send_ref, weighted_ref, low_ref, power_ref,
-):
-    parts = x_ref.shape[0]
-    padded = low_ref.shape[1]
-    full = coef // STEP * STEP
-    cls = cls_ref[...].reshape(1, parts)
+def weights(coef, padded, x_ref, orient_ref, tilt_ref):
+    parts = orient_ref.shape[0]
     orient = orient_ref[...].reshape(1, parts)
-    core = lax.axis_index("dom") % 2
-    order = iota((2 * chips, parts), 0)
-    order = jnp.where(order < chips, 2 * order + core, 2 * (order - chips) + 1 - core)
-    hot = (order == cls).astype(bf16)
     turn = turns(
         to_column(orient.astype(f32)),
         to_column(tilt_ref[0:1, :].astype(f32)),
@@ -134,28 +137,33 @@
     out_row, in_row = iota((2 * parts, 2 * parts), 0), iota((2 * parts, 2 * parts), 1)
     wanted = jnp.where(out_row < parts, 2 * out_row, 2 * (out_row - parts) + 1)
     split = (in_row == wanted).astype(bf16)
-
-    def block(x, start, width, valid):
-        both = dot(split, x.reshape(2 * parts, x.shape[2]))
+    for start in range(0, padded, STEP):
+        width = min(STEP, padded - start)
+        valid = min(STEP, coef - start)
+        both = dot(split, x_ref[:, :, start : start + valid].reshape(2 * parts, valid))
         if valid < width:
             both = jnp.concatenate([both, jnp.zeros((2 * parts, width - valid), f32)], axis=1)
-        real, imag = both[:parts], both[parts:]
         index = (iota((1, width), 1) + start).astype(f32)
         wedge = wedge_of(*freqs(index), *factors)
         if valid < width:
             wedge = jnp.where(index < coef, wedge, 0.0)
-        cols = pl.ds(start, width)
-        low_ref[:, cols] = wedge.astype(bf16)
-        energy = wedge * (real * real + imag * imag)
-        total = energy[:, :LANES]
-        for j in range(1, width // LANES):
-            total = total + energy[:, j * LANES : (j + 1) * LANES]
-        power_ref[...] += total
+        yield start, width, wedge, both[:parts], both[parts:]
+
+
+def sums_kernel(
+    coef, chips, rows, half, x_ref, cls_ref, orient_ref, tilt_ref, keep_ref, send_ref
+):
+    parts = orient_ref.shape[0]
+    cls = cls_ref[...].reshape(1, parts)
+    core = lax.axis_index("dom") % 2
+    order = iota((2 * chips, parts), 0)
+    order = jnp.where(order < chips, 2 * order + core, 2 * (order - chips) + 1 - core)
+    hot = (order == cls).astype(bf16)
+    padded = -(-coef // LANES) * LANES
+    for start, width, wedge, real, imag in weights(coef, padded, x_ref, orient_ref, tilt_ref):
         tile = start // LANES
         for part, value in enumerate((real, imag)):
-            value = (wedge * value).astype(bf16)
-            weighted_ref[part * parts : (part + 1) * parts, cols] = value
-            summed = dot(hot, value)
+            summed = dot(hot, (wedge * value).astype(bf16))
             for j in range(width // LANES):
                 for q in range(0, chips, 8):
                     place = pl.ds(q * rows + part * half + tile + j, 8, stride=rows)
@@ -163,21 +171,37 @@
                     keep_ref[place, :] = summed[q : q + 8, lanes]
                     send_ref[place, :] = summed[chips + q : chips + q + 8, lanes]
 
-    power_ref[...] = jnp.zeros_like(power_ref)
-
-    def step(s, carry):
-        start = pl.multiple_of(s * STEP, STEP)
-        block(x_ref[:, :, pl.ds(start, STEP)], start, STEP, STEP)
-        return carry
-
-    lax.fori_loop(0, full // STEP, step, 0)
-    block(x_ref[:, :, full:coef], full, padded - full, coef - full)
+
+def weigh_kernel(coef, x_ref, orient_ref, tilt_ref, weighted_ref, low_ref, power_ref):
+    parts, padded = low_ref.shape
+    total = jnp.zeros(power_ref.shape, f32)
+    for start, width, wedge, real, imag in weights(coef, padded, x_ref, orient_ref, tilt_ref):
+        cols = slice(start, start + width)
+        low_ref[:, cols] = wedge.astype(bf16)
+        energy = wedge * (real * real + imag * imag)
+        for j in range(width // LANES):
+            total = total + energy[:, j * LANES : (j + 1) * LANES]
+        weighted_ref[:parts, cols] = (wedge * real).astype(bf16)
+        weighted_ref[parts:, cols] = (wedge * imag).astype(bf16)
+    power_ref[...] = total
 
 
 def add_kernel(chips, rows, room, keep_ref, got_ref, out_ref):
     for q in range(chips):
         place = pl.ds(q * rows, room)
         out_ref[q] = (keep_ref[place, :] + got_ref[place, :]).astype(bf16)
+
+
+def join_kernel(*refs):
+    *pieces, out_ref, sems = refs
+    copies = [
+        pltpu.make_async_copy(piece, out_ref.at[pl.ds(i * FAR, FAR)], sems.at[i])
+        for i, piece in enumerate(pieces)
+    ]
+    for copy in copies:
+        copy.start()
+    for copy in copies:
+        copy.wait()
 
 
 def table_kernel(table_ref):
@@ -207,7 +231,8 @@
         device = out_row - part * devices
         chip = device // 2
         near = (chip % per_far) ^ (me // 2 % per_far)
-        place = near * FAR + chip // per_far
+        far = (chip // per_far) ^ (me // 2 // per_far)
+        place = near * FAR + far
         return (in_row == 2 * place + part) & (device % 2 == parity)
 
     pick_a, pick_b = picker(core).astype(bf16), picker(1 - core).astype(bf16)
@@ -322,7 +347,6 @@
     assert owned == 1 and classes <= 256 and chips % 8 == 0 and chips & (chips - 1) == 0 and 2 * part_rows <= LANES
     groups = [[2 * q + c for q in range(chips)] for c in range(2)]
     near = devices // FAR
-    far = [[d + near * q for q in range(FAR)] for d in range(near)]
     swap = [(d, d ^ 1) for d in range(devices)]
     tiles = -(-coef // LANES)
     half = -(-tiles // 4) * 4
@@ -330,7 +354,6 @@
     rows = room + 1
     padded = tiles * LANES
     wide = padded + LANES
-    assert padded - coef // STEP * STEP <= LANES
     shape = jax.ShapeDtypeStruct
     hbm = pl.BlockSpec(memory_space=pltpu.HBM)
     vmem = pl.BlockSpec(memory_space=VMEM)
@@ -338,29 +361,30 @@
     cls = assignment.reshape(part_rows)
     packet = pl.pallas_call(
         functools.partial(pack_kernel, padded),
-        out_shape=shape((FAR, 2, wide), bf16),
-        in_specs=[vmem] * 4,
+        out_shape=shape((1, 2, wide), bf16),
+        in_specs=[hbm] * 4,
         out_specs=hbm,
-        scratch_shapes=[VMEM((2, wide), bf16), pltpu.SemaphoreType.DMA((FAR,))],
-        compiler_params=pltpu.CompilerParams(vmem_limit_bytes=4 << 20),
+        scratch_shapes=[
+            VMEM(references.shape, bf16),
+            VMEM((part_rows,), i32),
+            VMEM((part_rows,), i32),
+            VMEM(tilt_range.shape, i32),
+            VMEM((2, wide), bf16),
+            pltpu.SemaphoreType.DMA((4,)),
+            pltpu.SemaphoreType.DMA((1,)),
+        ],
+        cost_estimate=pl.CostEstimate(flops=0, bytes_accessed=20 * 10**6, transcendentals=0),
         name="pack",
     )(references, cls, orientation, tilt_range)
 
-    same = lax.all_to_all(packet, "dom", 0, 0, axis_index_groups=far, tiled=True)
-    outs = (
-        shape((chips * rows, LANES), f32),
-        shape((chips * rows, LANES), f32),
-        shape((2 * part_rows, padded), bf16),
-        shape((part_rows, padded), bf16),
-        shape((part_rows, LANES), f32),
-    )
-    keep, send, weighted, low, power = pl.pallas_call(
-        functools.partial(pre_kernel, coef, chips, rows, half),
+    outs = (shape((chips * rows, LANES), f32), shape((chips * rows, LANES), f32))
+    keep, send = pl.pallas_call(
+        functools.partial(sums_kernel, coef, chips, rows, half),
         out_shape=outs,
-        in_specs=[vmem, vmem, vmem, vmem],
-        out_specs=(vmem, vmem, vmem, vmem, vmem),
+        in_specs=[vmem] * 4,
+        out_specs=(vmem, vmem),
         compiler_params=limit(*outs, particles),
-        name="pre",
+        name="sums",
     )(particles, cls, orientation, tilt_range)
     got = lax.ppermute(send, "dom", swap)
     chip_sum = pl.pallas_call(
@@ -372,6 +396,25 @@
         name="add",
     )(keep, got)
     arrived = lax.all_to_all(chip_sum, "dom", 0, 0, axis_index_groups=groups, tiled=True)
+    pieces = [packet]
+    for j in range(1, FAR):
+        hop = [(d, d ^ (near * j)) for d in range(devices)]
+        pieces.append(lax.ppermute(packet, "dom", hop))
+    same = jnp.concatenate(pieces)
+    outs = (
+        shape((2 * part_rows, padded), bf16),
+        shape((part_rows, padded), bf16),
+        shape((part_rows, LANES), f32),
+    )
+    weighted, low, power = pl.pallas_call(
+        functools.partial(weigh_kernel, coef),
+        out_shape=outs,
+        in_specs=[vmem] * 3,
+        out_specs=(vmem, vmem, vmem),
+        compiler_params=limit(*outs, particles),
+        cost_estimate=pl.CostEstimate(flops=10**7, bytes_accessed=10**6, transcendentals=0),
+        name="weigh",
+    )(particles, orientation, tilt_range)
     table = pl.pallas_call(
         table_kernel,
         out_shape=shape((3, 8, padded), f32),
@@ -379,11 +422,19 @@
         compiler_params=pltpu.CompilerParams(vmem_limit_bytes=4 << 20),
         name="table",
     )()
-    bit = 1
-    while bit < chips // FAR:
-        swapped = lax.ppermute(same, "dom", [(d, d ^ (2 * bit)) for d in range(devices)])
-        same = jnp.concatenate([same, swapped])
-        bit *= 2
+    pieces = [same]
+    for j in range(1, chips // FAR):
+        hop = [(d, d ^ (2 * j)) for d in range(devices)]
+        pieces.append(lax.ppermute(same, "dom", hop))
+    same = pl.pallas_call(
+        join_kernel,
+        out_shape=shape((chips, 2, wide), bf16),
+        in_specs=[hbm] * len(pieces),
+        out_specs=hbm,
+        scratch_shapes=[pltpu.SemaphoreType.DMA((len(pieces),))],
+        compiler_params=pltpu.CompilerParams(vmem_limit_bytes=4 << 20),
+        name="join",
+    )(*pieces)
     other = lax.ppermute(same, "dom", swap)
 
     outs = (

time: 53 us -> 42.9 us (0.81)
  Pallas kernels: 16 us -> 12 us
  local copies, waits for them, and re-layouts: 6.33 us -> 2.95 us
  waiting for transfers between devices: 11.9 us -> 8.78 us
  starting transfers between devices: 15.6 us -> 16.6 us
  other arithmetic: 1.92 us -> 1.05 us
    all_to_all x1, waiting for transfers between devices: 6.81 us -> 0.01 us  [body(): lax.all_to_all(chip_sum, 'dom', 0, 0, axis_index_groups=groups, tiled=True)]
    all_to_all x1 -> x0, starting transfers between devices: 6.36 us -> none  [body(): lax.all_to_all(packet, 'dom', 0, 0, axis_index_groups=far, tiled=True)]
    ppermute x2 -> x6, starting transfers between devices: 3.01 us -> 8.86 us  [the longest x3 5.31 us: body(): pieces.append(lax.ppermute(packet, 'dom', hop))]
    ppermute x2 -> x6, waiting for transfers between devices: 3.43 us -> 8.77 us  [the longest x3 8.76 us: body(): pieces.append(lax.ppermute(same, 'dom', hop))]
    pallas_call x2 -> x4, Pallas kernels: 10 us -> 5.99 us  [the longest x1 2.54 us: body(): pl.pallas_call(functools.partial(sums_kernel, coef, chips, rows, half), o...]
    unnamed x18 -> x16, local copies, waits for them, and re-layouts: 5.2 us -> 2.95 us
    ppermute x1, waiting for transfers between devices: 1.69 us -> 0.01 us  [body(): other = lax.ppermute(same, 'dom', swap)]
    concatenate x1 -> x0, local copies, waits for them, and re-layouts: 1.14 us -> none  [body(): same = jnp.concatenate([same, swapped])]
  transfers between devices with their start and end apart: 6 -> 9, of which waited for: 3 -> 3; matrix products, arithmetic and copies ran while one was open for 8% -> 2% of each run, Pallas kernels for 28% -> 21%
where the time goes in v3:
time: 42.9 us; the launch traced here: 42.2 us
  starting transfers between devices  16.6 us (39%)
  Pallas kernels  12 us (28%)
  waiting for transfers between devices  8.78 us (20%)
  local copies, waits for them, and re-layouts  2.95 us (7%)
  other arithmetic  1.05 us (2%)
  between operations  0.78 us (2%)
    ppermute x3, waiting for transfers between devices, body(): pieces.append(lax.ppermute(same, 'dom', hop))  8.76 us
    all_to_all x1, starting transfers between devices, body(): lax.all_to_all(chip_sum, 'dom', 0, 0, axis_index_groups=groups, tiled=True)  7.14 us
    ppermute x3, starting transfers between devices, body(): pieces.append(lax.ppermute(packet, 'dom', hop))  5.31 us
    pallas_call x1, Pallas kernels, body(): pl.pallas_call(functools.partial(post_kernel, coef), out_shape=outs, in_s...  4.16 us
    ppermute x3, starting transfers between devices, body(): pieces.append(lax.ppermute(same, 'dom', hop))  3.55 us
    unnamed x16, local copies, waits for them, and re-layouts  2.95 us
    pallas_call x1, Pallas kernels, body(): pl.pallas_call(functools.partial(sums_kernel, coef, chips, rows, half), o...  2.54 us
    pallas_call x1, Pallas kernels, body(): pl.pallas_call(functools.partial(pack_kernel, padded), out_shape=shape((1...  1.53 us
  transfers between devices with their start and end apart: 9, of which 3 were waited for; matrix products, arithmetic and copies ran while one was open for 2% of the time, Pallas kernels for 21%

profile of v3, /device:TPU:0, one launch (start us, length us, event | category | flops | bytes accessed | tf_op | source)
XLA Modules:
  0.0 42.2 jit_solution(14105775102895762745)
XLA Ops:
  0.6 0.0 copy-start.2
  0.6 0.0 copy-start.4
  0.7 0.7 %copy-done.2 = s32[2,32]{1,0:T(2,128)S(1)} copy-done((s32[2,32]{1,0:T(2,128)S(1)}, s32[2,32]{1,0:T(2,128)}, u32[]{:S(2)}) %copy-start.2) | copy-done | bytes 280
  1.3 1.2 %copy-done = bf16[32,2,7488]{2,1,0:T(2,128)(2,1)S(1)} copy-done((bf16[32,2,7488]{2,1,0:T(2,128)(2,1)S(1)}, bf16[32,2,7488]{2,1,0:T(2,128)(2,1)}, u32[]{:S(2)}) %copy-start) | copy-done | bytes 958488
  2.5 0.7 %copy-done.6 = s32[32,1]{0,1:T(1,128)S(1)} copy-done((s32[32,1]{0,1:T(1,128)S(1)}, s32[32,1]{0,1:T(1,128)}, u32[]{:S(2)}) %copy-start.6) | copy-done | bytes 152
  3.2 2.5 %sums.1 = (f32[1936,128]{1,0:T(8,128)S(1)}, f32[1936,128]{1,0:T(8,128)S(1)}) custom-call(bf16[32,2,7488]{2,1,0:T(2,128)(2,1)S(1)} %copy-done, s32[32]{0:T(128)S(1)} %bitcast.3, s32[32]{0:T(128)S(1)} %copy-done.4, s32[2,32]{1,0:T(2,128)S(1)} %copy-done.2), custom_call_target="tpu_custom_call" | custom-call | tf_op jit(solution)/shard_map/sums/pallas_call | solution.py:381
  5.7 0.6 %collective-permute-start.7 = (f32[1936,128]{1,0:T(8,128)S(1)}, f32[1936,128]{1,0:T(8,128)S(1)}, u32[]{:S(2)}, u32[]{:S(2)}) collective-permute-start(f32[1936,128]{1,0:T(8,128)S(1)} %get-tuple-element.16), channel_id=1, source_target_pairs={{0,1},{1,0},{2,3},{3,2},{4,5},{5,4},{6,7},{7,6},{8,9},{9,8},{10,11... | collective-permute-start | bytes 2973704 | tf_op jit(solution)/shard_map/ppermute | solution.py:389
  6.3 1.5 %pack.1 = bf16[1,2,7680]{2,1,0:T(2,128)(2,1)} custom-call(bf16[1,2,7488]{2,1,0:T(2,128)(2,1)} %ref_hbm.1, s32[32]{0:T(128)} %bitcast.2, s32[32]{0:T(128)} %orient_ref.3, s32[2,32]{1,0:T(2,128)} %tilt_ref.3), custom_call_target="tpu_custom_call" | custom-call | bytes 20000000 | tf_op jit(solution)/shard_map/pack/pallas_call | solution.py:362
  7.8 4.7 %collective-permute-start.2 = (bf16[1,2,7680]{2,1,0:T(2,128)(2,1)}, bf16[1,2,7680]{2,1,0:T(2,128)(2,1)S(1)}, u32[]{:S(2)}, u32[]{:S(2)}) collective-permute-start(bf16[1,2,7680]{2,1,0:T(2,128)(2,1)} %pack.1), channel_id=1, source_target_pairs={{0,24},{1,25},{2,26},{3,27},{4,28},{5,29},{6,30},{7,31},{8,16},{9,... | collective-permute-start | bytes 92168 | tf_op jit(solution)/shard_map/ppermute | solution.py:402
  12.5 0.0 collective-permute-start.1
  12.5 0.6 %collective-permute-start = (bf16[1,2,7680]{2,1,0:T(2,128)(2,1)}, bf16[1,2,7680]{2,1,0:T(2,128)(2,1)}, u32[]{:S(2)}, u32[]{:S(2)}) collective-permute-start(bf16[1,2,7680]{2,1,0:T(2,128)(2,1)} %pack.1), channel_id=1, source_target_pairs={{0,8},{1,9},{2,10},{3,11},{4,12},{5,13},{6,14},{7,15},{8,0},{9,1},... | collective-permute-start | bytes 92168 | tf_op jit(solution)/shard_map/ppermute | solution.py:402
  13.1 1.0 %add.1 = bf16[16,120,128]{2,1,0:T(8,128)(2,1)} custom-call(f32[1936,128]{1,0:T(8,128)S(1)} %get-tuple-element.15.keep_ref, f32[1936,128]{1,0:T(8,128)S(1)} %collective-permute-done.7.got_ref), custom_call_target="tpu_custom_call" | custom-call | tf_op jit(solution)/shard_map/add/pallas_call | solution.py:390
  14.1 7.1 %all-to-all-start = ((bf16[16,120,128]{2,1,0:T(8,128)(2,1)}), bf16[16,120,128]{2,1,0:T(8,128)(2,1)S(1)}, u32[]{:S(2)}, u32[]{:S(2)}) async-start(bf16[16,120,128]{2,1,0:T(8,128)(2,1)} %add.1), calls=%async_computation | async-start | bytes 983040 | tf_op jit(solution)/shard_map/all_to_all | solution.py:398
  21.2 0.0 copy-start.1
  21.2 0.0 collective-permute-done.2
  21.3 1.0 %pad_maximum_fusion.refs_0_ = bf16[4,2,7680]{2,1,0:T(2,128)(2,1)S(1)} fusion(bf16[1,2,7680]{2,1,0:T(2,128)(2,1)S(1)} %collective-permute-done.2, bf16[1,2,7680]{2,1,0:T(2,128)(2,1)S(1)} %collective-permute-done.1, bf16[1,2,7680]{2,1,0:T(2,128)(2,1)} %collective-permute-done, bf16[1,2,7680]{2,1,0:T(2,128)(2,1)S(1)} %copy-done.7), kind=kLoop, calls=%fused_computation | loop fusion | flops 184320 | bytes 245760 | tf_op jit(solution)/shard_map/concatenate | solution.py:403
  22.3 2.9 %collective-permute-start.5 = (bf16[4,2,7680]{2,1,0:T(2,128)(2,1)S(1)}, bf16[4,2,7680]{2,1,0:T(2,128)(2,1)S(1)}, u32[]{:S(2)}, u32[]{:S(2)}) collective-permute-start(bf16[4,2,7680]{2,1,0:T(2,128)(2,1)S(1)} %pad_maximum_fusion.refs_0_), channel_id=1, source_target_pairs={{0,6},{1,7},{2,4},{3,5},{4,2},{5,3},{6,0},{7,1},{8,14},{9,15},{10,... | collective-permute-start | bytes 368648 | tf_op jit(solution)/shard_map/ppermute | solution.py:428
  25.2 0.6 %collective-permute-start.4 = (bf16[4,2,7680]{2,1,0:T(2,128)(2,1)S(1)}, bf16[4,2,7680]{2,1,0:T(2,128)(2,1)S(1)}, u32[]{:S(2)}, u32[]{:S(2)}) collective-permute-start(bf16[4,2,7680]{2,1,0:T(2,128)(2,1)S(1)} %pad_maximum_fusion.refs_0_), channel_id=1, source_target_pairs={{0,4},{1,5},{2,6},{3,7},{4,0},{5,1},{6,2},{7,3},{8,12},{9,13},{10,... | collective-permute-start | bytes 368648 | tf_op jit(solution)/shard_map/ppermute | solution.py:428
  25.8 0.1 collective-permute-start.3
  25.9 7.3 %collective-permute-done.5.refs_3_ = bf16[4,2,7680]{2,1,0:T(2,128)(2,1)S(1)} collective-permute-done((bf16[4,2,7680]{2,1,0:T(2,128)(2,1)S(1)}, bf16[4,2,7680]{2,1,0:T(2,128)(2,1)S(1)}, u32[]{:S(2)}, u32[]{:S(2)}) %collective-permute-start.5) | collective-permute-done | bytes 122912 | tf_op jit(solution)/shard_map/ppermute | solution.py:428
  33.2 0.6 %collective-permute-done.4.refs_2_ = bf16[4,2,7680]{2,1,0:T(2,128)(2,1)S(1)} collective-permute-done((bf16[4,2,7680]{2,1,0:T(2,128)(2,1)S(1)}, bf16[4,2,7680]{2,1,0:T(2,128)(2,1)S(1)}, u32[]{:S(2)}, u32[]{:S(2)}) %collective-permute-start.4) | collective-permute-done | bytes 122912 | tf_op jit(solution)/shard_map/ppermute | solution.py:428
  33.8 0.9 %collective-permute-done.3.refs_1_ = bf16[4,2,7680]{2,1,0:T(2,128)(2,1)S(1)} collective-permute-done((bf16[4,2,7680]{2,1,0:T(2,128)(2,1)S(1)}, bf16[4,2,7680]{2,1,0:T(2,128)(2,1)S(1)}, u32[]{:S(2)}, u32[]{:S(2)}) %collective-permute-start.3) | collective-permute-done | bytes 122912 | tf_op jit(solution)/shard_map/ppermute | solution.py:428
  34.7 0.6 %join.1.same_ref = bf16[16,2,7680]{2,1,0:T(2,128)(2,1)S(1)} custom-call(bf16[4,2,7680]{2,1,0:T(2,128)(2,1)S(1)} %pad_maximum_fusion.refs_0_, bf16[4,2,7680]{2,1,0:T(2,128)(2,1)S(1)} %collective-permute-done.3.refs_1_, bf16[4,2,7680]{2,1,0:T(2,128)(2,1)S(1)} %collective-permute-done.4.refs_2_, bf16[4,2,7680]{2,1,0:T(2,128)(2,1)S(1)} %collective-permute-done.5.refs_3_), custom_call_target="tpu_custom_call" | custom-call | tf_op jit(solution)/shard_map/join/pallas_call | solution.py:429
  35.3 0.0 copy-start.3
  35.3 0.0 copy-start.5
  35.3 0.1 collective-permute-start.6
  35.4 0.2 table.1
  35.6 0.4 copy-done.3
  36.0 1.3 %weigh.1 = (bf16[64,7552]{1,0:T(8,128)(2,1)S(1)}, bf16[32,7552]{1,0:T(8,128)(2,1)S(1)}, f32[32,128]{1,0:T(8,128)S(1)}) custom-call(bf16[32,2,7488]{2,1,0:T(2,128)(2,1)S(1)} %copy-done.1, s32[32]{0:T(128)S(1)} %copy-done.5, s32[2,32]{1,0:T(2,128)S(1)} %copy-done.3), custom_call_target="tpu_custom_call" | custom-call | flops 10000000 | bytes 1000000 | tf_op jit(solution)/shard_map/weigh/pallas_call | solution.py:409
  37.3 0.0 collective-permute-done.6.other_ref
  37.3 4.2 %post.1 = (f32[32,32]{1,0:T(8,128)}, f32[1,32]{1,0:T(1,128)}, f32[64,128]{1,0:T(8,128)S(1)}) custom-call(bf16[16,2,7680]{2,1,0:T(2,128)(2,1)S(1)} %join.1.same_ref, bf16[16,2,7680]{2,1,0:T(2,128)(2,1)S(1)} %collective-permute-done.6.other_ref, bf16[64,7552]{1,0:T(8,128)(2,1)S(1)} %get-tuple-element.11.weighted_ref, ...), custom_call_target="tpu_custom_call" | custom-call | tf_op jit(solution)/shard_map/post/pallas_call | solution.py:445
  41.5 0.7 %means.1 = f32[1,2,7488]{2,1,0:T(2,128)} custom-call(bf16[16,120,128]{2,1,0:T(8,128)(2,1)S(1)} %all-to-all-done.arrived_ref, f32[64,128]{1,0:T(8,128)S(1)} %get-tuple-element.17.bottom_ref), custom_call_target="tpu_custom_call" | custom-call | tf_op jit(solution)/shard_map/means/pallas_call | solution.py:458
  (11 shorter events, 0.0 us)
Async XLA Ops:
  0.6 0.7 %copy-start.2 = (s32[2,32]{1,0:T(2,128)S(1)}, s32[2,32]{1,0:T(2,128)}, u32[]{:S(2)}) copy-start(s32[2,32]{1,0:T(2,128)} %tilt_ref.3) | copy-start | bytes 772
  0.6 0.7 %copy-start.4 = (s32[32]{0:T(128)S(1)}, s32[32]{0:T(128)}, u32[]{:S(2)}) copy-start(s32[32]{0:T(128)} %orient_ref.3) | copy-start | bytes 388
  1.3 1.2 %copy-start = (bf16[32,2,7488]{2,1,0:T(2,128)(2,1)S(1)}, bf16[32,2,7488]{2,1,0:T(2,128)(2,1)}, u32[]{:S(2)}) copy-start(bf16[32,2,7488]{2,1,0:T(2,128)(2,1)} %x_ref.3) | copy-start | bytes 2875396
  2.5 0.7 %copy-start.6 = (s32[32,1]{0,1:T(1,128)S(1)}, s32[32,1]{0,1:T(1,128)}, u32[]{:S(2)}) copy-start(s32[32,1]{0,1:T(1,128)} %param.7) | copy-start | bytes 388
  5.7 7.4 %collective-permute-start.7 = (f32[1936,128]{1,0:T(8,128)S(1)}, f32[1936,128]{1,0:T(8,128)S(1)}, u32[]{:S(2)}, u32[]{:S(2)}) collective-permute-start(f32[1936,128]{1,0:T(8,128)S(1)} %get-tuple-element.16), channel_id=1, source_target_pairs={{0,1},{1,0},{2,3},{3,2},{4,5},{5,4},{6,7},{7,6},{8,9},{9,8},{10,11... | collective-permute-start | bytes 2973704 | tf_op jit(solution)/shard_map/ppermute | solution.py:389
  7.8 13.4 %collective-permute-start.2 = (bf16[1,2,7680]{2,1,0:T(2,128)(2,1)}, bf16[1,2,7680]{2,1,0:T(2,128)(2,1)S(1)}, u32[]{:S(2)}, u32[]{:S(2)}) collective-permute-start(bf16[1,2,7680]{2,1,0:T(2,128)(2,1)} %pack.1), channel_id=1, source_target_pairs={{0,24},{1,25},{2,26},{3,27},{4,28},{5,29},{6,30},{7,31},{8,16},{9,... | collective-permute-start | bytes 92168 | tf_op jit(solution)/shard_map/ppermute | solution.py:402
  12.5 8.8 %collective-permute-start.1 = (bf16[1,2,7680]{2,1,0:T(2,128)(2,1)}, bf16[1,2,7680]{2,1,0:T(2,128)(2,1)S(1)}, u32[]{:S(2)}, u32[]{:S(2)}) collective-permute-start(bf16[1,2,7680]{2,1,0:T(2,128)(2,1)} %pack.1), channel_id=1, source_target_pairs={{0,16},{1,17},{2,18},{3,19},{4,20},{5,21},{6,22},{7,23},{8,24},{9,... | collective-permute-start | bytes 92168 | tf_op jit(solution)/shard_map/ppermute | solution.py:402
  12.5 8.8 %collective-permute-start = (bf16[1,2,7680]{2,1,0:T(2,128)(2,1)}, bf16[1,2,7680]{2,1,0:T(2,128)(2,1)}, u32[]{:S(2)}, u32[]{:S(2)}) collective-permute-start(bf16[1,2,7680]{2,1,0:T(2,128)(2,1)} %pack.1), channel_id=1, source_target_pairs={{0,8},{1,9},{2,10},{3,11},{4,12},{5,13},{6,14},{7,15},{8,0},{9,1},... | collective-permute-start | bytes 92168 | tf_op jit(solution)/shard_map/ppermute | solution.py:402
  14.1 7.2 %copy-start.7 = (bf16[1,2,7680]{2,1,0:T(2,128)(2,1)S(1)}, bf16[1,2,7680]{2,1,0:T(2,128)(2,1)}, u32[]{:S(2)}) copy-start(bf16[1,2,7680]{2,1,0:T(2,128)(2,1)} %pack.1) | copy-start | bytes 92164
  14.1 27.4 %all-to-all-start = ((bf16[16,120,128]{2,1,0:T(8,128)(2,1)}), bf16[16,120,128]{2,1,0:T(8,128)(2,1)S(1)}, u32[]{:S(2)}, u32[]{:S(2)}) async-start(bf16[16,120,128]{2,1,0:T(8,128)(2,1)} %add.1), calls=%async_computation | async-start | bytes 983040 | tf_op jit(solution)/shard_map/all_to_all | solution.py:398
  21.2 14.3 %copy-start.1 = (bf16[32,2,7488]{2,1,0:T(2,128)(2,1)S(1)}, bf16[32,2,7488]{2,1,0:T(2,128)(2,1)}, u32[]{:S(2)}) copy-start(bf16[32,2,7488]{2,1,0:T(2,128)(2,1)} %x_ref.3) | copy-start | bytes 2875396
  22.3 10.9 %collective-permute-start.5 = (bf16[4,2,7680]{2,1,0:T(2,128)(2,1)S(1)}, bf16[4,2,7680]{2,1,0:T(2,128)(2,1)S(1)}, u32[]{:S(2)}, u32[]{:S(2)}) collective-permute-start(bf16[4,2,7680]{2,1,0:T(2,128)(2,1)S(1)} %pad_maximum_fusion.refs_0_), channel_id=1, source_target_pairs={{0,6},{1,7},{2,4},{3,5},{4,2},{5,3},{6,0},{7,1},{8,14},{9,15},{10,... | collective-permute-start | bytes 368648 | tf_op jit(solution)/shard_map/ppermute | solution.py:428
  25.2 8.6 %collective-permute-start.4 = (bf16[4,2,7680]{2,1,0:T(2,128)(2,1)S(1)}, bf16[4,2,7680]{2,1,0:T(2,128)(2,1)S(1)}, u32[]{:S(2)}, u32[]{:S(2)}) collective-permute-start(bf16[4,2,7680]{2,1,0:T(2,128)(2,1)S(1)} %pad_maximum_fusion.refs_0_), channel_id=1, source_target_pairs={{0,4},{1,5},{2,6},{3,7},{4,0},{5,1},{6,2},{7,3},{8,12},{9,13},{10,... | collective-permute-start | bytes 368648 | tf_op jit(solution)/shard_map/ppermute | solution.py:428
  25.8 8.9 %collective-permute-start.3 = (bf16[4,2,7680]{2,1,0:T(2,128)(2,1)S(1)}, bf16[4,2,7680]{2,1,0:T(2,128)(2,1)S(1)}, u32[]{:S(2)}, u32[]{:S(2)}) collective-permute-start(bf16[4,2,7680]{2,1,0:T(2,128)(2,1)S(1)} %pad_maximum_fusion.refs_0_), channel_id=1, source_target_pairs={{0,2},{1,3},{2,0},{3,1},{4,6},{5,7},{6,4},{7,5},{8,10},{9,11},{10,... | collective-permute-start | bytes 368648 | tf_op jit(solution)/shard_map/ppermute | solution.py:428
  35.3 0.7 %copy-start.3 = (s32[2,32]{1,0:T(2,128)S(1)}, s32[2,32]{1,0:T(2,128)}, u32[]{:S(2)}) copy-start(s32[2,32]{1,0:T(2,128)} %tilt_ref.3) | copy-start | bytes 772
  35.3 0.7 %copy-start.5 = (s32[32]{0:T(128)S(1)}, s32[32]{0:T(128)}, u32[]{:S(2)}) copy-start(s32[32]{0:T(128)} %orient_ref.3) | copy-start | bytes 388
  35.3 1.9 %collective-permute-start.6 = (bf16[16,2,7680]{2,1,0:T(2,128)(2,1)S(1)}, bf16[16,2,7680]{2,1,0:T(2,128)(2,1)S(1)}, u32[]{:S(2)}, u32[]{:S(2)}) collective-permute-start(bf16[16,2,7680]{2,1,0:T(2,128)(2,1)S(1)} %join.1.same_ref), channel_id=1, source_target_pairs={{0,1},{1,0},{2,3},{3,2},{4,5},{5,4},{6,7},{7,6},{8,9},{9,8},{10,11... | collective-permute-start | bytes 1474568 | tf_op jit(solution)/shard_map/ppermute | solution.py:438

commit v4 on v3

--- a/solution.py
+++ b/solution.py
@@ -87,52 +87,9 @@
     return jnp.sum(jnp.where(same, row, 0.0), axis=1, keepdims=True)
 
 
-def pack_kernel(
-    padded, ref_hbm, cls_hbm, orient_hbm, tilt_hbm, packet_ref,
-    ref_buf, cls_ref, orient_ref, tilt_ref, pack, in_sems, sems,
-):
-    coef = ref_hbm.shape[2]
-    parts = orient_ref.shape[0]
-    loads = [
-        pltpu.make_async_copy(source, target, in_sems.at[i])
-        for i, (source, target) in enumerate(
-            ((ref_hbm, ref_buf), (cls_hbm, cls_ref), (orient_hbm, orient_ref), (tilt_hbm, tilt_ref))
-        )
-    ]
-    for copy in loads:
-        copy.start()
-    for copy in loads:
-        copy.wait()
-    cls = cls_ref[...].reshape(1, parts)
-    orient = orient_ref[...].reshape(1, parts)
-    first = jnp.where(iota((2, parts), 0) == 0, cls, orient).astype(f32).astype(bf16)
-    second = tilt_ref[...].astype(f32).astype(bf16)
-    source, lane = iota((parts, LANES), 0), iota((parts, LANES), 1)
-    labels = dot(first, (lane == source).astype(bf16)) + dot(
-        second, (lane == source + parts).astype(bf16)
-    )
-    pack[:, padded - LANES : padded] = jnp.zeros((2, LANES), bf16)
-    pack[:, 0:coef] = ref_buf[0]
-    pack[:, padded : padded + LANES] = labels.astype(bf16)
-    copies = [
-        pltpu.make_async_copy(pack, packet_ref.at[q], sems.at[q])
-        for q in range(packet_ref.shape[0])
-    ]
-    for copy in copies:
-        copy.start()
-    for copy in copies:
-        copy.wait()
-
-
-def weights(coef, padded, x_ref, orient_ref, tilt_ref):
-    parts = orient_ref.shape[0]
-    orient = orient_ref[...].reshape(1, parts)
-    turn = turns(
-        to_column(orient.astype(f32)),
-        to_column(tilt_ref[0:1, :].astype(f32)),
-        to_column(tilt_ref[1:2, :].astype(f32)),
-        LANES,
-    )
+def weights(coef, padded, x_ref, label_ref):
+    parts = label_ref.shape[1]
+    turn = turns(*[to_column(label_ref[i : i + 1, :].astype(f32)) for i in (1, 2, 3)], LANES)
     factors = [turn[:, i : i + 1] for i in range(5)]
     out_row, in_row = iota((2 * parts, 2 * parts), 0), iota((2 * parts, 2 * parts), 1)
     wanted = jnp.where(out_row < parts, 2 * out_row, 2 * (out_row - parts) + 1)
@@ -151,16 +108,31 @@
 
 
 def sums_kernel(
-    coef, chips, rows, half, x_ref, cls_ref, orient_ref, tilt_ref, keep_ref, send_ref
+    coef, chips, rows, half, x_ref, ref_ref, label_ref, packet_ref, keep_ref, send_ref
 ):
-    parts = orient_ref.shape[0]
-    cls = cls_ref[...].reshape(1, parts)
-    core = lax.axis_index("dom") % 2
-    order = iota((2 * chips, parts), 0)
-    order = jnp.where(order < chips, 2 * order + core, 2 * (order - chips) + 1 - core)
+    parts = label_ref.shape[1]
+    padded = -(-coef // LANES) * LANES
+    cls = label_ref[0:1, :]
+
+    first = label_ref[0:2, :].astype(f32).astype(bf16)
+    second = label_ref[2:4, :].astype(f32).astype(bf16)
+    source, lane = iota((parts, LANES), 0), iota((parts, LANES), 1)
+    labels = dot(first, (lane == source).astype(bf16)) + dot(
+        second, (lane == source + parts).astype(bf16)
+    )
+    packet_ref[0, :, padded - LANES : padded] = jnp.zeros((2, LANES), bf16)
+    packet_ref[0, :, 0:coef] = ref_ref[0]
+    packet_ref[0, :, padded : padded + LANES] = labels.astype(bf16)
+
+    me = lax.axis_index("dom")
+    core, chip = me % 2, me // 2
+    nears = chips // FAR
+    row = iota((2 * chips, parts), 0)
+    place = row % chips
+    q = ((place % FAR) ^ (chip // nears)) * nears + ((place // FAR) ^ (chip % nears))
+    order = 2 * q + jnp.where(row < chips, core, 1 - core)
     hot = (order == cls).astype(bf16)
-    padded = -(-coef // LANES) * LANES
-    for start, width, wedge, real, imag in weights(coef, padded, x_ref, orient_ref, tilt_ref):
+    for start, width, wedge, real, imag in weights(coef, padded, x_ref, label_ref):
         tile = start // LANES
         for part, value in enumerate((real, imag)):
             summed = dot(hot, (wedge * value).astype(bf16))
@@ -172,10 +144,10 @@
                     send_ref[place, :] = summed[chips + q : chips + q + 8, lanes]
 
 
-def weigh_kernel(coef, x_ref, orient_ref, tilt_ref, weighted_ref, low_ref, power_ref):
+def weigh_kernel(coef, x_ref, label_ref, weighted_ref, low_ref, power_ref):
     parts, padded = low_ref.shape
     total = jnp.zeros(power_ref.shape, f32)
-    for start, width, wedge, real, imag in weights(coef, padded, x_ref, orient_ref, tilt_ref):
+    for start, width, wedge, real, imag in weights(coef, padded, x_ref, label_ref):
         cols = slice(start, start + width)
         low_ref[:, cols] = wedge.astype(bf16)
         energy = wedge * (real * real + imag * imag)
@@ -186,16 +158,43 @@
     power_ref[...] = total
 
 
-def add_kernel(chips, rows, room, keep_ref, got_ref, out_ref):
-    for q in range(chips):
-        place = pl.ds(q * rows, room)
-        out_ref[q] = (keep_ref[place, :] + got_ref[place, :]).astype(bf16)
+def core_kernel(rows, keep_ref, got_ref, *outs):
+    room = outs[0].shape[1]
+    for r in range(len(outs) * FAR):
+        place = pl.ds(r * rows, room)
+        out_ref = outs[r // FAR]
+        out_ref[r % FAR] = (keep_ref[place, :] + got_ref[place, :]).astype(out_ref.dtype)
+
+
+def near_kernel(*refs):
+    own_ref, *came = refs[:-FAR]
+    outs = refs[-FAR:]
+    for k, out_ref in enumerate(outs):
+        total = own_ref[k]
+        for came_ref in came:
+            total = total + came_ref[k].astype(f32)
+        out_ref[0] = total.astype(out_ref.dtype)
+
+
+def join(pieces):
+    size, *rest = pieces[0].shape
+    hbm = pl.BlockSpec(memory_space=pltpu.HBM)
+    return pl.pallas_call(
+        join_kernel,
+        out_shape=jax.ShapeDtypeStruct((size * len(pieces), *rest), pieces[0].dtype),
+        in_specs=[hbm] * len(pieces),
+        out_specs=hbm,
+        scratch_shapes=[pltpu.SemaphoreType.DMA((len(pieces),))],
+        compiler_params=pltpu.CompilerParams(vmem_limit_bytes=4 << 20),
+        name="join",
+    )(*pieces)
 
 
 def join_kernel(*refs):
     *pieces, out_ref, sems = refs
+    size = pieces[0].shape[0]
     copies = [
-        pltpu.make_async_copy(piece, out_ref.at[pl.ds(i * FAR, FAR)], sems.at[i])
+        pltpu.make_async_copy(piece, out_ref.at[pl.ds(i * size, size)], sems.at[i])
         for i, piece in enumerate(pieces)
     ]
     for copy in copies:
@@ -318,11 +317,12 @@
     )
 
 
-def final_kernel(coef, half, arrived_ref, bottom_ref, out_ref, ratio):
+def final_kernel(coef, half, *refs):
+    own_ref, *came, bottom_ref, out_ref, ratio = refs
     tiles = -(-coef // LANES)
-    total = arrived_ref[0].astype(f32)
-    for q in range(1, arrived_ref.shape[0]):
-        total = total + arrived_ref[q].astype(f32)
+    total = own_ref[0]
+    for came_ref in came:
+        total = total + came_ref[0].astype(f32)
     bottom = bottom_ref[...]
     ratio[0:half, :] = total[0:half] / bottom[0:half]
     ratio[half : 2 * half, :] = total[half : 2 * half] / bottom[0:half]
@@ -345,9 +345,6 @@
     chips = devices // 2
     classes = owned * devices
     assert owned == 1 and classes <= 256 and chips % 8 == 0 and chips & (chips - 1) == 0 and 2 * part_rows <= LANES
-    groups = [[2 * q + c for q in range(chips)] for c in range(2)]
-    near = devices // FAR
-    swap = [(d, d ^ 1) for d in range(devices)]
     tiles = -(-coef // LANES)
     half = -(-tiles // 4) * 4
     room = 2 * half
@@ -355,52 +352,56 @@
     padded = tiles * LANES
     wide = padded + LANES
     shape = jax.ShapeDtypeStruct
-    hbm = pl.BlockSpec(memory_space=pltpu.HBM)
     vmem = pl.BlockSpec(memory_space=VMEM)
 
-    cls = assignment.reshape(part_rows)
-    packet = pl.pallas_call(
-        functools.partial(pack_kernel, padded),
-        out_shape=shape((1, 2, wide), bf16),
-        in_specs=[hbm] * 4,
-        out_specs=hbm,
-        scratch_shapes=[
-            VMEM(references.shape, bf16),
-            VMEM((part_rows,), i32),
-            VMEM((part_rows,), i32),
-            VMEM(tilt_range.shape, i32),
-            VMEM((2, wide), bf16),
-            pltpu.SemaphoreType.DMA((4,)),
-            pltpu.SemaphoreType.DMA((1,)),
-        ],
-        cost_estimate=pl.CostEstimate(flops=0, bytes_accessed=20 * 10**6, transcendentals=0),
-        name="pack",
-    )(references, cls, orientation, tilt_range)
-
-    outs = (shape((chips * rows, LANES), f32), shape((chips * rows, LANES), f32))
-    keep, send = pl.pallas_call(
+    labels = jnp.concatenate([assignment.reshape(1, -1), orientation.reshape(1, -1), tilt_range])
+    nears = chips // FAR
+
+    def hops(step):
+        return [(d, d ^ step) for d in range(devices)]
+
+    outs = (
+        shape((1, 2, wide), bf16),
+        shape((chips * rows, LANES), f32),
+        shape((chips * rows, LANES), f32),
+    )
+    packet, keep, send = pl.pallas_call(
         functools.partial(sums_kernel, coef, chips, rows, half),
         out_shape=outs,
-        in_specs=[vmem] * 4,
-        out_specs=(vmem, vmem),
+        in_specs=[vmem] * 3,
+        out_specs=(vmem,) * 3,
         compiler_params=limit(*outs, particles),
         name="sums",
-    )(particles, cls, orientation, tilt_range)
-    got = lax.ppermute(send, "dom", swap)
-    chip_sum = pl.pallas_call(
-        functools.partial(add_kernel, chips, rows, room),
-        out_shape=shape((chips, room, LANES), bf16),
-        in_specs=[vmem, vmem],
-        out_specs=vmem,
-        compiler_params=limit(keep, got, keep),
-        name="add",
+    )(particles, references, labels)
+    got = lax.ppermute(send, "dom", hops(1))
+    pieces = [packet]
+    for k in range(1, FAR):
+        pieces.append(lax.ppermute(packet, "dom", hops(2 * nears * k)))
+    outs = [shape((FAR, room, LANES), f32 if j == 0 else bf16) for j in range(nears)]
+    own, *leave = pl.pallas_call(
+        functools.partial(core_kernel, rows),
+        out_shape=outs,
+        in_specs=[vmem] * 2,
+        out_specs=[vmem] * nears,
+        compiler_params=limit(keep, got, *outs),
+        name="core_add",
     )(keep, got)
-    arrived = lax.all_to_all(chip_sum, "dom", 0, 0, axis_index_groups=groups, tiled=True)
-    pieces = [packet]
-    for j in range(1, FAR):
-        hop = [(d, d ^ (near * j)) for d in range(devices)]
-        pieces.append(lax.ppermute(packet, "dom", hop))
-    same = jnp.concatenate(pieces)
+    came = []
+    for j in range(1, nears):
+        came.append(lax.ppermute(leave[j - 1], "dom", hops(2 * j)))
+    outs = [shape((1, room, LANES), f32 if k == 0 else bf16) for k in range(FAR)]
+    own, *leave = pl.pallas_call(
+        near_kernel,
+        out_shape=outs,
+        in_specs=[vmem] * nears,
+        out_specs=[vmem] * FAR,
+        compiler_params=limit(own, *came, *outs),
+        name="near_add",
+    )(own, *came)
+    came = []
+    for k in range(1, FAR):
+        came.append(lax.ppermute(leave[k - 1], "dom", hops(2 * nears * k)))
+    same = join(pieces)
     outs = (
         shape((2 * part_rows, padded), bf16),
         shape((part_rows, padded), bf16),
@@ -409,12 +410,12 @@
     weighted, low, power = pl.pallas_call(
         functools.partial(weigh_kernel, coef),
         out_shape=outs,
-        in_specs=[vmem] * 3,
+        in_specs=[vmem] * 2,
         out_specs=(vmem, vmem, vmem),
         compiler_params=limit(*outs, particles),
         cost_estimate=pl.CostEstimate(flops=10**7, bytes_accessed=10**6, transcendentals=0),
         name="weigh",
-    )(particles, orientation, tilt_range)
+    )(particles, labels)
     table = pl.pallas_call(
         table_kernel,
         out_shape=shape((3, 8, padded), f32),
@@ -423,19 +424,10 @@
         name="table",
     )()
     pieces = [same]
-    for j in range(1, chips // FAR):
-        hop = [(d, d ^ (2 * j)) for d in range(devices)]
-        pieces.append(lax.ppermute(same, "dom", hop))
-    same = pl.pallas_call(
-        join_kernel,
-        out_shape=shape((chips, 2, wide), bf16),
-        in_specs=[hbm] * len(pieces),
-        out_specs=hbm,
-        scratch_shapes=[pltpu.SemaphoreType.DMA((len(pieces),))],
-        compiler_params=pltpu.CompilerParams(vmem_limit_bytes=4 << 20),
-        name="join",
-    )(*pieces)
-    other = lax.ppermute(same, "dom", swap)
+    for j in range(1, nears):
+        pieces.append(lax.ppermute(same, "dom", hops(2 * j)))
+    same = join(pieces)
+    other = lax.ppermute(same, "dom", hops(1))
 
     outs = (
         shape((part_rows, classes), f32),
@@ -458,12 +450,12 @@
     class_means = pl.pallas_call(
         functools.partial(final_kernel, coef, half),
         out_shape=shape((owned, 2, coef), f32),
-        in_specs=[vmem, vmem],
+        in_specs=[vmem] * (FAR + 1),
         out_specs=vmem,
         scratch_shapes=[VMEM((room, LANES), f32)],
-        compiler_params=limit(arrived),
+        compiler_params=pltpu.CompilerParams(vmem_limit_bytes=4 << 20),
         name="means",
-    )(arrived, bottom)
+    )(own, *came, bottom)
     return (scores, class_means, load.reshape(classes))
 
 

time: 42.9 us -> 45.8 us (1.068); the launches traced: 42.2 us -> 45.6 us
  waiting for transfers between devices: 8.78 us -> 14.8 us
  Pallas kernels: 12 us -> 9.88 us
  other arithmetic: 1.05 us -> 0.01 us
  starting transfers between devices: 16.6 us -> 17.5 us
    ppermute x8 -> x14, starting transfers between devices: 9.49 us -> 17.5 us  [the longest x3 5.3 us: body(): pieces.append(lax.ppermute(packet, 'dom', hops(2 * nears * k)))]
    all_to_all x1 -> x0, starting transfers between devices: 7.14 us -> none  [body(): lax.all_to_all(chip_sum, 'dom', 0, 0, axis_index_groups=groups, tiled=True)]
    ppermute x8 -> x14, waiting for transfers between devices: 8.77 us -> 14.8 us  [the longest x3 5.99 us: body(): came.append(lax.ppermute(leave[j - 1], 'dom', hops(2 * j)))]
    pallas_call x3 -> x4, Pallas kernels: 3.14 us -> 1.04 us  [the longest x2 0.82 us: join(): pl.pallas_call(join_kernel, out_shape=jax.ShapeDtypeStruct((size * len(pi...]
    concatenate x1, other arithmetic: 1.05 us -> 0.01 us  [body(): jnp.concatenate([assignment.reshape(1, -1), orientation.reshape(1, -1), t...]
    unnamed x16 -> x12, local copies, waits for them, and re-layouts: 2.95 us -> 2.62 us
  transfers between devices with their start and end apart: 9 -> 14, of which waited for: 3 -> 7; matrix products, arithmetic and copies ran while one was open for 2% -> 0% of each run, Pallas kernels for 21% -> 15%
where the time goes in v4:
time: 45.8 us; the launch traced here: 45.6 us
  starting transfers between devices  17.5 us (38%)
  waiting for transfers between devices  14.8 us (32%)
  Pallas kernels  9.88 us (22%)
  local copies, waits for them, and re-layouts  2.62 us (6%)
  between operations  0.76 us (2%)
    ppermute x3, waiting for transfers between devices, body(): came.append(lax.ppermute(leave[j - 1], 'dom', hops(2 * j)))  5.99 us
    ppermute x3, starting transfers between devices, body(): pieces.append(lax.ppermute(packet, 'dom', hops(2 * nears * k)))  5.3 us
    ppermute x3, waiting for transfers between devices, body(): pieces.append(lax.ppermute(same, 'dom', hops(2 * j)))  4.68 us
    ppermute x3, starting transfers between devices, body(): came.append(lax.ppermute(leave[k - 1], 'dom', hops(2 * nears * k)))  4.45 us
    pallas_call x1, Pallas kernels, body(): pl.pallas_call(functools.partial(post_kernel, coef), out_shape=outs, in_s...  4.16 us
    ppermute x3, waiting for transfers between devices, body(): pieces.append(lax.ppermute(packet, 'dom', hops(2 * nears * k)))  4.15 us
    ppermute x3, starting transfers between devices, body(): pieces.append(lax.ppermute(same, 'dom', hops(2 * j)))  3.55 us
    ppermute x3, starting transfers between devices, body(): came.append(lax.ppermute(leave[j - 1], 'dom', hops(2 * j)))  3.55 us
  transfers between devices with their start and end apart: 14, of which 7 were waited for; matrix products, arithmetic and copies ran while one was open for 0% of the time, Pallas kernels for 15%

profile of v4, /device:TPU:0, one launch (start us, length us, event | category | flops | bytes accessed | tf_op | source)
XLA Modules:
  0.0 45.6 jit_solution(10341526057199744969)
XLA Ops:
  0.7 0.6 %copy-done.5 = s32[32,1]{0,1:T(1,128)S(1)} copy-done((s32[32,1]{0,1:T(1,128)S(1)}, s32[32,1]{0,1:T(1,128)}, u32[]{:S(2)}) %copy-start.5) | copy-done | bytes 152
  1.4 1.2 %copy-done = bf16[32,2,7488]{2,1,0:T(2,128)(2,1)S(1)} copy-done((bf16[32,2,7488]{2,1,0:T(2,128)(2,1)S(1)}, bf16[32,2,7488]{2,1,0:T(2,128)(2,1)}, u32[]{:S(2)}) %copy-start) | copy-done | bytes 958488
  2.5 0.7 %copy-done.2 = bf16[1,2,7488]{2,1,0:T(2,128)(2,1)S(1)} copy-done((bf16[1,2,7488]{2,1,0:T(2,128)(2,1)S(1)}, bf16[1,2,7488]{2,1,0:T(2,128)(2,1)}, u32[]{:S(2)}) %copy-start.2) | copy-done | bytes 29976
  3.3 2.5 %sums.1 = (bf16[1,2,7680]{2,1,0:T(2,128)(2,1)S(1)}, f32[1936,128]{1,0:T(8,128)S(1)}, f32[1936,128]{1,0:T(8,128)S(1)}) custom-call(bf16[32,2,7488]{2,1,0:T(2,128)(2,1)S(1)} %copy-done, bf16[1,2,7488]{2,1,0:T(2,128)(2,1)S(1)} %copy-done.2, s32[4,32]{1,0:T(4,128)S(1)} %pad_add_fusion.label_ref), custom_call_target="tpu_custom_call" | custom-call | tf_op jit(solution)/shard_map/sums/pallas_call | solution.py:368
  5.8 0.6 %collective-permute-start.7 = (f32[1936,128]{1,0:T(8,128)S(1)}, f32[1936,128]{1,0:T(8,128)S(1)}, u32[]{:S(2)}, u32[]{:S(2)}) collective-permute-start(f32[1936,128]{1,0:T(8,128)S(1)} %get-tuple-element.26), channel_id=1, source_target_pairs={{0,1},{1,0},{2,3},{3,2},{4,5},{5,4},{6,7},{7,6},{8,9},{9,8},{10,11... | collective-permute-start | bytes 2973704 | tf_op jit(solution)/shard_map/ppermute | solution.py:376
  6.4 4.7 %collective-permute-start.2 = (bf16[1,2,7680]{2,1,0:T(2,128)(2,1)S(1)}, bf16[1,2,7680]{2,1,0:T(2,128)(2,1)S(1)}, u32[]{:S(2)}, u32[]{:S(2)}) collective-permute-start(bf16[1,2,7680]{2,1,0:T(2,128)(2,1)S(1)} %get-tuple-element.20.refs_0_), channel_id=1, source_target_pairs={{0,24},{1,25},{2,26},{3,27},{4,28},{5,29},{6,30},{7,31},{8,16},{9,... | collective-permute-start | bytes 92168 | tf_op jit(solution)/shard_map/ppermute | solution.py:379
  11.1 0.6 %collective-permute-start = (bf16[1,2,7680]{2,1,0:T(2,128)(2,1)S(1)}, bf16[1,2,7680]{2,1,0:T(2,128)(2,1)S(1)}, u32[]{:S(2)}, u32[]{:S(2)}) collective-permute-start(bf16[1,2,7680]{2,1,0:T(2,128)(2,1)S(1)} %get-tuple-element.20.refs_0_), channel_id=1, source_target_pairs={{0,8},{1,9},{2,10},{3,11},{4,12},{5,13},{6,14},{7,15},{8,0},{9,1},... | collective-permute-start | bytes 92168 | tf_op jit(solution)/shard_map/ppermute | solution.py:379
  11.7 1.3 %collective-permute-done.2.refs_3_ = bf16[1,2,7680]{2,1,0:T(2,128)(2,1)S(1)} collective-permute-done((bf16[1,2,7680]{2,1,0:T(2,128)(2,1)S(1)}, bf16[1,2,7680]{2,1,0:T(2,128)(2,1)S(1)}, u32[]{:S(2)}, u32[]{:S(2)}) %collective-permute-start.2) | collective-permute-done | bytes 30752 | tf_op jit(solution)/shard_map/ppermute | solution.py:379
  13.0 2.8 %collective-permute-done.1.refs_2_ = bf16[1,2,7680]{2,1,0:T(2,128)(2,1)S(1)} collective-permute-done((bf16[1,2,7680]{2,1,0:T(2,128)(2,1)S(1)}, bf16[1,2,7680]{2,1,0:T(2,128)(2,1)S(1)}, u32[]{:S(2)}, u32[]{:S(2)}) %collective-permute-start.1) | collective-permute-done | bytes 30752 | tf_op jit(solution)/shard_map/ppermute | solution.py:379
  15.9 0.2 join.2.refs_0_
  16.0 2.5 %collective-permute-start.5 = (bf16[4,2,7680]{2,1,0:T(2,128)(2,1)S(1)}, bf16[4,2,7680]{2,1,0:T(2,128)(2,1)S(1)}, u32[]{:S(2)}, u32[]{:S(2)}) collective-permute-start(bf16[4,2,7680]{2,1,0:T(2,128)(2,1)S(1)} %join.2.refs_0_), channel_id=1, source_target_pairs={{0,6},{1,7},{2,4},{3,5},{4,2},{5,3},{6,0},{7,1},{8,14},{9,15},{10,... | collective-permute-start | bytes 368648 | tf_op jit(solution)/shard_map/ppermute | solution.py:428
  18.6 0.5 %collective-permute-start.4 = (bf16[4,2,7680]{2,1,0:T(2,128)(2,1)S(1)}, bf16[4,2,7680]{2,1,0:T(2,128)(2,1)S(1)}, u32[]{:S(2)}, u32[]{:S(2)}) collective-permute-start(bf16[4,2,7680]{2,1,0:T(2,128)(2,1)S(1)} %join.2.refs_0_), channel_id=1, source_target_pairs={{0,4},{1,5},{2,6},{3,7},{4,0},{5,1},{6,2},{7,3},{8,12},{9,13},{10,... | collective-permute-start | bytes 368648 | tf_op jit(solution)/shard_map/ppermute | solution.py:428
  19.1 0.5 %collective-permute-start.3 = (bf16[4,2,7680]{2,1,0:T(2,128)(2,1)S(1)}, bf16[4,2,7680]{2,1,0:T(2,128)(2,1)S(1)}, u32[]{:S(2)}, u32[]{:S(2)}) collective-permute-start(bf16[4,2,7680]{2,1,0:T(2,128)(2,1)S(1)} %join.2.refs_0_), channel_id=1, source_target_pairs={{0,2},{1,3},{2,0},{3,1},{4,6},{5,7},{6,4},{7,5},{8,10},{9,11},{10,... | collective-permute-start | bytes 368648 | tf_op jit(solution)/shard_map/ppermute | solution.py:428
  19.6 2.9 %collective-permute-done.5.refs_3_ = bf16[4,2,7680]{2,1,0:T(2,128)(2,1)S(1)} collective-permute-done((bf16[4,2,7680]{2,1,0:T(2,128)(2,1)S(1)}, bf16[4,2,7680]{2,1,0:T(2,128)(2,1)S(1)}, u32[]{:S(2)}, u32[]{:S(2)}) %collective-permute-start.5) | collective-permute-done | bytes 122912 | tf_op jit(solution)/shard_map/ppermute | solution.py:428
  22.5 1.6 %collective-permute-done.4.refs_2_ = bf16[4,2,7680]{2,1,0:T(2,128)(2,1)S(1)} collective-permute-done((bf16[4,2,7680]{2,1,0:T(2,128)(2,1)S(1)}, bf16[4,2,7680]{2,1,0:T(2,128)(2,1)S(1)}, u32[]{:S(2)}, u32[]{:S(2)}) %collective-permute-start.4) | collective-permute-done | bytes 122912 | tf_op jit(solution)/shard_map/ppermute | solution.py:428
  24.1 0.2 collective-permute-done.3.refs_1_
  24.3 0.6 %join.3.same_ref = bf16[16,2,7680]{2,1,0:T(2,128)(2,1)S(1)} custom-call(bf16[4,2,7680]{2,1,0:T(2,128)(2,1)S(1)} %join.2.refs_0_, bf16[4,2,7680]{2,1,0:T(2,128)(2,1)S(1)} %collective-permute-done.3.refs_1_, bf16[4,2,7680]{2,1,0:T(2,128)(2,1)S(1)} %collective-permute-done.4.refs_2_, bf16[4,2,7680]{2,1,0:T(2,128)(2,1)S(1)} %collective-permute-done.5.refs_3_), custom_call_target="tpu_custom_call" | custom-call | tf_op jit(solution)/shard_map/join/pallas_call | solution.py:182
  24.9 0.1 collective-permute-start.6
  25.0 0.2 core_add.1
  25.2 1.5 %collective-permute-start.8 = (bf16[4,120,128]{2,1,0:T(8,128)(2,1)S(1)}, bf16[4,120,128]{2,1,0:T(8,128)(2,1)S(1)}, u32[]{:S(2)}, u32[]{:S(2)}) collective-permute-start(bf16[4,120,128]{2,1,0:T(8,128)(2,1)S(1)} %get-tuple-element.28), channel_id=1, source_target_pairs={{0,2},{1,3},{2,0},{3,1},{4,6},{5,7},{6,4},{7,5},{8,10},{9,11},{10,... | collective-permute-start | bytes 368648 | tf_op jit(solution)/shard_map/ppermute | solution.py:391
  26.7 0.7 %collective-permute-start.9 = (bf16[4,120,128]{2,1,0:T(8,128)(2,1)S(1)}, bf16[4,120,128]{2,1,0:T(8,128)(2,1)S(1)}, u32[]{:S(2)}, u32[]{:S(2)}) collective-permute-start(bf16[4,120,128]{2,1,0:T(8,128)(2,1)S(1)} %get-tuple-element.29), channel_id=1, source_target_pairs={{0,4},{1,5},{2,6},{3,7},{4,0},{5,1},{6,2},{7,3},{8,12},{9,13},{10,... | collective-permute-start | bytes 368648 | tf_op jit(solution)/shard_map/ppermute | solution.py:391
  27.4 1.3 %collective-permute-start.10 = (bf16[4,120,128]{2,1,0:T(8,128)(2,1)S(1)}, bf16[4,120,128]{2,1,0:T(8,128)(2,1)S(1)}, u32[]{:S(2)}, u32[]{:S(2)}) collective-permute-start(bf16[4,120,128]{2,1,0:T(8,128)(2,1)S(1)} %get-tuple-element.30), channel_id=1, source_target_pairs={{0,6},{1,7},{2,4},{3,5},{4,2},{5,3},{6,0},{7,1},{8,14},{9,15},{10,... | collective-permute-start | bytes 368648 | tf_op jit(solution)/shard_map/ppermute | solution.py:391
  28.7 2.5 %collective-permute-done.8.refs_1_ = bf16[4,120,128]{2,1,0:T(8,128)(2,1)S(1)} collective-permute-done((bf16[4,120,128]{2,1,0:T(8,128)(2,1)S(1)}, bf16[4,120,128]{2,1,0:T(8,128)(2,1)S(1)}, u32[]{:S(2)}, u32[]{:S(2)}) %collective-permute-start.8) | collective-permute-done | bytes 122912 | tf_op jit(solution)/shard_map/ppermute | solution.py:391
  31.3 3.5 %collective-permute-done.9.refs_2_ = bf16[4,120,128]{2,1,0:T(8,128)(2,1)S(1)} collective-permute-done((bf16[4,120,128]{2,1,0:T(8,128)(2,1)S(1)}, bf16[4,120,128]{2,1,0:T(8,128)(2,1)S(1)}, u32[]{:S(2)}, u32[]{:S(2)}) %collective-permute-start.9) | collective-permute-done | bytes 122912 | tf_op jit(solution)/shard_map/ppermute | solution.py:391
  34.7 0.1 near_add.1
  34.8 0.5 %collective-permute-start.11 = (bf16[1,120,128]{2,1,0:T(8,128)(2,1)S(1)}, bf16[1,120,128]{2,1,0:T(8,128)(2,1)S(1)}, u32[]{:S(2)}, u32[]{:S(2)}) collective-permute-start(bf16[1,120,128]{2,1,0:T(8,128)(2,1)S(1)} %get-tuple-element.32), channel_id=1, source_target_pairs={{0,8},{1,9},{2,10},{3,11},{4,12},{5,13},{6,14},{7,15},{8,0},{9,1},... | collective-permute-start | bytes 92168 | tf_op jit(solution)/shard_map/ppermute | solution.py:403
  35.3 1.9 %collective-permute-start.12 = (bf16[1,120,128]{2,1,0:T(8,128)(2,1)S(1)}, bf16[1,120,128]{2,1,0:T(8,128)(2,1)S(1)}, u32[]{:S(2)}, u32[]{:S(2)}) collective-permute-start(bf16[1,120,128]{2,1,0:T(8,128)(2,1)S(1)} %get-tuple-element.33), channel_id=1, source_target_pairs={{0,16},{1,17},{2,18},{3,19},{4,20},{5,21},{6,22},{7,23},{8,24},{9,... | collective-permute-start | bytes 92168 | tf_op jit(solution)/shard_map/ppermute | solution.py:403
  37.2 2.0 %collective-permute-start.13 = (bf16[1,120,128]{2,1,0:T(8,128)(2,1)S(1)}, bf16[1,120,128]{2,1,0:T(8,128)(2,1)S(1)}, u32[]{:S(2)}, u32[]{:S(2)}) collective-permute-start(bf16[1,120,128]{2,1,0:T(8,128)(2,1)S(1)} %get-tuple-element.34), channel_id=1, source_target_pairs={{0,24},{1,25},{2,26},{3,27},{4,28},{5,29},{6,30},{7,31},{8,16},{9,... | collective-permute-start | bytes 92168 | tf_op jit(solution)/shard_map/ppermute | solution.py:403
  39.3 0.1 table.1
  39.4 1.3 %weigh.1 = (bf16[64,7552]{1,0:T(8,128)(2,1)S(1)}, bf16[32,7552]{1,0:T(8,128)(2,1)S(1)}, f32[32,128]{1,0:T(8,128)S(1)}) custom-call(bf16[32,2,7488]{2,1,0:T(2,128)(2,1)S(1)} %copy-done.1, s32[4,32]{1,0:T(4,128)S(1)} %pad_add_fusion.label_ref), custom_call_target="tpu_custom_call" | custom-call | flops 10000000 | bytes 1000000 | tf_op jit(solution)/shard_map/weigh/pallas_call | solution.py:410
  40.8 4.2 %post.1 = (f32[32,32]{1,0:T(8,128)}, f32[1,32]{1,0:T(1,128)}, f32[64,128]{1,0:T(8,128)S(1)}) custom-call(bf16[16,2,7680]{2,1,0:T(2,128)(2,1)S(1)} %join.3.same_ref, bf16[16,2,7680]{2,1,0:T(2,128)(2,1)S(1)} %collective-permute-done.6.other_ref, bf16[64,7552]{1,0:T(8,128)(2,1)S(1)} %get-tuple-element.21.weighted_ref, ...), custom_call_target="tpu_custom_call" | custom-call | tf_op jit(solution)/shard_map/post/pallas_call | solution.py:437
  44.9 0.7 %means.1 = f32[1,2,7488]{2,1,0:T(2,128)} custom-call(f32[1,120,128]{2,1,0:T(8,128)S(1)} %get-tuple-element.31.refs_0_, bf16[1,120,128]{2,1,0:T(8,128)(2,1)S(1)} %collective-permute-done.11.refs_1_, bf16[1,120,128]{2,1,0:T(8,128)(2,1)S(1)} %collective-permute-done.12.refs_2_, bf16[1,120,128]{2,1,0:T(8,128)(2,1)S(1)} %collective-permute-done.13.refs_3_, ...), custom_call_target="tpu_custom_call" | custom-call | tf_op jit(solution)/shard_map/means/pallas_call | solution.py:450
  (18 shorter events, 0.1 us)
Async XLA Ops:
  0.6 0.7 %copy-start.5 = (s32[32,1]{0,1:T(1,128)S(1)}, s32[32,1]{0,1:T(1,128)}, u32[]{:S(2)}) copy-start(s32[32,1]{0,1:T(1,128)} %param.7) | copy-start | bytes 388
  0.6 0.7 %copy-start.3 = (s32[2,32]{1,0:T(2,128)S(1)}, s32[2,32]{1,0:T(2,128)}, u32[]{:S(2)}) copy-start(s32[2,32]{1,0:T(2,128)} %param.9) | copy-start | bytes 772
  0.7 0.7 %copy-start.4 = (s32[32]{0:T(128)S(1)}, s32[32]{0:T(128)}, u32[]{:S(2)}) copy-start(s32[32]{0:T(128)} %param.8) | copy-start | bytes 388
  1.3 1.2 %copy-start = (bf16[32,2,7488]{2,1,0:T(2,128)(2,1)S(1)}, bf16[32,2,7488]{2,1,0:T(2,128)(2,1)}, u32[]{:S(2)}) copy-start(bf16[32,2,7488]{2,1,0:T(2,128)(2,1)} %x_ref.3) | copy-start | bytes 2875396
  2.5 0.8 %copy-start.2 = (bf16[1,2,7488]{2,1,0:T(2,128)(2,1)S(1)}, bf16[1,2,7488]{2,1,0:T(2,128)(2,1)}, u32[]{:S(2)}) copy-start(bf16[1,2,7488]{2,1,0:T(2,128)(2,1)} %ref_ref.1) | copy-start | bytes 89860
  5.8 19.2 %collective-permute-start.7 = (f32[1936,128]{1,0:T(8,128)S(1)}, f32[1936,128]{1,0:T(8,128)S(1)}, u32[]{:S(2)}, u32[]{:S(2)}) collective-permute-start(f32[1936,128]{1,0:T(8,128)S(1)} %get-tuple-element.26), channel_id=1, source_target_pairs={{0,1},{1,0},{2,3},{3,2},{4,5},{5,4},{6,7},{7,6},{8,9},{9,8},{10,11... | collective-permute-start | bytes 2973704 | tf_op jit(solution)/shard_map/ppermute | solution.py:376
  6.4 6.6 %collective-permute-start.2 = (bf16[1,2,7680]{2,1,0:T(2,128)(2,1)S(1)}, bf16[1,2,7680]{2,1,0:T(2,128)(2,1)S(1)}, u32[]{:S(2)}, u32[]{:S(2)}) collective-permute-start(bf16[1,2,7680]{2,1,0:T(2,128)(2,1)S(1)} %get-tuple-element.20.refs_0_), channel_id=1, source_target_pairs={{0,24},{1,25},{2,26},{3,27},{4,28},{5,29},{6,30},{7,31},{8,16},{9,... | collective-permute-start | bytes 92168 | tf_op jit(solution)/shard_map/ppermute | solution.py:379
  11.1 4.8 %collective-permute-start.1 = (bf16[1,2,7680]{2,1,0:T(2,128)(2,1)S(1)}, bf16[1,2,7680]{2,1,0:T(2,128)(2,1)S(1)}, u32[]{:S(2)}, u32[]{:S(2)}) collective-permute-start(bf16[1,2,7680]{2,1,0:T(2,128)(2,1)S(1)} %get-tuple-element.20.refs_0_), channel_id=1, source_target_pairs={{0,16},{1,17},{2,18},{3,19},{4,20},{5,21},{6,22},{7,23},{8,24},{9,... | collective-permute-start | bytes 92168 | tf_op jit(solution)/shard_map/ppermute | solution.py:379
  11.1 4.8 %collective-permute-start = (bf16[1,2,7680]{2,1,0:T(2,128)(2,1)S(1)}, bf16[1,2,7680]{2,1,0:T(2,128)(2,1)S(1)}, u32[]{:S(2)}, u32[]{:S(2)}) collective-permute-start(bf16[1,2,7680]{2,1,0:T(2,128)(2,1)S(1)} %get-tuple-element.20.refs_0_), channel_id=1, source_target_pairs={{0,8},{1,9},{2,10},{3,11},{4,12},{5,13},{6,14},{7,15},{8,0},{9,1},... | collective-permute-start | bytes 92168 | tf_op jit(solution)/shard_map/ppermute | solution.py:379
  16.0 6.4 %collective-permute-start.5 = (bf16[4,2,7680]{2,1,0:T(2,128)(2,1)S(1)}, bf16[4,2,7680]{2,1,0:T(2,128)(2,1)S(1)}, u32[]{:S(2)}, u32[]{:S(2)}) collective-permute-start(bf16[4,2,7680]{2,1,0:T(2,128)(2,1)S(1)} %join.2.refs_0_), channel_id=1, source_target_pairs={{0,6},{1,7},{2,4},{3,5},{4,2},{5,3},{6,0},{7,1},{8,14},{9,15},{10,... | collective-permute-start | bytes 368648 | tf_op jit(solution)/shard_map/ppermute | solution.py:428
  18.6 5.5 %collective-permute-start.4 = (bf16[4,2,7680]{2,1,0:T(2,128)(2,1)S(1)}, bf16[4,2,7680]{2,1,0:T(2,128)(2,1)S(1)}, u32[]{:S(2)}, u32[]{:S(2)}) collective-permute-start(bf16[4,2,7680]{2,1,0:T(2,128)(2,1)S(1)} %join.2.refs_0_), channel_id=1, source_target_pairs={{0,4},{1,5},{2,6},{3,7},{4,0},{5,1},{6,2},{7,3},{8,12},{9,13},{10,... | collective-permute-start | bytes 368648 | tf_op jit(solution)/shard_map/ppermute | solution.py:428
  19.1 5.2 %collective-permute-start.3 = (bf16[4,2,7680]{2,1,0:T(2,128)(2,1)S(1)}, bf16[4,2,7680]{2,1,0:T(2,128)(2,1)S(1)}, u32[]{:S(2)}, u32[]{:S(2)}) collective-permute-start(bf16[4,2,7680]{2,1,0:T(2,128)(2,1)S(1)} %join.2.refs_0_), channel_id=1, source_target_pairs={{0,2},{1,3},{2,0},{3,1},{4,6},{5,7},{6,4},{7,5},{8,10},{9,11},{10,... | collective-permute-start | bytes 368648 | tf_op jit(solution)/shard_map/ppermute | solution.py:428
  24.9 15.8 %collective-permute-start.6 = (bf16[16,2,7680]{2,1,0:T(2,128)(2,1)S(1)}, bf16[16,2,7680]{2,1,0:T(2,128)(2,1)S(1)}, u32[]{:S(2)}, u32[]{:S(2)}) collective-permute-start(bf16[16,2,7680]{2,1,0:T(2,128)(2,1)S(1)} %join.3.same_ref), channel_id=1, source_target_pairs={{0,1},{1,0},{2,3},{3,2},{4,5},{5,4},{6,7},{7,6},{8,9},{9,8},{10,11... | collective-permute-start | bytes 1474568 | tf_op jit(solution)/shard_map/ppermute | solution.py:430
  25.2 14.2 %copy-start.1 = (bf16[32,2,7488]{2,1,0:T(2,128)(2,1)S(1)}, bf16[32,2,7488]{2,1,0:T(2,128)(2,1)}, u32[]{:S(2)}) copy-start(bf16[32,2,7488]{2,1,0:T(2,128)(2,1)} %x_ref.3) | copy-start | bytes 2875396
  25.2 6.1 %collective-permute-start.8 = (bf16[4,120,128]{2,1,0:T(8,128)(2,1)S(1)}, bf16[4,120,128]{2,1,0:T(8,128)(2,1)S(1)}, u32[]{:S(2)}, u32[]{:S(2)}) collective-permute-start(bf16[4,120,128]{2,1,0:T(8,128)(2,1)S(1)} %get-tuple-element.28), channel_id=1, source_target_pairs={{0,2},{1,3},{2,0},{3,1},{4,6},{5,7},{6,4},{7,5},{8,10},{9,11},{10,... | collective-permute-start | bytes 368648 | tf_op jit(solution)/shard_map/ppermute | solution.py:391
  26.7 8.1 %collective-permute-start.9 = (bf16[4,120,128]{2,1,0:T(8,128)(2,1)S(1)}, bf16[4,120,128]{2,1,0:T(8,128)(2,1)S(1)}, u32[]{:S(2)}, u32[]{:S(2)}) collective-permute-start(bf16[4,120,128]{2,1,0:T(8,128)(2,1)S(1)} %get-tuple-element.29), channel_id=1, source_target_pairs={{0,4},{1,5},{2,6},{3,7},{4,0},{5,1},{6,2},{7,3},{8,12},{9,13},{10,... | collective-permute-start | bytes 368648 | tf_op jit(solution)/shard_map/ppermute | solution.py:391
  27.4 7.3 %collective-permute-start.10 = (bf16[4,120,128]{2,1,0:T(8,128)(2,1)S(1)}, bf16[4,120,128]{2,1,0:T(8,128)(2,1)S(1)}, u32[]{:S(2)}, u32[]{:S(2)}) collective-permute-start(bf16[4,120,128]{2,1,0:T(8,128)(2,1)S(1)} %get-tuple-element.30), channel_id=1, source_target_pairs={{0,6},{1,7},{2,4},{3,5},{4,2},{5,3},{6,0},{7,1},{8,14},{9,15},{10,... | collective-permute-start | bytes 368648 | tf_op jit(solution)/shard_map/ppermute | solution.py:391
  34.8 10.1 %collective-permute-start.11 = (bf16[1,120,128]{2,1,0:T(8,128)(2,1)S(1)}, bf16[1,120,128]{2,1,0:T(8,128)(2,1)S(1)}, u32[]{:S(2)}, u32[]{:S(2)}) collective-permute-start(bf16[1,120,128]{2,1,0:T(8,128)(2,1)S(1)} %get-tuple-element.32), channel_id=1, source_target_pairs={{0,8},{1,9},{2,10},{3,11},{4,12},{5,13},{6,14},{7,15},{8,0},{9,1},... | collective-permute-start | bytes 92168 | tf_op jit(solution)/shard_map/ppermute | solution.py:403
  35.3 9.6 %collective-permute-start.12 = (bf16[1,120,128]{2,1,0:T(8,128)(2,1)S(1)}, bf16[1,120,128]{2,1,0:T(8,128)(2,1)S(1)}, u32[]{:S(2)}, u32[]{:S(2)}) collective-permute-start(bf16[1,120,128]{2,1,0:T(8,128)(2,1)S(1)} %get-tuple-element.33), channel_id=1, source_target_pairs={{0,16},{1,17},{2,18},{3,19},{4,20},{5,21},{6,22},{7,23},{8,24},{9,... | collective-permute-start | bytes 92168 | tf_op jit(solution)/shard_map/ppermute | solution.py:403
  37.2 7.7 %collective-permute-start.13 = (bf16[1,120,128]{2,1,0:T(8,128)(2,1)S(1)}, bf16[1,120,128]{2,1,0:T(8,128)(2,1)S(1)}, u32[]{:S(2)}, u32[]{:S(2)}) collective-permute-start(bf16[1,120,128]{2,1,0:T(8,128)(2,1)S(1)} %get-tuple-element.34), channel_id=1, source_target_pairs={{0,24},{1,25},{2,26},{3,27},{4,28},{5,29},{6,30},{7,31},{8,16},{9,... | collective-permute-start | bytes 92168 | tf_op jit(solution)/shard_map/ppermute | solution.py:403

commit v5 on v4

--- a/solution.py
+++ b/solution.py
@@ -21,6 +21,7 @@
 CHUNK = 512
 GROUP = 128
 FAR = 4
+PIECES = 1
 VMEM = pltpu.VMEM
 f32 = jnp.float32
 bf16 = jnp.bfloat16
@@ -87,7 +88,7 @@
     return jnp.sum(jnp.where(same, row, 0.0), axis=1, keepdims=True)
 
 
-def weights(coef, padded, x_ref, label_ref):
+def weights(coef, padded, read, label_ref):
     parts = label_ref.shape[1]
     turn = turns(*[to_column(label_ref[i : i + 1, :].astype(f32)) for i in (1, 2, 3)], LANES)
     factors = [turn[:, i : i + 1] for i in range(5)]
@@ -97,7 +98,7 @@
     for start in range(0, padded, STEP):
         width = min(STEP, padded - start)
         valid = min(STEP, coef - start)
-        both = dot(split, x_ref[:, :, start : start + valid].reshape(2 * parts, valid))
+        both = dot(split, read(start, valid))
         if valid < width:
             both = jnp.concatenate([both, jnp.zeros((2 * parts, width - valid), f32)], axis=1)
         index = (iota((1, width), 1) + start).astype(f32)
@@ -108,18 +109,43 @@
 
 
 def sums_kernel(
-    coef, chips, rows, half, x_ref, ref_ref, label_ref, packet_ref, keep_ref, send_ref
+    coef, chips, rows, half, x_hbm, ref_hbm, cls_hbm, orient_hbm, tilt_hbm,
+    packet_ref, keep_ref, send_ref, label_ref,
+    x_ref, ref_ref, cls_ref, orient_ref, tilt_ref, in_sems, x_sems,
 ):
     parts = label_ref.shape[1]
     padded = -(-coef // LANES) * LANES
+    pairs = ((cls_hbm, cls_ref), (orient_hbm, orient_ref), (tilt_hbm, tilt_ref), (ref_hbm, ref_ref))
+    loads = [pltpu.make_async_copy(a, b, in_sems.at[i]) for i, (a, b) in enumerate(pairs)]
+    for copy in loads:
+        copy.start()
+    pieces = x_sems.shape[0]
+    span = -(-coef // (STEP * pieces)) * STEP
+    copies = []
+    for i in range(pieces):
+        cols = pl.ds(i * span, min(span, coef - i * span))
+        copies.append(
+            pltpu.make_async_copy(x_hbm.at[:, :, cols], x_ref.at[:, :, cols], x_sems.at[i])
+        )
+        copies[-1].start()
+    for copy in loads:
+        copy.wait()
+    label_ref[0:1, :] = cls_ref[...].reshape(1, parts)
+    label_ref[1:2, :] = orient_ref[...].reshape(1, parts)
+    label_ref[2:4, :] = tilt_ref[...]
     cls = label_ref[0:1, :]
 
-    first = label_ref[0:2, :].astype(f32).astype(bf16)
-    second = label_ref[2:4, :].astype(f32).astype(bf16)
-    source, lane = iota((parts, LANES), 0), iota((parts, LANES), 1)
-    labels = dot(first, (lane == source).astype(bf16)) + dot(
-        second, (lane == source + parts).astype(bf16)
-    )
+    def read(start, valid):
+        if start % span == 0:
+            copies[start // span].wait()
+        return x_ref[:, :, start : start + valid].reshape(2 * parts, valid)
+
+
+    spread = (iota((parts, LANES), 1) % parts == iota((parts, LANES), 0)).astype(bf16)
+    repeated = dot(label_ref[...].astype(f32).astype(bf16), spread)
+    lane = iota(repeated.shape, 1) // parts
+    row = jnp.sum(jnp.where(lane == iota(repeated.shape, 0), repeated, 0.0), axis=0, keepdims=True)
+    labels = jnp.where(iota((2, LANES), 0) == 0, row, -1.0)
     packet_ref[0, :, padded - LANES : padded] = jnp.zeros((2, LANES), bf16)
     packet_ref[0, :, 0:coef] = ref_ref[0]
     packet_ref[0, :, padded : padded + LANES] = labels.astype(bf16)
@@ -132,7 +158,7 @@
     q = ((place % FAR) ^ (chip // nears)) * nears + ((place // FAR) ^ (chip % nears))
     order = 2 * q + jnp.where(row < chips, core, 1 - core)
     hot = (order == cls).astype(bf16)
-    for start, width, wedge, real, imag in weights(coef, padded, x_ref, label_ref):
+    for start, width, wedge, real, imag in weights(coef, padded, read, label_ref):
         tile = start // LANES
         for part, value in enumerate((real, imag)):
             summed = dot(hot, (wedge * value).astype(bf16))
@@ -147,7 +173,11 @@
 def weigh_kernel(coef, x_ref, label_ref, weighted_ref, low_ref, power_ref):
     parts, padded = low_ref.shape
     total = jnp.zeros(power_ref.shape, f32)
-    for start, width, wedge, real, imag in weights(coef, padded, x_ref, label_ref):
+
+    def read(start, valid):
+        return x_ref[:, :, start : start + valid].reshape(2 * parts, valid)
+
+    for start, width, wedge, real, imag in weights(coef, padded, read, label_ref):
         cols = slice(start, start + width)
         low_ref[:, cols] = wedge.astype(bf16)
         energy = wedge * (real * real + imag * imag)
@@ -178,7 +208,7 @@
 
 def join(pieces):
     size, *rest = pieces[0].shape
-    hbm = pl.BlockSpec(memory_space=pltpu.HBM)
+    hbm = pl.BlockSpec(memory_space=pl.ANY)
     return pl.pallas_call(
         join_kernel,
         out_shape=jax.ShapeDtypeStruct((size * len(pieces), *rest), pieces[0].dtype),
@@ -210,44 +240,66 @@
             table_ref[i, :, t * LANES : (t + 1) * LANES] = row
 
 
+def device_of(place, nears, flip):
+    me = lax.axis_index("dom")
+    chip = me // 2
+    far, near = place % FAR, place // FAR
+    return 2 * ((far ^ (chip // nears)) * nears + (near ^ (chip % nears))) + me % 2 * (
+        1 - 2 * flip
+    ) + flip
+
+
+def match(block_ref, weighted_ref, low_ref, flip):
+    chips = block_ref.shape[0]
+    parts, padded = low_ref.shape
+    devices = 2 * chips
+    inter = jnp.zeros((2 * parts, devices), f32)
+    energy = jnp.zeros((parts, devices), f32)
+    for start in range(0, padded, CHUNK):
+        width = min(CHUNK, padded - start)
+        cols = slice(start, start + width)
+        rows = block_ref[:, :, cols].reshape(devices, width)
+        inter = inter + dot_nt(weighted_ref[:, cols], rows)
+        square = rows.astype(f32) * rows.astype(f32)
+        pair = square + pltpu.roll(square, devices - 1, 0)
+        energy = energy + dot_nt(low_ref[:, cols], pair.astype(bf16))
+    row, column = iota((devices, devices), 0), iota((devices, devices), 1)
+    here = device_of(row // 2, chips // FAR, flip) == column
+    real = (here & (row % 2 == 0)).astype(f32)
+    imag = (here & (row % 2 == 1)).astype(f32)
+
+    def pick(a, b):
+        return jnp.dot(a, b, precision=lax.Precision.HIGHEST, preferred_element_type=f32)
+
+    return pick(inter[:parts], real) + pick(inter[parts:], imag), pick(energy, real)
+
+
+def own_kernel(same_ref, weighted_ref, low_ref, inter_ref, energy_ref):
+    inter_ref[...], energy_ref[...] = match(same_ref, weighted_ref, low_ref, 0)
+
+
 def post_kernel(
-    coef, same_ref, other_ref, weighted_ref, low_ref, power_ref, table,
+    coef, same_ref, other_ref, weighted_ref, low_ref, power_ref, table, inter_ref, energy_ref,
     score_ref, load_ref, bottom_ref,
     squares, listed,
 ):
     chips = same_ref.shape[0]
     parts, padded = low_ref.shape
     devices = 2 * chips
-    per_far = chips // FAR
     classes = score_ref.shape[1]
     tiles = padded // LANES
     me = lax.axis_index("dom")
-    core = me % 2
-
-    def picker(parity):
-        out_row, in_row = iota((2 * devices, 2 * chips), 0), iota((2 * devices, 2 * chips), 1)
-        part = (out_row >= devices).astype(i32)
-        device = out_row - part * devices
-        chip = device // 2
-        near = (chip % per_far) ^ (me // 2 % per_far)
-        far = (chip // per_far) ^ (me // 2 // per_far)
-        place = near * FAR + far
-        return (in_row == 2 * place + part) & (device % 2 == parity)
-
-    pick_a, pick_b = picker(core).astype(bf16), picker(1 - core).astype(bf16)
-
-    def rows_of(start, width):
-        cols = pl.ds(start, width)
-        a = same_ref[:, :, cols].reshape(2 * chips, width)
-        b = other_ref[:, :, cols].reshape(2 * chips, width)
-        return dot(pick_a, a) + dot(pick_b, b)
-
-    labels = rows_of(padded, LANES)
-    cls, orient = labels[:devices, :parts], labels[devices:, :parts]
-    low_bin, high_bin = labels[:devices, parts : 2 * parts], labels[devices:, parts : 2 * parts]
+
+    cols = slice(padded, padded + LANES)
+    labels = jnp.concatenate(
+        [ref[:, :, cols].reshape(2 * chips, LANES).astype(f32) for ref in (same_ref, other_ref)]
+    )
+    every = labels.shape[0]
+    cls = labels[:, :parts]
+
     class_col = iota((classes, parts), 0).astype(f32)
     tally = jnp.zeros((classes, parts), f32)
-    for r in range(devices):
+    for r in range(0, every, 2):
         tally = tally + jnp.where(cls[r : r + 1] == class_col, 1.0, 0.0)
     tally = jnp.sum(tally, axis=1, keepdims=True)
     diagonal = iota((classes, classes), 0) == iota((classes, classes), 1)
@@ -257,24 +309,24 @@
     chosen = cls == me.astype(f32)
     mask = chosen.astype(bf16)
     before = (iota((parts, parts), 0) < iota((parts, parts), 1)).astype(bf16)
-    above = (iota((devices, devices), 0) > iota((devices, devices), 1)).astype(bf16)
-    in_row = dot(mask, jnp.ones((parts, parts), bf16))
-    rank = dot(mask, before) + dot(above, in_row.astype(bf16))
-    rank = jnp.where(chosen, rank, -1.0)
+    rank = jnp.where(chosen, dot(mask, before), -1.0).astype(bf16)
+    held = dot(mask, jnp.ones((parts, every), bf16))
+    earlier, later = iota((every, every), 0), iota((every, every), 1)
+    start = jnp.sum(jnp.where(earlier < later, held, 0.0), axis=0, keepdims=True)
+    stop = jnp.sum(jnp.where(earlier <= later, held, 0.0), axis=0, keepdims=True)
     count = jnp.sum(jnp.where(chosen, 1.0, 0.0)).astype(i32)
+    spread = (iota((parts, LANES), 1) % parts == iota((parts, LANES), 0)).astype(bf16)
+    gather = (iota((LANES, 8), 0) // parts == iota((LANES, 8), 1) + 1).astype(bf16)
 
     squares[...] = jnp.zeros_like(squares)
 
     def group(g, total):
-        base = (g * GROUP).astype(f32)
-        slot = iota((GROUP, parts), 0).astype(f32) + base
-        values = [jnp.zeros((GROUP, 1), f32)] * 3
-        columns = jnp.zeros((GROUP, 8), f32)
-        pick = iota((8, parts), 0)
-        for r in range(devices):
-            hit = (rank[r : r + 1] == slot).astype(bf16)
-            row = jnp.where(pick == 0, orient[r : r + 1], jnp.where(pick == 1, low_bin[r : r + 1], high_bin[r : r + 1]))
-            columns = columns + dot_nt(hit, row.astype(bf16))
+        slot = iota((GROUP, 1), 0).astype(f32) + (g * GROUP).astype(f32)
+        in_row = (slot >= start) & (slot < stop)
+        row = in_row.astype(bf16)
+        within = slot - jnp.sum(jnp.where(in_row, start, 0.0), axis=1, keepdims=True)
+        hit = dot((dot(row, rank) == within).astype(bf16), spread)
+        columns = dot((hit * dot(row, labels.astype(bf16))).astype(bf16), gather)
         turn = turns(columns[:, 0:1], columns[:, 1:2], columns[:, 2:3], 8)
         empty = iota((GROUP, 8), 0) + g * GROUP >= count
         listed[...] = jnp.where(empty & (iota((GROUP, 8), 1) == 4), 100.0, turn)
@@ -300,17 +352,9 @@
         cols = slice(t * LANES, (t + 1) * LANES)
         bottom_ref[t : t + 1, :] = jnp.sum(squares[:, cols], axis=0, keepdims=True) + extra
 
-    intersection = jnp.zeros((parts, classes), f32)
-    energy = jnp.zeros((parts, classes), f32)
-    for start in range(0, padded, CHUNK):
-        width = min(CHUNK, padded - start)
-        cols = slice(start, start + width)
-        both = rows_of(start, width)
-        real, imag = both[:devices], both[devices:]
-        ref_power = (real * real + imag * imag).astype(bf16)
-        intersection = intersection + dot_nt(weighted_ref[:parts, cols], real.astype(bf16))
-        intersection = intersection + dot_nt(weighted_ref[parts:, cols], imag.astype(bf16))
-        energy = energy + dot_nt(low_ref[:, cols], ref_power)
+    inter, energy = match(other_ref, weighted_ref, low_ref, 1)
+    intersection = inter + inter_ref[...]
+    energy = energy + energy_ref[...]
     power = jnp.sum(power_ref[...], axis=1, keepdims=True)
     score_ref[...] = intersection / (
         math.sqrt(coef) * jnp.sqrt((energy / coef + EPS) * (power / coef + EPS))
@@ -353,8 +397,8 @@
     wide = padded + LANES
     shape = jax.ShapeDtypeStruct
     vmem = pl.BlockSpec(memory_space=VMEM)
-
-    labels = jnp.concatenate([assignment.reshape(1, -1), orientation.reshape(1, -1), tilt_range])
+    hbm = pl.BlockSpec(memory_space=pltpu.HBM)
+
     nears = chips // FAR
 
     def hops(step):
@@ -364,15 +408,26 @@
         shape((1, 2, wide), bf16),
         shape((chips * rows, LANES), f32),
         shape((chips * rows, LANES), f32),
-    )
-    packet, keep, send = pl.pallas_call(
+        shape((4, part_rows), i32),
+    )
+    operands = (particles, references, assignment.reshape(part_rows), orientation, tilt_range)
+    packet, keep, send, labels = pl.pallas_call(
         functools.partial(sums_kernel, coef, chips, rows, half),
         out_shape=outs,
-        in_specs=[vmem] * 3,
-        out_specs=(vmem,) * 3,
+        in_specs=[hbm] * 5,
+        out_specs=(vmem,) * 4,
+        scratch_shapes=[
+            VMEM(particles.shape, bf16),
+            VMEM(references.shape, bf16),
+            VMEM((part_rows,), i32),
+            VMEM((part_rows,), i32),
+            VMEM(tilt_range.shape, i32),
+            pltpu.SemaphoreType.DMA((4,)),
+            pltpu.SemaphoreType.DMA((PIECES,)),
+        ],
         compiler_params=limit(*outs, particles),
         name="sums",
-    )(particles, references, labels)
+    )(*[pltpu.with_memory_space_constraint(a, pltpu.HBM) for a in operands])
     got = lax.ppermute(send, "dom", hops(1))
     pieces = [packet]
     for k in range(1, FAR):
@@ -429,6 +484,15 @@
     same = join(pieces)
     other = lax.ppermute(same, "dom", hops(1))
 
+    outs = (shape((part_rows, classes), f32),) * 2
+    inter, energy = pl.pallas_call(
+        own_kernel,
+        out_shape=outs,
+        in_specs=[vmem] * 3,
+        out_specs=(vmem, vmem),
+        compiler_params=limit(same, weighted, low),
+        name="own",
+    )(same, weighted, low)
     outs = (
         shape((part_rows, classes), f32),
         shape((1, classes), f32),
@@ -437,7 +501,7 @@
     scores, load, bottom = pl.pallas_call(
         functools.partial(post_kernel, coef),
         out_shape=outs,
-        in_specs=[vmem] * 6,
+        in_specs=[vmem] * 8,
         out_specs=(vmem, vmem, vmem),
         scratch_shapes=[
             VMEM((8, padded), f32),
@@ -445,7 +509,7 @@
         ],
         compiler_params=limit(same, other, weighted, low, table, *outs),
         name="post",
-    )(same, other, weighted, low, power, table)
+    )(same, other, weighted, low, power, table, inter, energy)
 
     class_means = pl.pallas_call(
         functools.partial(final_kernel, coef, half),

time: 45.8 us -> 44.5 us (0.972)
  local copies, waits for them, and re-layouts: 2.62 us -> 0.01 us
  Pallas kernels: 9.88 us -> 11.3 us
    unnamed x12 -> x2, local copies, waits for them, and re-layouts: 2.62 us -> 0.01 us
    pallas_call x1, Pallas kernels: 2.54 us -> 3.73 us  [body(): pl.pallas_call(functools.partial(sums_kernel, coef, chips, rows, half), o...]
    pallas_call x0 -> x1, Pallas kernels: none -> 1.03 us  [body(): pl.pallas_call(own_kernel, out_shape=outs, in_specs=[vmem] * 3, out_specs...]
    pallas_call x1, Pallas kernels: 4.16 us -> 3.39 us  [body(): pl.pallas_call(functools.partial(post_kernel, coef), out_shape=outs, in_s...]
  transfers between devices with their start and end apart: 14 -> 14, of which waited for: 7 -> 7; matrix products, arithmetic and copies ran while one was open for 0% -> 0% of each run, Pallas kernels for 15% -> 16%
where the time goes in v5:
time: 44.5 us; the launch traced here: 44.4 us
  starting transfers between devices  17.5 us (39%)
  waiting for transfers between devices  14.9 us (33%)
  Pallas kernels  11.3 us (25%)
  between operations  0.72 us (2%)
    ppermute x3, waiting for transfers between devices, body(): came.append(lax.ppermute(leave[j - 1], 'dom', hops(2 * j)))  6.01 us
    ppermute x3, starting transfers between devices, body(): pieces.append(lax.ppermute(packet, 'dom', hops(2 * nears * k)))  5.31 us
    ppermute x3, waiting for transfers between devices, body(): pieces.append(lax.ppermute(same, 'dom', hops(2 * j)))  4.68 us
    ppermute x3, starting transfers between devices, body(): came.append(lax.ppermute(leave[k - 1], 'dom', hops(2 * nears * k)))  4.45 us
    ppermute x3, waiting for transfers between devices, body(): pieces.append(lax.ppermute(packet, 'dom', hops(2 * nears * k)))  4.15 us
    pallas_call x1, Pallas kernels, body(): pl.pallas_call(functools.partial(sums_kernel, coef, chips, rows, half), o...  3.73 us
    ppermute x3, starting transfers between devices, body(): pieces.append(lax.ppermute(same, 'dom', hops(2 * j)))  3.55 us
    ppermute x3, starting transfers between devices, body(): came.append(lax.ppermute(leave[j - 1], 'dom', hops(2 * j)))  3.55 us
  transfers between devices with their start and end apart: 14, of which 7 were waited for; matrix products, arithmetic and copies ran while one was open for 0% of the time, Pallas kernels for 16%

profile of v5, /device:TPU:0, one launch (start us, length us, event | category | flops | bytes accessed | tf_op | source)
XLA Modules:
  0.0 44.4 jit_solution(4139773907535343772)
XLA Ops:
  0.6 3.7 %sums.1 = (bf16[1,2,7680]{2,1,0:T(2,128)(2,1)S(1)}, f32[1936,128]{1,0:T(8,128)S(1)}, f32[1936,128]{1,0:T(8,128)S(1)}, s32[4,32]{1,0:T(4,128)S(1)}) custom-call(bf16[32,2,7488]{2,1,0:T(2,128)(2,1)} %x_ref.1, bf16[1,2,7488]{2,1,0:T(2,128)(2,1)} %ref_hbm.1, s32[32]{0:T(128)} %bitcast.2, s32[32]{0:T(128)} %orient_hbm.1, s32[2,32]{1,0:T(2,128)} %tilt_hbm.1), custom_call_target="tpu_custom_call" | custom-call | tf_op jit(solution)/shard_map/sums/pallas_call | solution.py:414
  4.4 0.6 %collective-permute-start.7 = (f32[1936,128]{1,0:T(8,128)S(1)}, f32[1936,128]{1,0:T(8,128)S(1)}, u32[]{:S(2)}, u32[]{:S(2)}) collective-permute-start(f32[1936,128]{1,0:T(8,128)S(1)} %get-tuple-element.32), channel_id=1, source_target_pairs={{0,1},{1,0},{2,3},{3,2},{4,5},{5,4},{6,7},{7,6},{8,9},{9,8},{10,11... | collective-permute-start | bytes 2973704 | tf_op jit(solution)/shard_map/ppermute | solution.py:431
  4.9 4.7 %collective-permute-start.2 = (bf16[1,2,7680]{2,1,0:T(2,128)(2,1)S(1)}, bf16[1,2,7680]{2,1,0:T(2,128)(2,1)S(1)}, u32[]{:S(2)}, u32[]{:S(2)}) collective-permute-start(bf16[1,2,7680]{2,1,0:T(2,128)(2,1)S(1)} %get-tuple-element.23.refs_0_), channel_id=1, source_target_pairs={{0,24},{1,25},{2,26},{3,27},{4,28},{5,29},{6,30},{7,31},{8,16},{9,... | collective-permute-start | bytes 92168 | tf_op jit(solution)/shard_map/ppermute | solution.py:434
  9.6 0.0 collective-permute-start.1
  9.6 0.6 %collective-permute-start = (bf16[1,2,7680]{2,1,0:T(2,128)(2,1)S(1)}, bf16[1,2,7680]{2,1,0:T(2,128)(2,1)S(1)}, u32[]{:S(2)}, u32[]{:S(2)}) collective-permute-start(bf16[1,2,7680]{2,1,0:T(2,128)(2,1)S(1)} %get-tuple-element.23.refs_0_), channel_id=1, source_target_pairs={{0,8},{1,9},{2,10},{3,11},{4,12},{5,13},{6,14},{7,15},{8,0},{9,1},... | collective-permute-start | bytes 92168 | tf_op jit(solution)/shard_map/ppermute | solution.py:434
  10.2 1.3 %collective-permute-done.2.refs_3_ = bf16[1,2,7680]{2,1,0:T(2,128)(2,1)S(1)} collective-permute-done((bf16[1,2,7680]{2,1,0:T(2,128)(2,1)S(1)}, bf16[1,2,7680]{2,1,0:T(2,128)(2,1)S(1)}, u32[]{:S(2)}, u32[]{:S(2)}) %collective-permute-start.2) | collective-permute-done | bytes 30752 | tf_op jit(solution)/shard_map/ppermute | solution.py:434
  11.6 2.8 %collective-permute-done.1.refs_2_ = bf16[1,2,7680]{2,1,0:T(2,128)(2,1)S(1)} collective-permute-done((bf16[1,2,7680]{2,1,0:T(2,128)(2,1)S(1)}, bf16[1,2,7680]{2,1,0:T(2,128)(2,1)S(1)}, u32[]{:S(2)}, u32[]{:S(2)}) %collective-permute-start.1) | collective-permute-done | bytes 30752 | tf_op jit(solution)/shard_map/ppermute | solution.py:434
  14.4 0.2 join.2.refs_0_
  14.6 2.5 %collective-permute-start.5 = (bf16[4,2,7680]{2,1,0:T(2,128)(2,1)S(1)}, bf16[4,2,7680]{2,1,0:T(2,128)(2,1)S(1)}, u32[]{:S(2)}, u32[]{:S(2)}) collective-permute-start(bf16[4,2,7680]{2,1,0:T(2,128)(2,1)S(1)} %join.2.refs_0_), channel_id=1, source_target_pairs={{0,6},{1,7},{2,4},{3,5},{4,2},{5,3},{6,0},{7,1},{8,14},{9,15},{10,... | collective-permute-start | bytes 368648 | tf_op jit(solution)/shard_map/ppermute | solution.py:483
  17.1 0.5 %collective-permute-start.4 = (bf16[4,2,7680]{2,1,0:T(2,128)(2,1)S(1)}, bf16[4,2,7680]{2,1,0:T(2,128)(2,1)S(1)}, u32[]{:S(2)}, u32[]{:S(2)}) collective-permute-start(bf16[4,2,7680]{2,1,0:T(2,128)(2,1)S(1)} %join.2.refs_0_), channel_id=1, source_target_pairs={{0,4},{1,5},{2,6},{3,7},{4,0},{5,1},{6,2},{7,3},{8,12},{9,13},{10,... | collective-permute-start | bytes 368648 | tf_op jit(solution)/shard_map/ppermute | solution.py:483
  17.6 0.5 %collective-permute-start.3 = (bf16[4,2,7680]{2,1,0:T(2,128)(2,1)S(1)}, bf16[4,2,7680]{2,1,0:T(2,128)(2,1)S(1)}, u32[]{:S(2)}, u32[]{:S(2)}) collective-permute-start(bf16[4,2,7680]{2,1,0:T(2,128)(2,1)S(1)} %join.2.refs_0_), channel_id=1, source_target_pairs={{0,2},{1,3},{2,0},{3,1},{4,6},{5,7},{6,4},{7,5},{8,10},{9,11},{10,... | collective-permute-start | bytes 368648 | tf_op jit(solution)/shard_map/ppermute | solution.py:483
  18.1 2.9 %collective-permute-done.5.refs_3_ = bf16[4,2,7680]{2,1,0:T(2,128)(2,1)S(1)} collective-permute-done((bf16[4,2,7680]{2,1,0:T(2,128)(2,1)S(1)}, bf16[4,2,7680]{2,1,0:T(2,128)(2,1)S(1)}, u32[]{:S(2)}, u32[]{:S(2)}) %collective-permute-start.5) | collective-permute-done | bytes 122912 | tf_op jit(solution)/shard_map/ppermute | solution.py:483
  21.0 1.6 %collective-permute-done.4.refs_2_ = bf16[4,2,7680]{2,1,0:T(2,128)(2,1)S(1)} collective-permute-done((bf16[4,2,7680]{2,1,0:T(2,128)(2,1)S(1)}, bf16[4,2,7680]{2,1,0:T(2,128)(2,1)S(1)}, u32[]{:S(2)}, u32[]{:S(2)}) %collective-permute-start.4) | collective-permute-done | bytes 122912 | tf_op jit(solution)/shard_map/ppermute | solution.py:483
  22.6 0.2 collective-permute-done.3.refs_1_
  22.8 0.6 %join.3.same_ref = bf16[16,2,7680]{2,1,0:T(2,128)(2,1)S(1)} custom-call(bf16[4,2,7680]{2,1,0:T(2,128)(2,1)S(1)} %join.2.refs_0_, bf16[4,2,7680]{2,1,0:T(2,128)(2,1)S(1)} %collective-permute-done.3.refs_1_, bf16[4,2,7680]{2,1,0:T(2,128)(2,1)S(1)} %collective-permute-done.4.refs_2_, bf16[4,2,7680]{2,1,0:T(2,128)(2,1)S(1)} %collective-permute-done.5.refs_3_), custom_call_target="tpu_custom_call" | custom-call | tf_op jit(solution)/shard_map/join/pallas_call | solution.py:212
  23.5 0.1 collective-permute-start.6
  23.5 0.2 core_add.1
  23.7 1.5 %collective-permute-start.8 = (bf16[4,120,128]{2,1,0:T(8,128)(2,1)S(1)}, bf16[4,120,128]{2,1,0:T(8,128)(2,1)S(1)}, u32[]{:S(2)}, u32[]{:S(2)}) collective-permute-start(bf16[4,120,128]{2,1,0:T(8,128)(2,1)S(1)} %get-tuple-element.34), channel_id=1, source_target_pairs={{0,2},{1,3},{2,0},{3,1},{4,6},{5,7},{6,4},{7,5},{8,10},{9,11},{10,... | collective-permute-start | bytes 368648 | tf_op jit(solution)/shard_map/ppermute | solution.py:446
  25.2 0.7 %collective-permute-start.9 = (bf16[4,120,128]{2,1,0:T(8,128)(2,1)S(1)}, bf16[4,120,128]{2,1,0:T(8,128)(2,1)S(1)}, u32[]{:S(2)}, u32[]{:S(2)}) collective-permute-start(bf16[4,120,128]{2,1,0:T(8,128)(2,1)S(1)} %get-tuple-element.35), channel_id=1, source_target_pairs={{0,4},{1,5},{2,6},{3,7},{4,0},{5,1},{6,2},{7,3},{8,12},{9,13},{10,... | collective-permute-start | bytes 368648 | tf_op jit(solution)/shard_map/ppermute | solution.py:446
  25.9 1.3 %collective-permute-start.10 = (bf16[4,120,128]{2,1,0:T(8,128)(2,1)S(1)}, bf16[4,120,128]{2,1,0:T(8,128)(2,1)S(1)}, u32[]{:S(2)}, u32[]{:S(2)}) collective-permute-start(bf16[4,120,128]{2,1,0:T(8,128)(2,1)S(1)} %get-tuple-element.36), channel_id=1, source_target_pairs={{0,6},{1,7},{2,4},{3,5},{4,2},{5,3},{6,0},{7,1},{8,14},{9,15},{10,... | collective-permute-start | bytes 368648 | tf_op jit(solution)/shard_map/ppermute | solution.py:446
  27.3 2.5 %collective-permute-done.8.refs_1_ = bf16[4,120,128]{2,1,0:T(8,128)(2,1)S(1)} collective-permute-done((bf16[4,120,128]{2,1,0:T(8,128)(2,1)S(1)}, bf16[4,120,128]{2,1,0:T(8,128)(2,1)S(1)}, u32[]{:S(2)}, u32[]{:S(2)}) %collective-permute-start.8) | collective-permute-done | bytes 122912 | tf_op jit(solution)/shard_map/ppermute | solution.py:446
  29.8 3.5 %collective-permute-done.9.refs_2_ = bf16[4,120,128]{2,1,0:T(8,128)(2,1)S(1)} collective-permute-done((bf16[4,120,128]{2,1,0:T(8,128)(2,1)S(1)}, bf16[4,120,128]{2,1,0:T(8,128)(2,1)S(1)}, u32[]{:S(2)}, u32[]{:S(2)}) %collective-permute-start.9) | collective-permute-done | bytes 122912 | tf_op jit(solution)/shard_map/ppermute | solution.py:446
  33.3 0.1 near_add.1
  33.4 0.5 %collective-permute-start.11 = (bf16[1,120,128]{2,1,0:T(8,128)(2,1)S(1)}, bf16[1,120,128]{2,1,0:T(8,128)(2,1)S(1)}, u32[]{:S(2)}, u32[]{:S(2)}) collective-permute-start(bf16[1,120,128]{2,1,0:T(8,128)(2,1)S(1)} %get-tuple-element.38), channel_id=1, source_target_pairs={{0,8},{1,9},{2,10},{3,11},{4,12},{5,13},{6,14},{7,15},{8,0},{9,1},... | collective-permute-start | bytes 92168 | tf_op jit(solution)/shard_map/ppermute | solution.py:458
  33.8 1.9 %collective-permute-start.12 = (bf16[1,120,128]{2,1,0:T(8,128)(2,1)S(1)}, bf16[1,120,128]{2,1,0:T(8,128)(2,1)S(1)}, u32[]{:S(2)}, u32[]{:S(2)}) collective-permute-start(bf16[1,120,128]{2,1,0:T(8,128)(2,1)S(1)} %get-tuple-element.39), channel_id=1, source_target_pairs={{0,16},{1,17},{2,18},{3,19},{4,20},{5,21},{6,22},{7,23},{8,24},{9,... | collective-permute-start | bytes 92168 | tf_op jit(solution)/shard_map/ppermute | solution.py:458
  35.7 2.1 %collective-permute-start.13 = (bf16[1,120,128]{2,1,0:T(8,128)(2,1)S(1)}, bf16[1,120,128]{2,1,0:T(8,128)(2,1)S(1)}, u32[]{:S(2)}, u32[]{:S(2)}) collective-permute-start(bf16[1,120,128]{2,1,0:T(8,128)(2,1)S(1)} %get-tuple-element.40), channel_id=1, source_target_pairs={{0,24},{1,25},{2,26},{3,27},{4,28},{5,29},{6,30},{7,31},{8,16},{9,... | collective-permute-start | bytes 92168 | tf_op jit(solution)/shard_map/ppermute | solution.py:458
  37.8 0.1 table.1
  38.0 1.3 %weigh.1 = (bf16[64,7552]{1,0:T(8,128)(2,1)S(1)}, bf16[32,7552]{1,0:T(8,128)(2,1)S(1)}, f32[32,128]{1,0:T(8,128)S(1)}) custom-call(bf16[32,2,7488]{2,1,0:T(2,128)(2,1)S(1)} %copy-done, s32[4,32]{1,0:T(4,128)S(1)} %get-tuple-element.24.label_ref), custom_call_target="tpu_custom_call" | custom-call | flops 10000000 | bytes 1000000 | tf_op jit(solution)/shard_map/weigh/pallas_call | solution.py:465
  39.3 1.0 %own.1 = (f32[32,32]{1,0:T(8,128)S(1)}, f32[32,32]{1,0:T(8,128)S(1)}) custom-call(bf16[16,2,7680]{2,1,0:T(2,128)(2,1)S(1)} %join.3.same_ref, bf16[64,7552]{1,0:T(8,128)(2,1)S(1)} %get-tuple-element.25.weighted_ref, bf16[32,7552]{1,0:T(8,128)(2,1)S(1)} %get-tuple-element.26.low_ref), custom_call_target="tpu_custom_call" | custom-call | tf_op jit(solution)/shard_map/own/pallas_call | solution.py:488
  40.3 0.0 collective-permute-done.6.other_ref
  40.3 3.4 %post.1 = (f32[32,32]{1,0:T(8,128)}, f32[1,32]{1,0:T(1,128)}, f32[64,128]{1,0:T(8,128)S(1)}) custom-call(bf16[16,2,7680]{2,1,0:T(2,128)(2,1)S(1)} %join.3.same_ref, bf16[16,2,7680]{2,1,0:T(2,128)(2,1)S(1)} %collective-permute-done.6.other_ref, bf16[64,7552]{1,0:T(8,128)(2,1)S(1)} %get-tuple-element.25.weighted_ref, ...), custom_call_target="tpu_custom_call" | custom-call | tf_op jit(solution)/shard_map/post/pallas_call | solution.py:501
  43.7 0.7 %means.1 = f32[1,2,7488]{2,1,0:T(2,128)} custom-call(f32[1,120,128]{2,1,0:T(8,128)S(1)} %get-tuple-element.37.refs_0_, bf16[1,120,128]{2,1,0:T(8,128)(2,1)S(1)} %collective-permute-done.11.refs_1_, bf16[1,120,128]{2,1,0:T(8,128)(2,1)S(1)} %collective-permute-done.12.refs_2_, bf16[1,120,128]{2,1,0:T(8,128)(2,1)S(1)} %collective-permute-done.13.refs_3_, ...), custom_call_target="tpu_custom_call" | custom-call | tf_op jit(solution)/shard_map/means/pallas_call | solution.py:514
  (8 shorter events, 0.0 us)
Async XLA Ops:
  4.4 19.2 %collective-permute-start.7 = (f32[1936,128]{1,0:T(8,128)S(1)}, f32[1936,128]{1,0:T(8,128)S(1)}, u32[]{:S(2)}, u32[]{:S(2)}) collective-permute-start(f32[1936,128]{1,0:T(8,128)S(1)} %get-tuple-element.32), channel_id=1, source_target_pairs={{0,1},{1,0},{2,3},{3,2},{4,5},{5,4},{6,7},{7,6},{8,9},{9,8},{10,11... | collective-permute-start | bytes 2973704 | tf_op jit(solution)/shard_map/ppermute | solution.py:431
  4.9 6.6 %collective-permute-start.2 = (bf16[1,2,7680]{2,1,0:T(2,128)(2,1)S(1)}, bf16[1,2,7680]{2,1,0:T(2,128)(2,1)S(1)}, u32[]{:S(2)}, u32[]{:S(2)}) collective-permute-start(bf16[1,2,7680]{2,1,0:T(2,128)(2,1)S(1)} %get-tuple-element.23.refs_0_), channel_id=1, source_target_pairs={{0,24},{1,25},{2,26},{3,27},{4,28},{5,29},{6,30},{7,31},{8,16},{9,... | collective-permute-start | bytes 92168 | tf_op jit(solution)/shard_map/ppermute | solution.py:434
  9.6 4.8 %collective-permute-start.1 = (bf16[1,2,7680]{2,1,0:T(2,128)(2,1)S(1)}, bf16[1,2,7680]{2,1,0:T(2,128)(2,1)S(1)}, u32[]{:S(2)}, u32[]{:S(2)}) collective-permute-start(bf16[1,2,7680]{2,1,0:T(2,128)(2,1)S(1)} %get-tuple-element.23.refs_0_), channel_id=1, source_target_pairs={{0,16},{1,17},{2,18},{3,19},{4,20},{5,21},{6,22},{7,23},{8,24},{9,... | collective-permute-start | bytes 92168 | tf_op jit(solution)/shard_map/ppermute | solution.py:434
  9.6 4.8 %collective-permute-start = (bf16[1,2,7680]{2,1,0:T(2,128)(2,1)S(1)}, bf16[1,2,7680]{2,1,0:T(2,128)(2,1)S(1)}, u32[]{:S(2)}, u32[]{:S(2)}) collective-permute-start(bf16[1,2,7680]{2,1,0:T(2,128)(2,1)S(1)} %get-tuple-element.23.refs_0_), channel_id=1, source_target_pairs={{0,8},{1,9},{2,10},{3,11},{4,12},{5,13},{6,14},{7,15},{8,0},{9,1},... | collective-permute-start | bytes 92168 | tf_op jit(solution)/shard_map/ppermute | solution.py:434
  14.6 6.4 %collective-permute-start.5 = (bf16[4,2,7680]{2,1,0:T(2,128)(2,1)S(1)}, bf16[4,2,7680]{2,1,0:T(2,128)(2,1)S(1)}, u32[]{:S(2)}, u32[]{:S(2)}) collective-permute-start(bf16[4,2,7680]{2,1,0:T(2,128)(2,1)S(1)} %join.2.refs_0_), channel_id=1, source_target_pairs={{0,6},{1,7},{2,4},{3,5},{4,2},{5,3},{6,0},{7,1},{8,14},{9,15},{10,... | collective-permute-start | bytes 368648 | tf_op jit(solution)/shard_map/ppermute | solution.py:483
  17.1 5.6 %collective-permute-start.4 = (bf16[4,2,7680]{2,1,0:T(2,128)(2,1)S(1)}, bf16[4,2,7680]{2,1,0:T(2,128)(2,1)S(1)}, u32[]{:S(2)}, u32[]{:S(2)}) collective-permute-start(bf16[4,2,7680]{2,1,0:T(2,128)(2,1)S(1)} %join.2.refs_0_), channel_id=1, source_target_pairs={{0,4},{1,5},{2,6},{3,7},{4,0},{5,1},{6,2},{7,3},{8,12},{9,13},{10,... | collective-permute-start | bytes 368648 | tf_op jit(solution)/shard_map/ppermute | solution.py:483
  17.6 5.2 %collective-permute-start.3 = (bf16[4,2,7680]{2,1,0:T(2,128)(2,1)S(1)}, bf16[4,2,7680]{2,1,0:T(2,128)(2,1)S(1)}, u32[]{:S(2)}, u32[]{:S(2)}) collective-permute-start(bf16[4,2,7680]{2,1,0:T(2,128)(2,1)S(1)} %join.2.refs_0_), channel_id=1, source_target_pairs={{0,2},{1,3},{2,0},{3,1},{4,6},{5,7},{6,4},{7,5},{8,10},{9,11},{10,... | collective-permute-start | bytes 368648 | tf_op jit(solution)/shard_map/ppermute | solution.py:483
  23.5 16.9 %collective-permute-start.6 = (bf16[16,2,7680]{2,1,0:T(2,128)(2,1)S(1)}, bf16[16,2,7680]{2,1,0:T(2,128)(2,1)S(1)}, u32[]{:S(2)}, u32[]{:S(2)}) collective-permute-start(bf16[16,2,7680]{2,1,0:T(2,128)(2,1)S(1)} %join.3.same_ref), channel_id=1, source_target_pairs={{0,1},{1,0},{2,3},{3,2},{4,5},{5,4},{6,7},{7,6},{8,9},{9,8},{10,11... | collective-permute-start | bytes 1474568 | tf_op jit(solution)/shard_map/ppermute | solution.py:485
  23.7 14.2 %copy-start = (bf16[32,2,7488]{2,1,0:T(2,128)(2,1)S(1)}, bf16[32,2,7488]{2,1,0:T(2,128)(2,1)}, u32[]{:S(2)}) copy-start(bf16[32,2,7488]{2,1,0:T(2,128)(2,1)} %x_ref.1) | copy-start | bytes 2875396
  23.7 6.1 %collective-permute-start.8 = (bf16[4,120,128]{2,1,0:T(8,128)(2,1)S(1)}, bf16[4,120,128]{2,1,0:T(8,128)(2,1)S(1)}, u32[]{:S(2)}, u32[]{:S(2)}) collective-permute-start(bf16[4,120,128]{2,1,0:T(8,128)(2,1)S(1)} %get-tuple-element.34), channel_id=1, source_target_pairs={{0,2},{1,3},{2,0},{3,1},{4,6},{5,7},{6,4},{7,5},{8,10},{9,11},{10,... | collective-permute-start | bytes 368648 | tf_op jit(solution)/shard_map/ppermute | solution.py:446
  25.2 8.1 %collective-permute-start.9 = (bf16[4,120,128]{2,1,0:T(8,128)(2,1)S(1)}, bf16[4,120,128]{2,1,0:T(8,128)(2,1)S(1)}, u32[]{:S(2)}, u32[]{:S(2)}) collective-permute-start(bf16[4,120,128]{2,1,0:T(8,128)(2,1)S(1)} %get-tuple-element.35), channel_id=1, source_target_pairs={{0,4},{1,5},{2,6},{3,7},{4,0},{5,1},{6,2},{7,3},{8,12},{9,13},{10,... | collective-permute-start | bytes 368648 | tf_op jit(solution)/shard_map/ppermute | solution.py:446
  25.9 7.3 %collective-permute-start.10 = (bf16[4,120,128]{2,1,0:T(8,128)(2,1)S(1)}, bf16[4,120,128]{2,1,0:T(8,128)(2,1)S(1)}, u32[]{:S(2)}, u32[]{:S(2)}) collective-permute-start(bf16[4,120,128]{2,1,0:T(8,128)(2,1)S(1)} %get-tuple-element.36), channel_id=1, source_target_pairs={{0,6},{1,7},{2,4},{3,5},{4,2},{5,3},{6,0},{7,1},{8,14},{9,15},{10,... | collective-permute-start | bytes 368648 | tf_op jit(solution)/shard_map/ppermute | solution.py:446
  33.4 10.4 %collective-permute-start.11 = (bf16[1,120,128]{2,1,0:T(8,128)(2,1)S(1)}, bf16[1,120,128]{2,1,0:T(8,128)(2,1)S(1)}, u32[]{:S(2)}, u32[]{:S(2)}) collective-permute-start(bf16[1,120,128]{2,1,0:T(8,128)(2,1)S(1)} %get-tuple-element.38), channel_id=1, source_target_pairs={{0,8},{1,9},{2,10},{3,11},{4,12},{5,13},{6,14},{7,15},{8,0},{9,1},... | collective-permute-start | bytes 92168 | tf_op jit(solution)/shard_map/ppermute | solution.py:458
  33.8 9.9 %collective-permute-start.12 = (bf16[1,120,128]{2,1,0:T(8,128)(2,1)S(1)}, bf16[1,120,128]{2,1,0:T(8,128)(2,1)S(1)}, u32[]{:S(2)}, u32[]{:S(2)}) collective-permute-start(bf16[1,120,128]{2,1,0:T(8,128)(2,1)S(1)} %get-tuple-element.39), channel_id=1, source_target_pairs={{0,16},{1,17},{2,18},{3,19},{4,20},{5,21},{6,22},{7,23},{8,24},{9,... | collective-permute-start | bytes 92168 | tf_op jit(solution)/shard_map/ppermute | solution.py:458
  35.7 8.0 %collective-permute-start.13 = (bf16[1,120,128]{2,1,0:T(8,128)(2,1)S(1)}, bf16[1,120,128]{2,1,0:T(8,128)(2,1)S(1)}, u32[]{:S(2)}, u32[]{:S(2)}) collective-permute-start(bf16[1,120,128]{2,1,0:T(8,128)(2,1)S(1)} %get-tuple-element.40), channel_id=1, source_target_pairs={{0,24},{1,25},{2,26},{3,27},{4,28},{5,29},{6,30},{7,31},{8,16},{9,... | collective-permute-start | bytes 92168 | tf_op jit(solution)/shard_map/ppermute | solution.py:458

commit v6 on v5

--- a/solution.py
+++ b/solution.py
@@ -17,7 +17,7 @@
 TAU = 0.5
 LOG2E = math.log2(math.e)
 LANES = 128
-STEP = 512
+STEP = 1024
 CHUNK = 512
 GROUP = 128
 FAR = 4
@@ -249,8 +249,13 @@
     ) + flip
 
 
-def match(block_ref, weighted_ref, low_ref, flip):
-    chips = block_ref.shape[0]
+def rows_of(pieces, cols):
+    block = jnp.concatenate([piece[:, :, cols] for piece in pieces])
+    return block.reshape(2 * block.shape[0], block.shape[2])
+
+
+def match(pieces, weighted_ref, low_ref, flip):
+    chips = FAR * len(pieces)
     parts, padded = low_ref.shape
     devices = 2 * chips
     inter = jnp.zeros((2 * parts, devices), f32)
@@ -258,7 +263,7 @@
     for start in range(0, padded, CHUNK):
         width = min(CHUNK, padded - start)
         cols = slice(start, start + width)
-        rows = block_ref[:, :, cols].reshape(devices, width)
+        rows = rows_of(pieces, cols)
         inter = inter + dot_nt(weighted_ref[:, cols], rows)
         square = rows.astype(f32) * rows.astype(f32)
         pair = square + pltpu.roll(square, devices - 1, 0)
@@ -274,16 +279,17 @@
     return pick(inter[:parts], real) + pick(inter[parts:], imag), pick(energy, real)
 
 
-def own_kernel(same_ref, weighted_ref, low_ref, inter_ref, energy_ref):
-    inter_ref[...], energy_ref[...] = match(same_ref, weighted_ref, low_ref, 0)
+def own_kernel(*refs):
+    *same, weighted_ref, low_ref, inter_ref, energy_ref = refs
+    inter_ref[...], energy_ref[...] = match(same, weighted_ref, low_ref, 0)
 
 
 def post_kernel(
-    coef, same_ref, other_ref, weighted_ref, low_ref, power_ref, table, inter_ref, energy_ref,
-    score_ref, load_ref, bottom_ref,
-    squares, listed,
+    coef, weighted_ref, low_ref, power_ref, table, inter_ref, energy_ref, *refs
 ):
-    chips = same_ref.shape[0]
+    *refs, score_ref, load_ref, bottom_ref, squares, listed = refs
+    same, other = refs[: len(refs) // 2], refs[len(refs) // 2 :]
+    chips = FAR * len(same)
     parts, padded = low_ref.shape
     devices = 2 * chips
     classes = score_ref.shape[1]
@@ -291,9 +297,7 @@
     me = lax.axis_index("dom")
 
     cols = slice(padded, padded + LANES)
-    labels = jnp.concatenate(
-        [ref[:, :, cols].reshape(2 * chips, LANES).astype(f32) for ref in (same_ref, other_ref)]
-    )
+    labels = jnp.concatenate([rows_of(half, cols).astype(f32) for half in (same, other)])
     every = labels.shape[0]
     cls = labels[:, :parts]
 
@@ -352,7 +356,7 @@
         cols = slice(t * LANES, (t + 1) * LANES)
         bottom_ref[t : t + 1, :] = jnp.sum(squares[:, cols], axis=0, keepdims=True) + extra
 
-    inter, energy = match(other_ref, weighted_ref, low_ref, 1)
+    inter, energy = match(other, weighted_ref, low_ref, 1)
     intersection = inter + inter_ref[...]
     energy = energy + energy_ref[...]
     power = jnp.sum(power_ref[...], axis=1, keepdims=True)
@@ -481,18 +485,19 @@
     pieces = [same]
     for j in range(1, nears):
         pieces.append(lax.ppermute(same, "dom", hops(2 * j)))
-    same = join(pieces)
-    other = lax.ppermute(same, "dom", hops(1))
+    other = []
+    for j in range(nears):
+        other.append(lax.ppermute(pieces[j], "dom", hops(1)))
 
     outs = (shape((part_rows, classes), f32),) * 2
     inter, energy = pl.pallas_call(
         own_kernel,
         out_shape=outs,
-        in_specs=[vmem] * 3,
+        in_specs=[vmem] * (nears + 2),
         out_specs=(vmem, vmem),
-        compiler_params=limit(same, weighted, low),
+        compiler_params=limit(*pieces, weighted, low),
         name="own",
-    )(same, weighted, low)
+    )(*pieces, weighted, low)
     outs = (
         shape((part_rows, classes), f32),
         shape((1, classes), f32),
@@ -501,15 +506,15 @@
     scores, load, bottom = pl.pallas_call(
         functools.partial(post_kernel, coef),
         out_shape=outs,
-        in_specs=[vmem] * 8,
+        in_specs=[vmem] * (6 + 2 * nears),
         out_specs=(vmem, vmem, vmem),
         scratch_shapes=[
             VMEM((8, padded), f32),
             VMEM((GROUP, 8), f32),
         ],
-        compiler_params=limit(same, other, weighted, low, table, *outs),
+        compiler_params=limit(*pieces, *other, weighted, low, table, *outs),
         name="post",
-    )(same, other, weighted, low, power, table, inter, energy)
+    )(weighted, low, power, table, inter, energy, *pieces, *other)
 
     class_means = pl.pallas_call(
         functools.partial(final_kernel, coef, half),

time: 44.5 us -> 38.7 us (0.87)
  waiting for transfers between devices: 14.9 us -> 7.51 us
  starting transfers between devices: 17.5 us -> 20.5 us
  Pallas kernels: 11.3 us -> 9.82 us
    ppermute x3, waiting for transfers between devices: 4.68 us -> 0.23 us  [body(): pieces.append(lax.ppermute(same, 'dom', hops(2 * j)))]
    ppermute x3, waiting for transfers between devices: 6.01 us -> 3.1 us  [body(): came.append(lax.ppermute(leave[j - 1], 'dom', hops(2 * j)))]
    ppermute x3, starting transfers between devices: 3.55 us -> 5.88 us  [body(): came.append(lax.ppermute(leave[j - 1], 'dom', hops(2 * j)))]
    pallas_call x1, Pallas kernels: 3.73 us -> 2.91 us  [body(): pl.pallas_call(functools.partial(sums_kernel, coef, chips, rows, half), o...]
    ppermute x1 -> x4, starting transfers between devices: 0.07 us -> 0.8 us  [body(): other.append(lax.ppermute(pieces[j], 'dom', hops(1)))]
    pallas_call x2 -> x1, Pallas kernels: 0.82 us -> 0.17 us  [join(): pl.pallas_call(join_kernel, out_shape=jax.ShapeDtypeStruct((size * len(pi...]
  transfers between devices with their start and end apart: 14 -> 17, of which waited for: 7 -> 5; matrix products, arithmetic and copies ran while one was open for 0% -> 0% of each run, Pallas kernels for 16% -> 16%
where the time goes in v6:
time: 38.7 us; the launch traced here: 38.6 us
  starting transfers between devices  20.5 us (53%)
  Pallas kernels  9.82 us (25%)
  waiting for transfers between devices  7.51 us (19%)
  between operations  0.71 us (2%)
    ppermute x3, starting transfers between devices, body(): came.append(lax.ppermute(leave[j - 1], 'dom', hops(2 * j)))  5.88 us
    ppermute x3, starting transfers between devices, body(): pieces.append(lax.ppermute(packet, 'dom', hops(2 * nears * k)))  5.31 us
    ppermute x3, starting transfers between devices, body(): came.append(lax.ppermute(leave[k - 1], 'dom', hops(2 * nears * k)))  4.45 us
    ppermute x3, waiting for transfers between devices, body(): pieces.append(lax.ppermute(packet, 'dom', hops(2 * nears * k)))  4.15 us
    ppermute x3, starting transfers between devices, body(): pieces.append(lax.ppermute(same, 'dom', hops(2 * j)))  3.55 us
    pallas_call x1, Pallas kernels, body(): pl.pallas_call(functools.partial(post_kernel, coef), out_shape=outs, in_s...  3.37 us
    ppermute x3, waiting for transfers between devices, body(): came.append(lax.ppermute(leave[j - 1], 'dom', hops(2 * j)))  3.1 us
    pallas_call x1, Pallas kernels, body(): pl.pallas_call(functools.partial(sums_kernel, coef, chips, rows, half), o...  2.91 us
  transfers between devices with their start and end apart: 17, of which 5 were waited for; matrix products, arithmetic and copies ran while one was open for 0% of the time, Pallas kernels for 16%

profile of v6, /device:TPU:0, one launch (start us, length us, event | category | flops | bytes accessed | tf_op | source)
XLA Modules:
  0.0 38.6 jit_solution(13385533127156654743)
XLA Ops:
  0.6 2.9 %sums.1 = (bf16[1,2,7680]{2,1,0:T(2,128)(2,1)S(1)}, f32[1936,128]{1,0:T(8,128)S(1)}, f32[1936,128]{1,0:T(8,128)S(1)}, s32[4,32]{1,0:T(4,128)S(1)}) custom-call(bf16[32,2,7488]{2,1,0:T(2,128)(2,1)} %x_ref.1, bf16[1,2,7488]{2,1,0:T(2,128)(2,1)} %ref_hbm.1, s32[32]{0:T(128)} %bitcast.2, s32[32]{0:T(128)} %orient_hbm.1, s32[2,32]{1,0:T(2,128)} %tilt_hbm.1), custom_call_target="tpu_custom_call" | custom-call | tf_op jit(solution)/shard_map/sums/pallas_call | solution.py:418
  3.6 0.6 %collective-permute-start.10 = (f32[1936,128]{1,0:T(8,128)S(1)}, f32[1936,128]{1,0:T(8,128)S(1)}, u32[]{:S(2)}, u32[]{:S(2)}) collective-permute-start(f32[1936,128]{1,0:T(8,128)S(1)} %get-tuple-element.32), channel_id=1, source_target_pairs={{0,1},{1,0},{2,3},{3,2},{4,5},{5,4},{6,7},{7,6},{8,9},{9,8},{10,11... | collective-permute-start | bytes 2973704 | tf_op jit(solution)/shard_map/ppermute | solution.py:435
  4.1 4.7 %collective-permute-start.2 = (bf16[1,2,7680]{2,1,0:T(2,128)(2,1)S(1)}, bf16[1,2,7680]{2,1,0:T(2,128)(2,1)S(1)}, u32[]{:S(2)}, u32[]{:S(2)}) collective-permute-start(bf16[1,2,7680]{2,1,0:T(2,128)(2,1)S(1)} %get-tuple-element.27.refs_0_), channel_id=1, source_target_pairs={{0,24},{1,25},{2,26},{3,27},{4,28},{5,29},{6,30},{7,31},{8,16},{9,... | collective-permute-start | bytes 92168 | tf_op jit(solution)/shard_map/ppermute | solution.py:438
  8.8 0.0 collective-permute-start.1
  8.8 0.6 %collective-permute-start = (bf16[1,2,7680]{2,1,0:T(2,128)(2,1)S(1)}, bf16[1,2,7680]{2,1,0:T(2,128)(2,1)S(1)}, u32[]{:S(2)}, u32[]{:S(2)}) collective-permute-start(bf16[1,2,7680]{2,1,0:T(2,128)(2,1)S(1)} %get-tuple-element.27.refs_0_), channel_id=1, source_target_pairs={{0,8},{1,9},{2,10},{3,11},{4,12},{5,13},{6,14},{7,15},{8,0},{9,1},... | collective-permute-start | bytes 92168 | tf_op jit(solution)/shard_map/ppermute | solution.py:438
  9.4 1.3 %collective-permute-done.2.refs_3_ = bf16[1,2,7680]{2,1,0:T(2,128)(2,1)S(1)} collective-permute-done((bf16[1,2,7680]{2,1,0:T(2,128)(2,1)S(1)}, bf16[1,2,7680]{2,1,0:T(2,128)(2,1)S(1)}, u32[]{:S(2)}, u32[]{:S(2)}) %collective-permute-start.2) | collective-permute-done | bytes 30752 | tf_op jit(solution)/shard_map/ppermute | solution.py:438
  10.7 2.8 %collective-permute-done.1.refs_2_ = bf16[1,2,7680]{2,1,0:T(2,128)(2,1)S(1)} collective-permute-done((bf16[1,2,7680]{2,1,0:T(2,128)(2,1)S(1)}, bf16[1,2,7680]{2,1,0:T(2,128)(2,1)S(1)}, u32[]{:S(2)}, u32[]{:S(2)}) %collective-permute-start.1) | collective-permute-done | bytes 30752 | tf_op jit(solution)/shard_map/ppermute | solution.py:438
  13.6 0.2 join.1.refs_0_
  13.8 2.5 %collective-permute-start.5 = (bf16[4,2,7680]{2,1,0:T(2,128)(2,1)S(1)}, bf16[4,2,7680]{2,1,0:T(2,128)(2,1)S(1)}, u32[]{:S(2)}, u32[]{:S(2)}) collective-permute-start(bf16[4,2,7680]{2,1,0:T(2,128)(2,1)S(1)} %join.1.refs_0_), channel_id=1, source_target_pairs={{0,6},{1,7},{2,4},{3,5},{4,2},{5,3},{6,0},{7,1},{8,14},{9,15},{10,... | collective-permute-start | bytes 368648 | tf_op jit(solution)/shard_map/ppermute | solution.py:487
  16.3 0.5 %collective-permute-start.4 = (bf16[4,2,7680]{2,1,0:T(2,128)(2,1)S(1)}, bf16[4,2,7680]{2,1,0:T(2,128)(2,1)S(1)}, u32[]{:S(2)}, u32[]{:S(2)}) collective-permute-start(bf16[4,2,7680]{2,1,0:T(2,128)(2,1)S(1)} %join.1.refs_0_), channel_id=1, source_target_pairs={{0,4},{1,5},{2,6},{3,7},{4,0},{5,1},{6,2},{7,3},{8,12},{9,13},{10,... | collective-permute-start | bytes 368648 | tf_op jit(solution)/shard_map/ppermute | solution.py:487
  16.8 0.5 %collective-permute-start.3 = (bf16[4,2,7680]{2,1,0:T(2,128)(2,1)S(1)}, bf16[4,2,7680]{2,1,0:T(2,128)(2,1)S(1)}, u32[]{:S(2)}, u32[]{:S(2)}) collective-permute-start(bf16[4,2,7680]{2,1,0:T(2,128)(2,1)S(1)} %join.1.refs_0_), channel_id=1, source_target_pairs={{0,2},{1,3},{2,0},{3,1},{4,6},{5,7},{6,4},{7,5},{8,10},{9,11},{10,... | collective-permute-start | bytes 368648 | tf_op jit(solution)/shard_map/ppermute | solution.py:487
  17.3 0.2 core_add.1
  17.5 1.6 %collective-permute-start.11 = (bf16[4,120,128]{2,1,0:T(8,128)(2,1)S(1)}, bf16[4,120,128]{2,1,0:T(8,128)(2,1)S(1)}, u32[]{:S(2)}, u32[]{:S(2)}) collective-permute-start(bf16[4,120,128]{2,1,0:T(8,128)(2,1)S(1)} %get-tuple-element.34), channel_id=1, source_target_pairs={{0,2},{1,3},{2,0},{3,1},{4,6},{5,7},{6,4},{7,5},{8,10},{9,11},{10,... | collective-permute-start | bytes 368648 | tf_op jit(solution)/shard_map/ppermute | solution.py:450
  19.0 1.5 %collective-permute-start.12 = (bf16[4,120,128]{2,1,0:T(8,128)(2,1)S(1)}, bf16[4,120,128]{2,1,0:T(8,128)(2,1)S(1)}, u32[]{:S(2)}, u32[]{:S(2)}) collective-permute-start(bf16[4,120,128]{2,1,0:T(8,128)(2,1)S(1)} %get-tuple-element.35), channel_id=1, source_target_pairs={{0,4},{1,5},{2,6},{3,7},{4,0},{5,1},{6,2},{7,3},{8,12},{9,13},{10,... | collective-permute-start | bytes 368648 | tf_op jit(solution)/shard_map/ppermute | solution.py:450
  20.6 2.8 %collective-permute-start.13 = (bf16[4,120,128]{2,1,0:T(8,128)(2,1)S(1)}, bf16[4,120,128]{2,1,0:T(8,128)(2,1)S(1)}, u32[]{:S(2)}, u32[]{:S(2)}) collective-permute-start(bf16[4,120,128]{2,1,0:T(8,128)(2,1)S(1)} %get-tuple-element.36), channel_id=1, source_target_pairs={{0,6},{1,7},{2,4},{3,5},{4,2},{5,3},{6,0},{7,1},{8,14},{9,15},{10,... | collective-permute-start | bytes 368648 | tf_op jit(solution)/shard_map/ppermute | solution.py:450
  23.4 0.0 collective-permute-done.4.refs_2_
  23.4 0.0 collective-permute-start.6
  23.4 0.2 collective-permute-done.3.refs_1_
  23.6 0.3 collective-permute-start.9
  23.9 2.1 %collective-permute-done.11.refs_1_ = bf16[4,120,128]{2,1,0:T(8,128)(2,1)S(1)} collective-permute-done((bf16[4,120,128]{2,1,0:T(8,128)(2,1)S(1)}, bf16[4,120,128]{2,1,0:T(8,128)(2,1)S(1)}, u32[]{:S(2)}, u32[]{:S(2)}) %collective-permute-start.11) | collective-permute-done | bytes 122912 | tf_op jit(solution)/shard_map/ppermute | solution.py:450
  26.0 0.5 %collective-permute-start.7 = (bf16[4,2,7680]{2,1,0:T(2,128)(2,1)S(1)}, bf16[4,2,7680]{2,1,0:T(2,128)(2,1)S(1)}, u32[]{:S(2)}, u32[]{:S(2)}) collective-permute-start(bf16[4,2,7680]{2,1,0:T(2,128)(2,1)S(1)} %collective-permute-done.3.refs_1_), channel_id=1, source_target_pairs={{0,1},{1,0},{2,3},{3,2},{4,5},{5,4},{6,7},{7,6},{8,9},{9,8},{10,11... | collective-permute-start | bytes 368648 | tf_op jit(solution)/shard_map/ppermute | solution.py:490
  26.5 1.0 %collective-permute-done.13.refs_3_ = bf16[4,120,128]{2,1,0:T(8,128)(2,1)S(1)} collective-permute-done((bf16[4,120,128]{2,1,0:T(8,128)(2,1)S(1)}, bf16[4,120,128]{2,1,0:T(8,128)(2,1)S(1)}, u32[]{:S(2)}, u32[]{:S(2)}) %collective-permute-start.13) | collective-permute-done | bytes 122912 | tf_op jit(solution)/shard_map/ppermute | solution.py:450
  27.5 0.1 near_add.1
  27.6 0.3 collective-permute-start.14
  27.8 1.9 %collective-permute-start.15 = (bf16[1,120,128]{2,1,0:T(8,128)(2,1)S(1)}, bf16[1,120,128]{2,1,0:T(8,128)(2,1)S(1)}, u32[]{:S(2)}, u32[]{:S(2)}) collective-permute-start(bf16[1,120,128]{2,1,0:T(8,128)(2,1)S(1)} %get-tuple-element.39), channel_id=1, source_target_pairs={{0,16},{1,17},{2,18},{3,19},{4,20},{5,21},{6,22},{7,23},{8,24},{9,... | collective-permute-start | bytes 92168 | tf_op jit(solution)/shard_map/ppermute | solution.py:462
  29.7 0.0 collective-permute-done.9.refs_7_
  29.7 2.3 %collective-permute-start.16 = (bf16[1,120,128]{2,1,0:T(8,128)(2,1)S(1)}, bf16[1,120,128]{2,1,0:T(8,128)(2,1)S(1)}, u32[]{:S(2)}, u32[]{:S(2)}) collective-permute-start(bf16[1,120,128]{2,1,0:T(8,128)(2,1)S(1)} %get-tuple-element.40), channel_id=1, source_target_pairs={{0,24},{1,25},{2,26},{3,27},{4,28},{5,29},{6,30},{7,31},{8,16},{9,... | collective-permute-start | bytes 92168 | tf_op jit(solution)/shard_map/ppermute | solution.py:462
  32.0 0.1 table.1
  32.2 1.3 %weigh.1 = (bf16[64,7552]{1,0:T(8,128)(2,1)S(1)}, bf16[32,7552]{1,0:T(8,128)(2,1)S(1)}, f32[32,128]{1,0:T(8,128)S(1)}) custom-call(bf16[32,2,7488]{2,1,0:T(2,128)(2,1)S(1)} %copy-done, s32[4,32]{1,0:T(4,128)S(1)} %get-tuple-element.23.label_ref), custom_call_target="tpu_custom_call" | custom-call | flops 10000000 | bytes 1000000 | tf_op jit(solution)/shard_map/weigh/pallas_call | solution.py:469
  33.5 1.0 %own.1 = (f32[32,32]{1,0:T(8,128)S(1)}, f32[32,32]{1,0:T(8,128)S(1)}) custom-call(bf16[4,2,7680]{2,1,0:T(2,128)(2,1)S(1)} %join.1.refs_0_, bf16[4,2,7680]{2,1,0:T(2,128)(2,1)S(1)} %collective-permute-done.3.refs_1_, bf16[4,2,7680]{2,1,0:T(2,128)(2,1)S(1)} %collective-permute-done.4.refs_2_, bf16[4,2,7680]{2,1,0:T(2,128)(2,1)S(1)} %collective-permute-done.5.refs_3_, ...), custom_call_target="tpu_custom_call" | custom-call | tf_op jit(solution)/shard_map/own/pallas_call | solution.py:493
  34.5 3.4 %post.1 = (f32[32,32]{1,0:T(8,128)}, f32[1,32]{1,0:T(1,128)}, f32[64,128]{1,0:T(8,128)S(1)}) custom-call(bf16[64,7552]{1,0:T(8,128)(2,1)S(1)} %get-tuple-element.24.refs_4_.weighted_ref, bf16[32,7552]{1,0:T(8,128)(2,1)S(1)} %get-tuple-element.25.refs_5_.low_ref, f32[32,128]{1,0:T(8,128)S(1)} %get-tuple-element.26.power_ref, f32[3,8,7552]{2,1,0:T(8,128)S(1)} %table.1, ...), custom_call_target="tpu_custom_call" | custom-call | tf_op jit(solution)/shard_map/post/pallas_call | solution.py:506
  37.9 0.7 %means.1 = f32[1,2,7488]{2,1,0:T(2,128)} custom-call(f32[1,120,128]{2,1,0:T(8,128)S(1)} %get-tuple-element.37.refs_0_, bf16[1,120,128]{2,1,0:T(8,128)(2,1)S(1)} %collective-permute-done.14.refs_1_, bf16[1,120,128]{2,1,0:T(8,128)(2,1)S(1)} %collective-permute-done.15.refs_2_, bf16[1,120,128]{2,1,0:T(8,128)(2,1)S(1)} %collective-permute-done.16.refs_3_, ...), custom_call_target="tpu_custom_call" | custom-call | tf_op jit(solution)/shard_map/means/pallas_call | solution.py:519
  (13 shorter events, 0.0 us)
Async XLA Ops:
  3.6 13.8 %collective-permute-start.10 = (f32[1936,128]{1,0:T(8,128)S(1)}, f32[1936,128]{1,0:T(8,128)S(1)}, u32[]{:S(2)}, u32[]{:S(2)}) collective-permute-start(f32[1936,128]{1,0:T(8,128)S(1)} %get-tuple-element.32), channel_id=1, source_target_pairs={{0,1},{1,0},{2,3},{3,2},{4,5},{5,4},{6,7},{7,6},{8,9},{9,8},{10,11... | collective-permute-start | bytes 2973704 | tf_op jit(solution)/shard_map/ppermute | solution.py:435
  4.1 6.6 %collective-permute-start.2 = (bf16[1,2,7680]{2,1,0:T(2,128)(2,1)S(1)}, bf16[1,2,7680]{2,1,0:T(2,128)(2,1)S(1)}, u32[]{:S(2)}, u32[]{:S(2)}) collective-permute-start(bf16[1,2,7680]{2,1,0:T(2,128)(2,1)S(1)} %get-tuple-element.27.refs_0_), channel_id=1, source_target_pairs={{0,24},{1,25},{2,26},{3,27},{4,28},{5,29},{6,30},{7,31},{8,16},{9,... | collective-permute-start | bytes 92168 | tf_op jit(solution)/shard_map/ppermute | solution.py:438
  8.8 4.8 %collective-permute-start.1 = (bf16[1,2,7680]{2,1,0:T(2,128)(2,1)S(1)}, bf16[1,2,7680]{2,1,0:T(2,128)(2,1)S(1)}, u32[]{:S(2)}, u32[]{:S(2)}) collective-permute-start(bf16[1,2,7680]{2,1,0:T(2,128)(2,1)S(1)} %get-tuple-element.27.refs_0_), channel_id=1, source_target_pairs={{0,16},{1,17},{2,18},{3,19},{4,20},{5,21},{6,22},{7,23},{8,24},{9,... | collective-permute-start | bytes 92168 | tf_op jit(solution)/shard_map/ppermute | solution.py:438
  8.8 4.8 %collective-permute-start = (bf16[1,2,7680]{2,1,0:T(2,128)(2,1)S(1)}, bf16[1,2,7680]{2,1,0:T(2,128)(2,1)S(1)}, u32[]{:S(2)}, u32[]{:S(2)}) collective-permute-start(bf16[1,2,7680]{2,1,0:T(2,128)(2,1)S(1)} %get-tuple-element.27.refs_0_), channel_id=1, source_target_pairs={{0,8},{1,9},{2,10},{3,11},{4,12},{5,13},{6,14},{7,15},{8,0},{9,1},... | collective-permute-start | bytes 92168 | tf_op jit(solution)/shard_map/ppermute | solution.py:438
  13.8 6.8 %collective-permute-start.5 = (bf16[4,2,7680]{2,1,0:T(2,128)(2,1)S(1)}, bf16[4,2,7680]{2,1,0:T(2,128)(2,1)S(1)}, u32[]{:S(2)}, u32[]{:S(2)}) collective-permute-start(bf16[4,2,7680]{2,1,0:T(2,128)(2,1)S(1)} %join.1.refs_0_), channel_id=1, source_target_pairs={{0,6},{1,7},{2,4},{3,5},{4,2},{5,3},{6,0},{7,1},{8,14},{9,15},{10,... | collective-permute-start | bytes 368648 | tf_op jit(solution)/shard_map/ppermute | solution.py:487
  16.3 7.1 %collective-permute-start.4 = (bf16[4,2,7680]{2,1,0:T(2,128)(2,1)S(1)}, bf16[4,2,7680]{2,1,0:T(2,128)(2,1)S(1)}, u32[]{:S(2)}, u32[]{:S(2)}) collective-permute-start(bf16[4,2,7680]{2,1,0:T(2,128)(2,1)S(1)} %join.1.refs_0_), channel_id=1, source_target_pairs={{0,4},{1,5},{2,6},{3,7},{4,0},{5,1},{6,2},{7,3},{8,12},{9,13},{10,... | collective-permute-start | bytes 368648 | tf_op jit(solution)/shard_map/ppermute | solution.py:487
  16.8 6.8 %collective-permute-start.3 = (bf16[4,2,7680]{2,1,0:T(2,128)(2,1)S(1)}, bf16[4,2,7680]{2,1,0:T(2,128)(2,1)S(1)}, u32[]{:S(2)}, u32[]{:S(2)}) collective-permute-start(bf16[4,2,7680]{2,1,0:T(2,128)(2,1)S(1)} %join.1.refs_0_), channel_id=1, source_target_pairs={{0,2},{1,3},{2,0},{3,1},{4,6},{5,7},{6,4},{7,5},{8,10},{9,11},{10,... | collective-permute-start | bytes 368648 | tf_op jit(solution)/shard_map/ppermute | solution.py:487
  17.5 14.7 %copy-start = (bf16[32,2,7488]{2,1,0:T(2,128)(2,1)S(1)}, bf16[32,2,7488]{2,1,0:T(2,128)(2,1)}, u32[]{:S(2)}) copy-start(bf16[32,2,7488]{2,1,0:T(2,128)(2,1)} %x_ref.1) | copy-start | bytes 2875396
  17.5 8.5 %collective-permute-start.11 = (bf16[4,120,128]{2,1,0:T(8,128)(2,1)S(1)}, bf16[4,120,128]{2,1,0:T(8,128)(2,1)S(1)}, u32[]{:S(2)}, u32[]{:S(2)}) collective-permute-start(bf16[4,120,128]{2,1,0:T(8,128)(2,1)S(1)} %get-tuple-element.34), channel_id=1, source_target_pairs={{0,2},{1,3},{2,0},{3,1},{4,6},{5,7},{6,4},{7,5},{8,10},{9,11},{10,... | collective-permute-start | bytes 368648 | tf_op jit(solution)/shard_map/ppermute | solution.py:450
  19.0 6.9 %collective-permute-start.12 = (bf16[4,120,128]{2,1,0:T(8,128)(2,1)S(1)}, bf16[4,120,128]{2,1,0:T(8,128)(2,1)S(1)}, u32[]{:S(2)}, u32[]{:S(2)}) collective-permute-start(bf16[4,120,128]{2,1,0:T(8,128)(2,1)S(1)} %get-tuple-element.35), channel_id=1, source_target_pairs={{0,4},{1,5},{2,6},{3,7},{4,0},{5,1},{6,2},{7,3},{8,12},{9,13},{10,... | collective-permute-start | bytes 368648 | tf_op jit(solution)/shard_map/ppermute | solution.py:450
  20.6 6.9 %collective-permute-start.13 = (bf16[4,120,128]{2,1,0:T(8,128)(2,1)S(1)}, bf16[4,120,128]{2,1,0:T(8,128)(2,1)S(1)}, u32[]{:S(2)}, u32[]{:S(2)}) collective-permute-start(bf16[4,120,128]{2,1,0:T(8,128)(2,1)S(1)} %get-tuple-element.36), channel_id=1, source_target_pairs={{0,6},{1,7},{2,4},{3,5},{4,2},{5,3},{6,0},{7,1},{8,14},{9,15},{10,... | collective-permute-start | bytes 368648 | tf_op jit(solution)/shard_map/ppermute | solution.py:450
  23.4 4.5 %collective-permute-start.6 = (bf16[4,2,7680]{2,1,0:T(2,128)(2,1)S(1)}, bf16[4,2,7680]{2,1,0:T(2,128)(2,1)S(1)}, u32[]{:S(2)}, u32[]{:S(2)}) collective-permute-start(bf16[4,2,7680]{2,1,0:T(2,128)(2,1)S(1)} %join.1.refs_0_), channel_id=1, source_target_pairs={{0,1},{1,0},{2,3},{3,2},{4,5},{5,4},{6,7},{7,6},{8,9},{9,8},{10,11... | collective-permute-start | bytes 368648 | tf_op jit(solution)/shard_map/ppermute | solution.py:490
  23.6 6.1 %collective-permute-start.9 = (bf16[4,2,7680]{2,1,0:T(2,128)(2,1)S(1)}, bf16[4,2,7680]{2,1,0:T(2,128)(2,1)S(1)}, u32[]{:S(2)}, u32[]{:S(2)}) collective-permute-start(bf16[4,2,7680]{2,1,0:T(2,128)(2,1)S(1)} %collective-permute-done.5.refs_3_), channel_id=1, source_target_pairs={{0,1},{1,0},{2,3},{3,2},{4,5},{5,4},{6,7},{7,6},{8,9},{9,8},{10,11... | collective-permute-start | bytes 368648 | tf_op jit(solution)/shard_map/ppermute | solution.py:490
  25.9 8.6 %collective-permute-start.8 = (bf16[4,2,7680]{2,1,0:T(2,128)(2,1)S(1)}, bf16[4,2,7680]{2,1,0:T(2,128)(2,1)S(1)}, u32[]{:S(2)}, u32[]{:S(2)}) collective-permute-start(bf16[4,2,7680]{2,1,0:T(2,128)(2,1)S(1)} %collective-permute-done.4.refs_2_), channel_id=1, source_target_pairs={{0,1},{1,0},{2,3},{3,2},{4,5},{5,4},{6,7},{7,6},{8,9},{9,8},{10,11... | collective-permute-start | bytes 368648 | tf_op jit(solution)/shard_map/ppermute | solution.py:490
  26.0 8.6 %collective-permute-start.7 = (bf16[4,2,7680]{2,1,0:T(2,128)(2,1)S(1)}, bf16[4,2,7680]{2,1,0:T(2,128)(2,1)S(1)}, u32[]{:S(2)}, u32[]{:S(2)}) collective-permute-start(bf16[4,2,7680]{2,1,0:T(2,128)(2,1)S(1)} %collective-permute-done.3.refs_1_), channel_id=1, source_target_pairs={{0,1},{1,0},{2,3},{3,2},{4,5},{5,4},{6,7},{7,6},{8,9},{9,8},{10,11... | collective-permute-start | bytes 368648 | tf_op jit(solution)/shard_map/ppermute | solution.py:490
  27.6 10.3 %collective-permute-start.14 = (bf16[1,120,128]{2,1,0:T(8,128)(2,1)S(1)}, bf16[1,120,128]{2,1,0:T(8,128)(2,1)S(1)}, u32[]{:S(2)}, u32[]{:S(2)}) collective-permute-start(bf16[1,120,128]{2,1,0:T(8,128)(2,1)S(1)} %get-tuple-element.38), channel_id=1, source_target_pairs={{0,8},{1,9},{2,10},{3,11},{4,12},{5,13},{6,14},{7,15},{8,0},{9,1},... | collective-permute-start | bytes 92168 | tf_op jit(solution)/shard_map/ppermute | solution.py:462
  27.8 10.1 %collective-permute-start.15 = (bf16[1,120,128]{2,1,0:T(8,128)(2,1)S(1)}, bf16[1,120,128]{2,1,0:T(8,128)(2,1)S(1)}, u32[]{:S(2)}, u32[]{:S(2)}) collective-permute-start(bf16[1,120,128]{2,1,0:T(8,128)(2,1)S(1)} %get-tuple-element.39), channel_id=1, source_target_pairs={{0,16},{1,17},{2,18},{3,19},{4,20},{5,21},{6,22},{7,23},{8,24},{9,... | collective-permute-start | bytes 92168 | tf_op jit(solution)/shard_map/ppermute | solution.py:462
  29.7 8.2 %collective-permute-start.16 = (bf16[1,120,128]{2,1,0:T(8,128)(2,1)S(1)}, bf16[1,120,128]{2,1,0:T(8,128)(2,1)S(1)}, u32[]{:S(2)}, u32[]{:S(2)}) collective-permute-start(bf16[1,120,128]{2,1,0:T(8,128)(2,1)S(1)} %get-tuple-element.40), channel_id=1, source_target_pairs={{0,24},{1,25},{2,26},{3,27},{4,28},{5,29},{6,30},{7,31},{8,16},{9,... | collective-permute-start | bytes 92168 | tf_op jit(solution)/shard_map/ppermute | solution.py:462
